TPU v7x, 32 devices: a whole 2x2x4 slice. The times are simulated.
32 devices in a mesh: seq: 8 (over y, x, core), head: 4 (over z).
Axes of the slice: x: 2, y: 2, z: 4, core: 2. Of those that a mesh axis runs over, the one named last changes fastest.
Arguments:
- hidden: bfloat16 [16384, 1536], P('seq'), may hold values from -6 to 6
- segment_ids: int32 [16384], P('seq'), may hold values from 0 to 15, as said below
- norm_gain: float32 [1536], replicated, may hold values from 0.5 to 1.5
- w_gate: bfloat16 [1536, 3072], P(None, 'head'), may hold values from -0.15625 to 0.15625
- w_value: bfloat16 [1536, 3072], P(None, 'head'), may hold values from -0.15625 to 0.15625
- w_state: bfloat16 [1536, 256], P(None, 'head'), may hold values from -0.15625 to 0.15625
- w_step: bfloat16 [1536, 48], P(None, 'head'), may hold values from -0.15625 to 0.15625
- conv_value: float32 [4, 3072], P(None, 'head'), may hold values from -3 to 3
- conv_value_bias: float32 [3072], P('head'), may hold values from -3 to 3
- conv_state: float32 [4, 256], P(None, 'head'), may hold values from -3 to 3
- conv_state_bias: float32 [256], P('head'), may hold values from -3 to 3
- decay_log: float32 [48], P('head'), may hold values from -2 to 1
- step_bias: float32 [48], P('head'), may hold values from -5 to -1
- skip_gain: float32 [48], P('head'), may hold values from 0.5 to 1.5
- gate_gain: float32 [3072], P('head'), may hold values from 0.5 to 1.5
- w_out: bfloat16 [3072, 1536], P('head'), may hold values from -0.109375 to 0.109375
- cotangent: bfloat16 [16384, 1536], P('seq'), may hold values from -6 to 6
Outputs:
- mixed: bfloat16 [16384, 1536], P('seq')
- grad_hidden: float32 [16384, 1536], P('seq')
- grad_norm_gain: float32 [1536], replicated
- grad_w_gate: float32 [1536, 3072], P(None, 'head')
- grad_w_value: float32 [1536, 3072], P(None, 'head')
- grad_w_state: float32 [1536, 256], P(None, 'head')
- grad_w_step: float32 [1536, 48], P(None, 'head')
- grad_conv_value: float32 [4, 3072], P(None, 'head')
- grad_conv_value_bias: float32 [3072], P('head')
- grad_conv_state: float32 [4, 256], P(None, 'head')
- grad_conv_state_bias: float32 [256], P('head')
- grad_decay_log: float32 [48], P('head')
- grad_step_bias: float32 [48], P('head')
- grad_skip_gain: float32 [48], P('head')
- grad_gate_gain: float32 [3072], P('head')
- grad_w_out: float32 [3072, 1536], P('head')
Inputs may be any that keep to these rules, and one draw needn't show every extreme that they name: `segment_ids`: entries start at 0 and rise by one at each document's first token, never falling; each document holds 1 to 2000 consecutive tokens and the first exactly 2000; no document starts at a token whose index is a multiple of 2048 other than 0.
All inputs are finite; a program needn't handle non-finite values.
Results may differ from a plain program's by a relative error of at most 0.0099.
Values may be sent and summed in bfloat16 or wider, within the bound.
A program may use at most 256 MiB of HBM per device.

v0:
```python
from functools import partial

import jax
import jax.numpy as jnp
from jax import lax
from jax.sharding import PartitionSpec as P

STATE = 128
GROUP = 256
INNER = 3072


EPSILON = 1e-05
VERY_NEGATIVE = -1e30
PRECISE = lax.Precision.HIGHEST


def passed_along(value, axis, steps):
    count = lax.axis_size(axis)
    first, last = (max(0, -steps), min(count, count - steps))
    return lax.ppermute(value, axis, [(source, source + steps) for source in range(first, last)])


def carried_in(part, axis, combine, identity, reverse):
    count = lax.axis_size(axis)
    place = lax.axis_index(axis)
    ahead = count - 1 - place if reverse else place
    gathered = jax.tree.map(lambda a: lax.all_gather(a, axis), part)
    state = jax.tree.map(lambda a, e: jnp.zeros_like(a) + jnp.asarray(e, a.dtype), part, identity)

    def one(step, state):
        source = count - 1 - step if reverse else step
        return combine(
            state, jax.tree.map(lambda a: lax.dynamic_index_in_dim(a, source, 0, False), gathered)
        )

    return lax.fori_loop(0, ahead, one, state)


def conv_piece(extended, kernel, kernel_bias, visible):
    tokens = visible.shape[0]
    summed = jnp.zeros((tokens, kernel.shape[1]), jnp.float32) + kernel_bias[None, :]
    for tap_index in range(kernel.shape[0]):
        summed = (
            summed
            + kernel[tap_index][None, :]
            * extended[tap_index : tap_index + tokens]
            * visible[:, tap_index : tap_index + 1]
        )
    return jax.nn.silu(summed)


def block_step(running_state, block_item):
    block_decay, block_state = block_item
    return (block_decay[:, None, None] * running_state + block_state, running_state)


def inject(reach_in, c_proj, state_in):
    return jnp.einsum("ih,in,hpn->ihp", reach_in, c_proj, state_in, precision=PRECISE)


def ssd_core(
    ssm_in, step_raw, decay_log, step_bias, skip_gain, b_proj, c_proj, segment_ids, entry_keep
):
    tokens, head_count, head_width = ssm_in.shape
    blocks = tokens // GROUP
    step_size = jax.nn.softplus(step_raw + step_bias)
    log_decay = -jnp.exp(decay_log) * step_size
    scaled = (ssm_in * step_size[:, :, None]).reshape(blocks, GROUP, head_count, head_width)
    cumulative = jnp.cumsum(log_decay.reshape(blocks, GROUP, head_count), axis=1)
    seg_block = segment_ids.reshape(blocks, GROUP)
    position = jnp.arange(GROUP)
    visible_pairs = (seg_block[:, :, None] == seg_block[:, None, :]) & (
        position[:, None] >= position[None, :]
    )[None]
    heads_first = jnp.transpose(cumulative, (0, 2, 1))
    log_ratio = heads_first[:, :, :, None] - heads_first[:, :, None, :]
    decays = jnp.exp(jnp.where(visible_pairs[:, None], log_ratio, VERY_NEGATIVE))
    b_block = b_proj.reshape(blocks, GROUP, -1)
    c_block = c_proj.reshape(blocks, GROUP, -1)
    scores = jnp.einsum("cin,cjn->cij", c_block, b_block, precision=PRECISE)
    within = jnp.einsum("chij,cjhp->cihp", decays * scores[:, None], scaled, precision=PRECISE)
    to_end = jnp.exp(
        jnp.where(
            (seg_block == seg_block[:, -1:])[:, :, None],
            cumulative[:, -1:] - cumulative,
            VERY_NEGATIVE,
        )
    )
    states = jnp.einsum("cjh,cjhp,cjn->chpn", to_end, scaled, b_block, precision=PRECISE)
    before = jnp.concatenate([seg_block[:1, :1], seg_block[:-1, -1:]], 0)
    from_start = jnp.exp(jnp.where((seg_block == before)[:, :, None], cumulative, VERY_NEGATIVE))
    initial = jnp.zeros((head_count, head_width, b_proj.shape[1]), jnp.float32)
    local_end, entering = lax.scan(block_step, initial, (from_start[:, -1], states))
    carried = jnp.einsum("cih,cin,chpn->cihp", from_start, c_block, entering, precision=PRECISE)
    offsets = jnp.cumsum(cumulative[:, -1], axis=0) - cumulative[:, -1]
    running = (cumulative + offsets[:, None]).reshape(tokens, head_count)
    reach_in = jnp.exp(jnp.where(entry_keep[:, None], running, VERY_NEGATIVE))
    result = (within + carried).reshape(tokens, head_count, head_width) + skip_gain[
        None, :, None
    ] * ssm_in
    return (result, local_end, reach_in[-1], reach_in)


def combine_forward(earlier, later):
    decay_early, state_early = earlier
    decay_late, state_late = later
    return (decay_early * decay_late, decay_late[:, None, None] * state_early + state_late)


def combine_backward(earlier, later):
    decay_early, grad_early = earlier
    decay_late, grad_late = later
    return (decay_early * decay_late, grad_late + decay_late[:, None, None] * grad_early)


def on_device(
    hidden,
    segment_ids,
    norm_gain,
    w_gate,
    w_value,
    w_state,
    w_step,
    conv_value,
    conv_value_bias,
    conv_state,
    conv_state_bias,
    decay_log,
    step_bias,
    skip_gain,
    gate_gain,
    w_out,
    cotangent,
):
    tokens, width_model = hidden.shape
    inner_local = w_value.shape[1]
    state_local = w_state.shape[1]
    heads_local = w_step.shape[1]
    head_width = inner_local // heads_local
    rim_rows = conv_value.shape[0] - 1
    source = hidden.astype(jnp.float32)
    inverse = lax.rsqrt(jnp.mean(source * source, -1, keepdims=True) + EPSILON)
    normed_low = (source * inverse * norm_gain).astype(jnp.bfloat16)
    w_local = jnp.concatenate([w_gate, w_value, w_state, w_step], 1)
    projected = jnp.dot(normed_low, w_local, preferred_element_type=jnp.float32)
    gate_raw = projected[:, :inner_local]
    conv_in = projected[:, inner_local : 2 * inner_local + state_local].astype(jnp.bfloat16)
    step_raw = projected[:, 2 * inner_local + state_local :]
    seg_wrapped = segment_ids % 256
    tail_ids = seg_wrapped[tokens - rim_rows :].astype(jnp.float32).astype(jnp.bfloat16)
    prev_rows, prev_ids = passed_along((conv_in[tokens - rim_rows :], tail_ids), "seq", 1)
    prev_seg = prev_ids.astype(jnp.float32).astype(jnp.int32)
    extended_ids = jnp.concatenate([prev_seg, seg_wrapped])
    visible = jnp.stack(
        [
            extended_ids[tap_index : tap_index + tokens] == seg_wrapped
            for tap_index in range(rim_rows + 1)
        ],
        1,
    ).astype(jnp.float32)
    extended = jnp.concatenate([prev_rows, conv_in], 0).astype(jnp.float32)
    kernel = jnp.concatenate([conv_value, conv_state], 1)
    kernel_bias = jnp.concatenate([conv_value_bias, conv_state_bias])
    conv_out, conv_pull = jax.vjp(
        partial(conv_piece, visible=visible), extended, kernel, kernel_bias
    )
    ssm_in = conv_out[:, :inner_local].reshape(tokens, heads_local, head_width)
    state_low = conv_out[:, inner_local:].astype(jnp.bfloat16)
    both_low = lax.all_gather(state_low, "head", axis=1, tiled=True)
    b_proj = both_low[:, :STATE].astype(jnp.float32)
    c_proj = both_low[:, STATE:].astype(jnp.float32)
    entry_keep = (seg_wrapped[0] == prev_seg[rim_rows - 1]) & (segment_ids == segment_ids[0])
    ssm_zero, local_end, carry_decay, reach_in = ssd_core(
        ssm_in, step_raw, decay_log, step_bias, skip_gain, b_proj, c_proj, segment_ids, entry_keep
    )
    totals, state_in = carried_in(
        (carry_decay, local_end),
        "seq",
        combine_forward,
        (jnp.ones_like(carry_decay), jnp.zeros_like(local_end)),
        False,
    )
    ssm_out = ssm_zero + inject(reach_in, c_proj, state_in)
    gate_act = jax.nn.silu(gate_raw)
    ssm_flat = ssm_out.reshape(tokens, inner_local)
    gated = ssm_flat * gate_act
    square_sum = lax.psum(jnp.sum(gated * gated, -1), "head")
    scale_rows = lax.rsqrt(square_sum / INNER + EPSILON)[:, None]
    gate_low = (gated * scale_rows * gate_gain).astype(jnp.bfloat16)
    partial_out = jnp.dot(gate_low, w_out, preferred_element_type=jnp.float32)
    mixed = (source + lax.psum(partial_out, "head")).astype(jnp.bfloat16)
    grad_w_out = lax.dot_general(
        gate_low, cotangent, (((0,), (0,)), ((), ())), preferred_element_type=jnp.float32
    )
    grad_gate_normed = lax.dot_general(
        cotangent, w_out, (((1,), (1,)), ((), ())), preferred_element_type=jnp.float32
    )
    grad_gate_gain = jnp.sum(grad_gate_normed * gated * scale_rows, 0)
    weighted = grad_gate_normed * gate_gain
    row_dot = lax.psum(jnp.sum(weighted * gated, -1), "head")
    grad_gated = scale_rows * weighted - gated * scale_rows**3 * (row_dot / INNER)[:, None]
    grad_ssm = (grad_gated * gate_act).reshape(tokens, heads_local, head_width)
    sigmoid_gate = jax.nn.sigmoid(gate_raw)
    grad_gate_raw = grad_gated * ssm_flat * sigmoid_gate * (1.0 + gate_raw * (1.0 - sigmoid_gate))
    grad_state_in = jnp.einsum("ih,in,ihp->hpn", reach_in, c_proj, grad_ssm, precision=PRECISE)
    totals_back, grad_end = carried_in(
        (carry_decay, grad_state_in),
        "seq",
        combine_backward,
        (jnp.ones_like(carry_decay), jnp.zeros_like(grad_state_in)),
        True,
    )
    grad_decay = jnp.sum(grad_end * state_in, (1, 2))

    def ssd_full(part_in, part_step, part_decay, part_bias, part_skip, part_b, part_c):
        result, end_state, decay_total, reach_again = ssd_core(
            part_in,
            part_step,
            part_decay,
            part_bias,
            part_skip,
            part_b,
            part_c,
            segment_ids,
            entry_keep,
        )
        return (result + inject(reach_again, part_c, state_in), end_state, decay_total)

    ignored, ssd_pull = jax.vjp(
        ssd_full, ssm_in, step_raw, decay_log, step_bias, skip_gain, b_proj, c_proj
    )
    (
        grad_ssm_in,
        grad_step_raw,
        grad_decay_log,
        grad_step_bias,
        grad_skip_gain,
        grad_b_proj,
        grad_c_proj,
    ) = ssd_pull((grad_ssm, grad_end, grad_decay))
    grad_state_local = lax.psum_scatter(
        jnp.concatenate([grad_b_proj, grad_c_proj], 1), "head", scatter_dimension=1, tiled=True
    )
    grad_conv_out = jnp.concatenate([grad_ssm_in.reshape(tokens, inner_local), grad_state_local], 1)
    grad_extended, grad_kernel, grad_kernel_bias = conv_pull(grad_conv_out)
    from_next = passed_along(grad_extended[:rim_rows], "seq", -1)
    grad_conv_in = grad_extended[rim_rows:] + jnp.pad(from_next, ((tokens - rim_rows, 0), (0, 0)))
    grad_projected = jnp.concatenate([grad_gate_raw, grad_conv_in, grad_step_raw], 1).astype(
        jnp.bfloat16
    )
    grad_w_local = lax.dot_general(
        normed_low, grad_projected, (((0,), (0,)), ((), ())), preferred_element_type=jnp.float32
    )
    grad_normed_part = lax.dot_general(
        grad_projected, w_local, (((1,), (1,)), ((), ())), preferred_element_type=jnp.float32
    )
    grad_normed = lax.psum(grad_normed_part, "head")
    weighted_in = grad_normed * norm_gain
    grad_norm_gain = jnp.sum(grad_normed * source * inverse, 0)
    grad_hidden = (
        cotangent.astype(jnp.float32)
        + inverse * weighted_in
        - source * inverse**3 * jnp.sum(weighted_in * source, -1, keepdims=True) / width_model
    )
    summed = lax.psum(
        (
            grad_norm_gain,
            grad_w_local[:, :inner_local],
            grad_w_local[:, inner_local : 2 * inner_local],
            grad_w_local[:, 2 * inner_local : 2 * inner_local + state_local],
            grad_w_local[:, 2 * inner_local + state_local :],
            grad_kernel[:, :inner_local],
            grad_kernel_bias[:inner_local],
            grad_kernel[:, inner_local:],
            grad_kernel_bias[inner_local:],
            grad_decay_log,
            grad_step_bias,
            grad_skip_gain,
            grad_gate_gain,
            grad_w_out,
        ),
        "seq",
    )
    return (
        mixed,
        grad_hidden,
        summed[0],
        summed[1],
        summed[2],
        summed[3],
        summed[4],
        summed[5],
        summed[6],
        summed[7],
        summed[8],
        summed[9],
        summed[10],
        summed[11],
        summed[12],
        summed[13],
    )


def solution(mesh):
    placed = (
        P("seq", None),
        P("seq"),
        P(),
        P(None, "head"),
        P(None, "head"),
        P(None, "head"),
        P(None, "head"),
        P(None, "head"),
        P("head"),
        P(None, "head"),
        P("head"),
        P("head"),
        P("head"),
        P("head"),
        P("head"),
        P("head", None),
        P("seq", None),
    )
    return jax.shard_map(
        on_device,
        mesh=mesh,
        in_specs=placed,
        out_specs=(
            P("seq", None),
            P("seq", None),
            P(),
            P(None, "head"),
            P(None, "head"),
            P(None, "head"),
            P(None, "head"),
            P(None, "head"),
            P("head"),
            P(None, "head"),
            P("head"),
            P("head"),
            P("head"),
            P("head"),
            P("head"),
            P("head", None),
        ),
        check_vma=False,
    )
```

profile of v0, /device:TPU:0, one launch (start us, length us, event | category | flops | bytes accessed | tf_op | source)
XLA Modules:
  0.0 1750.5 jit_solution(1373110879954876015)
XLA Ops:
  25.6 18.3 %fusion.131 = (bf16[2048,1612]{0,1:T(8,128)(2,1)}, f32[2048,1612]{0,1:T(8,128)}) fusion(bf16[1536,1612]{1,0:T(8,128)(2,1)} %concatenate.33, bf16[2048,1536]{1,0:T(8,128)(2,1)} %param.27, f32[1536]{0:T(1024)S(1)} %copy-done.58, f32[2048]{0:T(1024)S(1)} %get-tuple-element.648), kind=kOutput, calls=%fused_computation.236 | convolution fusion | flops 10157711360 | bytes 31066112 | tf_op jit(solution)/shard_map/dot_general | solution.py:146
  142.0 20.7 %while.75 = (s32[]{:T(128)}, f32[12,64,128]{2,1,0:T(8,128)S(1)}, f32[8,12,64,128]{3,2,1,0:T(8,128)}, f32[8,12]{1,0:T(8,128)}, f32[8,12,64,128]{3,2,1,0:T(8,128)}, /*index=5*/s32[]{:T(128)}, s32[]{:T(128)}) while((s32[]{:T(128)}, f32[12,64,128]{2,1,0:T(8,128)S(1)}, f32[8,12,64,128]{3,2,1,0:T(8,128)}, f32[8,12]{1,0:T(8,128)}, ...), condition=%wide.region_4.5_spmd.clone, body=%wide.region_3.4_spmd.clone.sunk | while | flops 393219 | bytes 1966832 | solution.py:94
  174.2 32.9 %fusion.7 = f32[8,12,64,256]{3,2,1,0:T(8,128)S(1)} fusion(f32[8,256,256]{2,1,0:T(8,128)S(1)} %fusion.132, f32[8,12,256]{2,1,0:T(8,128)S(1)} %copy-done.34, pred[8,256,256]{2,1,0:T(8,128)(4,1)} %compare_and_fusion, f32[8,256,12,64]{1,0,3,2:T(8,128)} %bitcast.294, f32[8,256,12]{1,2,0:T(8,128)S(1)} %copy.357), kind=kOutput, calls=%fused_computation.30 | convolution fusion | flops 4852285440 | bytes 15400960 | tf_op jit(solution)/shard_map/chij,cjhp->cihp/dot_general | solution.py:82
  216.1 30.6 %while.76 = (s32[]{:T(128)}, f32[12,64,128]{2,1,0:T(8,128)S(1)}, f32[8,12,64,128]{3,2,1,0:T(8,128)}, f32[8,12,1,1]{1,3,2,0:T(1,128)}, f32[8,12]{1,0:T(8,128)}, /...) while((s32[]{:T(128)}, f32[12,64,128]{2,1,0:T(8,128)S(1)}, f32[8,12,64,128]{3,2,1,0:T(8,128)}, ...), condition=%wide.region_16.17_spmd.clone, body=%wide.region_15.16_spmd.clone.sunk | while | flops 393219 | bytes 1968376 | solution.py:94
  263.5 12.5 psum.126
  276.1 11.6 multiply_reduce_fusion.7
  296.2 14.5 multiply_reduce_fusion.8
  320.5 14.3 fusion.94
  334.8 41.6 %fusion.10 = (f32[8,12,256]{2,1,0:T(8,128)S(1)}, f32[8,12,256]{2,1,0:T(8,128)S(1)}, f32[8,256,256]{2,1,0:T(8,128)S(1)}) fusion(f32[8,256,256]{2,1,0:T(8,128)S(1)} %copy-done.23, f32[8,12,256]{2,1,0:T(8,128)S(1)} %copy-done.34, pred[8,256,256]{2,1,0:T(8,128)(4,1)S(1)} %copy-done.30, f32[8,256,12,64]{1,0,3,2:T(8,128)} %bitcast.295, ...), kind=kOutput, calls=%fused_computation.32 | convolution fusion | flops 4889460736 | bytes 17694720 | tf_op jit(solution)/shard_map/transpose(jvp(chij,cjhp->cihp))/dot_general | solution.py:82
  434.6 22.4 %while.74 = (s32[]{:T(128)}, f32[12,64,128]{2,1,0:T(8,128)S(1)}, f32[8,12]{1,0:T(8,128)S(1)}, f32[8,12,64,128]{3,2,1,0:T(8,128)}, f32[8,12,64,128]{3,2,1,0:T(8,1...) while((s32[]{:T(128)}, f32[12,64,128]{2,1,0:T(8,128)S(1)}, ...), condition=%wide.region_19.20_spmd, body=%wide.region_17.19_spmd.sunk | while | flops 393207 | bytes 2359713 | solution.py:94
  457.0 11.5 multiply_reduce_fusion.5
  468.5 13.6 fusion.91
  490.6 25.3 %bitcast_add_fusion.5 = f32[8,256,12,64]{1,3,2,0:T(8,128)S(1)} fusion(f32[8,256,12,64]{1,3,2,0:T(8,128)} %get-tuple-element.659, f32[8,256,12]{1,2,0:T(8,128)S(1)} %copy-done.26, f32[8,256,256]{2,1,0:T(8,128)} %copy-done.22, f32[8,12,256]{2,1,0:T(8,128)S(1)} %copy-done.35, pred[8,256,256]{2,1,0:T(8,128)(4,1)} %compare_and_fusion, ...), kind=kOutput, calls=%fused_computation.76 | convolution fusion | flops 4853858304 | bytes 21692416 | tf_op jit(solution)/shard_map/transpose(jvp(chij,cjhp->cihp))/dot_general | solution.py:82
  537.7 19.9 %reduce-window.16 = f32[8,12,2,128]{3,1,2,0:T(8,128)S(1)} reduce-window(f32[8,12,2,128]{3,1,2,0:T(8,128)S(1)} %copy.400, f32[]{:T(128)} %constant.186.clone.1), window={size=1x1x1x128 pad=0_0x0_0x0_0x0_127}, to_apply=%region_29.30 | reduce-window | flops 3121152 | bytes 196612 | tf_op jit(solution)/shard_map/reduce-window.2
  573.7 20.4 %multiply_reduce_fusion.4 = (f32[832]{0:T(1024)S(1)}, f32[832]{0:T(1024)S(1)}, f32[832]{0:T(1024)S(1)}, f32[832]{0:T(1024)S(1)}, f32[832]{0:T(1024)S(1)}, /*index=5*/f32[2048,832]{0,1:T(8,128)}) fusion(f32[2051,832]{0,1:T(8,128)} %copy-done.1, f32[2048]{0:T(1024)S(1)} %bitcast.346, f32[2048]{0:T(1024)S(1)} %bitcast.349, f32[2048]{0:T(1024)S(1)} %bitcast.352, ...), kind=kLoop, calls=%fused_computation.63 | loop fusion | flops 39186368 | bytes 47759616 | tf_op jit(solution)/shard_map/transpose(jvp())/reduce_sum | solution.py:46
  605.1 11.1 pad_add_fusion
  620.6 22.1 %fusion.76 = f32[1536,1612]{0,1:T(8,128)} fusion(bf16[2048,12]{0,1:T(8,128)(2,1)S(1)} %get-tuple-element.613, bf16[2048,832]{0,1:T(8,128)(2,1)S(1)} %fusion.33, bf16[2048,768]{0,1:T(8,128)(2,1)} %get-tuple-element.623, bf16[2048,1536]{1,0:T(8,128)(2,1)} %param.27, f32[1536]{0:T(1024)S(1)} %copy-done.59, f32[2048]{0:T(1024)S(1)} %copy-done.46), kind=kOutput, calls=%fused_computation.132 | convolution fusion | flops 10174218240 | bytes 22812672 | tf_op jit(solution)/shard_map/dot_general | solution.py:252
  655.1 11.2 fusion.123
  666.3 16.6 fusion.77
  684.0 164.8 %all-reduce.20.cloned.1.call-done = (f32[1536,768]{0,1:T(8,128)}, f32[1536,768]{0,1:T(8,128)}, f32[1536,64]{0,1:T(8,128)}, f32[1536,12]{0,1:T(8,128)}, f32[768,1536]{1,0:T(8,128)}) async-done(((f32[1536,768]{0,1:T(8,128)}, f32[1536,768]{0,1:T(8,128)}, f32[1536,64]{0,1:T(8,128)}, f32[1536,12]{0,1:T(8,128)}, f32[768,1536]{1,0:T(8,128)}), (f32[1536,768]{0,1:T(8,128)}, f32[1536,768]{0,1:T(8,128)}, ...) | async-done | bytes 14622736 | tf_op jit(solution)/shard_map/psum | solution.py:266
  861.1 823.6 %all-reduce.22.cloned.1.call-done = (f32[2048,1536]{1,0:T(8,128)}, f32[2048,1536]{1,0:T(8,128)}) async-done(((f32[2048,1536]{1,0:T(8,128)}, f32[2048,1536]{1,0:T(8,128)}), (f32[2048,1536]{1,0:T(8,128)}, f32[2048,1536]{1,0:T(8,128)})) %all-reduce.22.cloned.1.call-update) | async-done | bytes 25165840 | tf_op jit(solution)/shard_map/psum | solution.py:192
  1684.7 9.8 fusion.20
  1694.9 17.6 %fusion.17 = (f32[2048,1536]{1,0:T(8,128)}, bf16[2048,1536]{1,0:T(8,128)(2,1)}) fusion(bf16[2048,1536]{1,0:T(8,128)(2,1)} %param.27, bf16[2048,1536]{1,0:T(8,128)(2,1)} %param.43, f32[2048,1536]{1,0:T(8,128)S(1)} %copy-done.6, f32[2048]{0:T(1024)S(1)} %get-tuple-element.526, f32[2048]{0:T(1024)S(1)} %copy-done.60, f32[1536]{0:T(1024)S(1)} %copy-done.59, ...), kind=kLoop, calls=%fused_computation.39 | loop fusion | flops 34603008 | bytes 56653824 | tf_op jit(solution)/shard_map/sub | solution.py:262
  1712.5 24.4 %all-reduce.14 = (f32[1536]{0:T(1024)}, f32[4,768]{1,0:T(4,128)}, f32[768]{0:T(1024)}, f32[4,64]{1,0:T(4,128)}, f32[64]{0:T(128)}, /*index=5*/f32[12]{0:T(128)}, f32[12]{0:T(128)}, f32[12]{0:T(128)}, f32[768]{0:T(1024)}) all-reduce(f32[1536]{0:T(1024)S(1)} %get-tuple-element.525, ...), channel_id=1, replica_groups=mesh['seq'=8,'head'=4] {'seq'}, use_global_device_ids=true, to_apply=%region_34.35 | all-reduce | flops 6500 | bytes 52000 | tf_op jit(solution)/shard_map/psum | solution.py:266
  (484 shorter events, 402.8 us)
Async XLA Ops:
  7.2 268.9 %copy-start = (bf16[768,1536]{1,0:T(8,128)(2,1)S(1)}, bf16[768,1536]{1,0:T(8,128)(2,1)}, u32[]{:S(2)}) copy-start(bf16[768,1536]{1,0:T(8,128)(2,1)} %param.42) | copy-start | bytes 7077892
  7.2 118.4 %all-gather.7.cloned.1.call-start = ((), (), s32[]{:S(2)}) async-start(), calls=%async_computation.1 | async-start | bytes 1310720 | tf_op jit(solution)/shard_map/all_gather | solution.py:170
  8.1 48.5 %copy-start.61 = (s32[2048]{0:T(1024)}, s32[2048]{0:T(1024)S(1)}, u32[]{:S(2)}) copy-start(s32[2048]{0:T(1024)S(1)} %add_select_fusion) | copy-start | bytes 24580
  8.7 69.0 %collective-permute-start.1 = (bf16[3]{0:T(256)(128)(2,1)}, bf16[3]{0:T(256)(128)(2,1)}, u32[]{:S(2)}, u32[]{:S(2)}) collective-permute-start(bf16[3]{0:T(256)(128)(2,1)} %fusion.114), channel_id=1, source_target_pairs={{0,4},{4,8},{8,12},{12,16},{16,20},{20,24},{24,28},{1,5},{5,9},{9,... | collective-permute-start | bytes 26 | tf_op jit(solution)/shard_map/ppermute | solution.py:21
  16.3 27.6 %copy-start.45 = (f32[2048]{0:T(1024)}, f32[2048]{0:T(1024)S(1)}, u32[]{:S(2)}) copy-start(f32[2048]{0:T(1024)S(1)} %get-tuple-element.648) | copy-start | bytes 24580
  25.6 24.9 %copy-start.47 = (s32[2048]{0:T(1024)S(1)}, s32[2048]{0:T(1024)}, u32[]{:S(2)}) copy-start(s32[2048]{0:T(1024)} %param.28) | copy-start | bytes 24580
  45.7 33.4 %collective-permute-start = (bf16[3,832]{0,1:T(8,128)(2,1)}, bf16[3,832]{0,1:T(8,128)(2,1)}, u32[]{:S(2)}, u32[]{:S(2)}) collective-permute-start(bf16[3,832]{0,1:T(8,128)(2,1)} %slice.209), channel_id=1, source_target_pairs={{0,4},{4,8},{8,12},{12,16},{16,20},{20,24},{24,28},{1,5},{5,9},{9,... | collective-permute-start | bytes 14984 | tf_op jit(solution)/shard_map/ppermute | solution.py:21
  58.7 24.1 %copy-start.24 = (f32[2048,12]{0,1:T(8,128)}, f32[2048,12]{0,1:T(8,128)S(1)}, u32[]{:S(2)}) copy-start(f32[2048,12]{0,1:T(8,128)S(1)} %get-tuple-element.620) | copy-start | bytes 294916
  94.5 152.1 %all-gather.9.cloned.1.call-start = ((), (), s32[]{:S(2)}) async-start(), calls=%async_computation.3 | async-start | bytes 3538944 | tf_op jit(solution)/shard_map/all_gather | solution.py:28
  94.6 240.1 %copy-start.20 = (f32[8,256,12]{1,2,0:T(8,128)}, f32[8,256,12]{1,2,0:T(8,128)S(1)}, u32[]{:S(2)}) copy-start(f32[8,256,12]{1,2,0:T(8,128)S(1)} %copy.357) | copy-start | bytes 294916
  163.5 260.7 %all-gather.11.cloned.1.call-start = ((), (), s32[]{:S(2)}) async-start(), calls=%async_computation.4 | async-start | bytes 3538944 | tf_op jit(solution)/shard_map/all_gather | solution.py:28
  174.2 33.0 %copy-start.22 = (f32[8,256,256]{2,1,0:T(8,128)}, f32[8,256,256]{2,1,0:T(8,128)S(1)}, u32[]{:S(2)}) copy-start(f32[8,256,256]{2,1,0:T(8,128)S(1)} %fusion.132) | copy-start | bytes 6291460
  174.2 33.0 %copy-start.10 = (bf16[8,256,128,1]{2,1,3,0:T(8,128)(2,1)S(1)}, bf16[8,256,128,1]{2,1,3,0:T(8,128)(2,1)}, u32[]{:S(2)}) copy-start(bf16[8,256,128,1]{2,1,3,0:T(8,128)(2,1)} %copy.407) | copy-start | bytes 1572868
  174.2 33.0 %copy-start.11 = (f32[8,12,64,128]{3,2,1,0:T(8,128)S(1)}, f32[8,12,64,128]{3,2,1,0:T(8,128)}, u32[]{:S(2)}) copy-start(f32[8,12,64,128]{3,2,1,0:T(8,128)} %get-tuple-element.347) | copy-start | bytes 9437188
  216.1 30.6 %copy-start.78 = (f32[12]{0:T(128)S(1)}, f32[12]{0:T(128)}, u32[]{:S(2)}) copy-start(f32[12]{0:T(128)} %param.40) | copy-start | bytes 148
  320.4 253.3 %reduce-scatter.2.cloned.1.call-start = ((), (), s32[]{:S(2)}) async-start(), calls=%async_computation.2 | async-start | bytes 2621440 | tf_op jit(solution)/shard_map/reduce_scatter | solution.py:242
  334.8 42.9 %copy-start.15 = (bf16[8,256,128]{2,1,0:T(8,128)(2,1)S(1)}, bf16[8,256,128]{2,1,0:T(8,128)(2,1)}, u32[]{:S(2)}) copy-start(bf16[8,256,128]{2,1,0:T(8,128)(2,1)} %copy.366) | copy-start | bytes 1572868
  490.6 358.3 %all-reduce.20.cloned.1.call-start = ((), (), s32[]{:S(2)}) async-start(), calls=%async_computation.5 | async-start | bytes 29294592 | tf_op jit(solution)/shard_map/psum | solution.py:266
  603.8 12.4 collective-permute-start.2
  620.6 22.1 %copy-start.17 = (bf16[2048,832]{0,1:T(8,128)(2,1)}, bf16[2048,832]{0,1:T(8,128)(2,1)S(1)}, u32[]{:S(2)}) copy-start(bf16[2048,832]{0,1:T(8,128)(2,1)S(1)} %fusion.33) | copy-start | bytes 10223620
  654.4 1030.3 %all-reduce.22.cloned.1.call-start = ((), (), s32[]{:S(2)}) async-start(), calls=%async_computation.6 | async-start | bytes 50331648 | tf_op jit(solution)/shard_map/psum | solution.py:192
  684.0 177.1 %copy-start.48 = (f32[4,832]{1,0:T(4,128)}, f32[4,832]{1,0:T(4,128)S(1)}, u32[]{:S(2)}) copy-start(f32[4,832]{1,0:T(4,128)S(1)} %pad_add_fusion.2) | copy-start | bytes 39940
  1694.8 42.1 %copy-start.31 = (f32[1536,64]{0,1:T(8,128)S(1)}, f32[1536,64]{0,1:T(8,128)}, u32[]{:S(2)}) copy-start(f32[1536,64]{0,1:T(8,128)} %get-tuple-element.973) | copy-start | bytes 1179652
  1694.9 42.9 %copy-start.44 = (f32[1536,12]{0,1:T(8,128)S(1)}, f32[1536,12]{0,1:T(8,128)}, u32[]{:S(2)}) copy-start(f32[1536,12]{0,1:T(8,128)} %get-tuple-element.974) | copy-start | bytes 221188
  (79 other events, 799.2 us)
Sparse Core Ops, SparseCore 0:
  94.7 27.6 all-gather.6
  163.7 32.4 all-gather.8
  320.5 37.8 all-gather.10
  490.7 42.3 reduce-scatter.1
  654.5 194.2 all-reduce.19
  851.9 832.7 all-reduce.21
where the time goes:
time: 1760 us; the launch traced here: 1750 us
  waiting for transfers between devices  989 us (56%)
  matrix products  286 us (16%)
  other arithmetic  223 us (13%)
  local copies, waits for them, and re-layouts  172 us (10%)
  blocking collectives  54.1 us (3%)
    psum x1, waiting for transfers between devices, on_device(): mixed = (source + lax.psum(partial_out, 'head')).astype(jnp.bfloat16)  824 us
    psum x1, waiting for transfers between devices, on_device(): lax.psum((grad_norm_gain, grad_w_local[:, :inner_local], grad_w_local[:,...  165 us
    dot_general x3, matrix products, ssd_core(): jnp.einsum('chij,cjhp->cihp', decays * scores[:, None], scaled, precision...  99.8 us
    unnamed x207, local copies, waits for them, and re-layouts  49.8 us
    dot_general x4, matrix products, ssd_core(): jnp.einsum('cih,cin,chpn->cihp', from_start, c_block, entering, precision...  35.2 us
  transfers between devices with their start and end apart: 9, of which 2 were waited for; matrix products, arithmetic and copies ran while one was open for 23% of the time, Pallas kernels for 0%

commit v1 on v0

v1 whole, which is shorter than its diff:
```python
from functools import partial

import jax
import jax.numpy as jnp
from jax import lax
from jax.experimental import pallas as pl
from jax.experimental.layout import Layout, with_layout_constraint
from jax.experimental.pallas import tpu as pltpu
from jax.sharding import PartitionSpec as P


EPSILON = 1e-05
VERY_NEGATIVE = -1e30
CHUNK = 256
SPAN = 128
STATE = 128
WIDTH = 64
LANES = 128
F32 = jnp.float32
BF16 = jnp.bfloat16
ONE = pl.Buffered(1)
EARLY = 40


def nn(a, b):
    return lax.dot_general(a, b, (((1,), (0,)), ((), ())), preferred_element_type=F32)


def nt(a, b):
    return lax.dot_general(a, b, (((1,), (1,)), ((), ())), preferred_element_type=F32)


def tn(a, b):
    return lax.dot_general(a, b, (((0,), (0,)), ((), ())), preferred_element_type=F32)


def exact(a, b):
    return lax.dot_general(
        a, b, (((1,), (0,)), ((), ())), preferred_element_type=F32, precision=lax.Precision.HIGHEST
    )


def iota(shape, axis):
    return lax.broadcasted_iota(jnp.int32, shape, axis)


def pair_of(columns, pair):
    rows = columns.shape[0]
    first = jnp.broadcast_to(columns[:, 2 * pair : 2 * pair + 1], (rows, LANES))
    second = jnp.broadcast_to(columns[:, 2 * pair + 1 : 2 * pair + 2], (rows, LANES))
    return jnp.where(iota((rows, LANES), 1) < WIDTH, first, second)


def spread(columns, low, width):
    parts = [pair_of(columns, (low + at) // LANES) for at in range(0, width, LANES)]
    return jnp.concatenate(parts, 1) if len(parts) > 1 else parts[0]


def head_sums(values, low):
    shape = (values.shape[1], LANES)
    picks = jnp.where(iota(shape, 1) == (iota(shape, 0) + low) // WIDTH, 1.0, 0.0).astype(BF16)
    high, rest = halves(values)
    return nn(high, picks) + nn(rest, picks)


def groups(inner):
    return [(low, min(2 * LANES, inner - low)) for low in range(0, inner, 2 * LANES)]


def from_before(rows, previous, steps):
    turned = pltpu.roll(rows, steps, 0)
    head = pltpu.roll(previous, steps, 0)
    top = jnp.where(iota(head.shape, 0) < steps, head, turned[:8])
    return jnp.concatenate([top, turned[8:]], 0)


def from_after(rows, following, steps):
    count = rows.shape[0]
    turned = pltpu.roll(rows, count - steps, 0)
    tail = pltpu.roll(following, 8 - steps, 0)
    bottom = jnp.where(iota(tail.shape, 0) >= 8 - steps, tail, turned[count - 8 :])
    return jnp.concatenate([turned[: count - 8], bottom], 0)


def softplus(v):
    return jnp.maximum(v, 0.0) + jnp.log1p(jnp.exp(-jnp.abs(v)))


def sigmoid(v):
    return 0.5 + 0.5 * jnp.tanh(0.5 * v)


def halves(value):
    high = value.astype(BF16)
    return high, (value - high.astype(F32)).astype(BF16)


def column(tokens, index, width=LANES):
    return jnp.broadcast_to(tokens[:, index : index + 1], (tokens.shape[0], width))


def conv_taps(taps, rows, previous, visible):
    pre = taps[4:5] + taps[3:4] * rows
    shifted = [rows]
    for steps in range(1, 4):
        moved = from_before(rows, previous, steps) * visible[steps - 1]
        shifted.append(moved)
        pre = pre + taps[3 - steps : 4 - steps] * moved
    return pre, shifted


def mask_of(tokens, seg_row):
    same = tokens[:, 0:1] == seg_row
    count = tokens.shape[0]
    causal = iota((count, count), 0) >= iota((count, count), 1)
    return jnp.where(same & causal, 0.0, VERY_NEGATIVE)


def prepare_kernel(
    ws_ref, cs_ref, csb_ref, cv_ref, cvb_ref, decay_ref, bias_ref, skip_ref, norm_ref, gain_ref,
    packed_ref, taps_ref, heads_ref, norm_out_ref, gain_out_ref,
):
    width = ws_ref.shape[1]
    packed_ref[:, :width] = ws_ref[...]
    taps = jnp.concatenate([cs_ref[...], csb_ref[...][None], jnp.zeros((3, cs_ref.shape[1]), F32)], 0)
    taps = jnp.transpose(jnp.pad(taps, ((0, LANES - 8), (0, LANES - taps.shape[1]))))[: taps.shape[1]]
    for k in range(3):
        high = taps.astype(BF16)
        packed_ref[:, width + LANES * k : width + LANES * (k + 1)] = high
        taps = taps - high.astype(F32)
    inner = cv_ref.shape[1]
    taps_ref[...] = jnp.concatenate([cv_ref[...], cvb_ref[...][None], jnp.zeros((3, inner), F32)], 0)
    rows = [-jnp.exp(decay_ref[...])[None], bias_ref[...][None], skip_ref[...][None]]
    count = decay_ref.shape[0]
    heads_ref[...] = jnp.pad(
        jnp.concatenate(rows + [jnp.zeros((5, count), F32)], 0), ((0, 0), (0, LANES - count))
    )
    norm_out_ref[...] = norm_ref[...][None]
    gain_out_ref[...] = gain_ref[...][None]


def prepare(w_state_t, conv_state, conv_state_bias, conv_value, conv_value_bias, decay, bias, skip, norm, gain):
    state_local, width = w_state_t.shape
    inner = conv_value.shape[1]
    return pl.pallas_call(
        prepare_kernel,
        out_shape=[
            jax.ShapeDtypeStruct((state_local, width + 3 * LANES), BF16),
            jax.ShapeDtypeStruct((8, inner), F32),
            jax.ShapeDtypeStruct((8, LANES), F32),
            jax.ShapeDtypeStruct((1, width), F32),
            jax.ShapeDtypeStruct((1, inner), F32),
        ],
        name="prepare",
    )(w_state_t, conv_state, conv_state_bias, conv_value, conv_value_bias, decay, bias, skip, norm, gain)


def assemble_kernel(count, taps_value_ref, *refs):
    parts, (weights_ref, taps_ref, columns) = refs[:count], refs[count:]
    rows, width = parts[0].shape[0], weights_ref.shape[1]
    inner = taps_value_ref.shape[1]
    place = lax.axis_index("head")
    for steps, part in enumerate(parts):
        at = pl.multiple_of(lax.rem(place - steps + count, count) * rows, rows)
        weights_ref[pl.ds(at, rows), :] = part[:, :width]
        columns[pl.ds(at, rows), :] = sum(
            part[:, width + LANES * k : width + LANES * (k + 1)].astype(F32) for k in range(3)
        )
    taps_ref[:, :inner] = taps_value_ref[...]
    taps_ref[:, inner:] = jnp.transpose(columns[...])[:8]


def assemble(taps_value, parts):
    rows, width = parts[0].shape[0], parts[0].shape[1] - 3 * LANES
    inner, total = taps_value.shape[1], rows * len(parts)
    return pl.pallas_call(
        partial(assemble_kernel, len(parts)),
        out_shape=[
            jax.ShapeDtypeStruct((total, width), BF16),
            jax.ShapeDtypeStruct((8, inner + total), F32),
        ],
        scratch_shapes=[pltpu.VMEM((total, LANES), F32)],
        name="assemble",
    )(taps_value, *parts)


def project_kernel(x_ref, gain_ref, wg_ref, wv_ref, ws_ref, normed_ref, gate_ref, conv_ref, step_ref):
    x = x_ref[...].astype(F32)
    inverse = lax.rsqrt(jnp.mean(x * x, -1, keepdims=True) + EPSILON)
    normed = (x * inverse * gain_ref[...]).astype(BF16)
    normed_ref[...] = normed
    gate_ref[...] = nn(normed, wg_ref[...])
    conv_ref[...] = nn(normed, wv_ref[...]).astype(BF16)
    step = nt(normed, ws_ref[...])
    step_ref[...] = jnp.concatenate([step, jnp.zeros((CHUNK, LANES - step.shape[1]), F32)], 1)


def project(hidden, gain, w_gate, w_value, w_step_t):
    tokens, width = hidden.shape
    inner = w_gate.shape[1]
    rows = lambda n: pl.BlockSpec((CHUNK, n), lambda i: (i, 0))
    whole = lambda a: pl.BlockSpec(a.shape, lambda i: (0, 0), pipeline_mode=ONE)
    return pl.pallas_call(
        project_kernel,
        grid=(tokens // CHUNK,),
        in_specs=[rows(width), whole(gain), whole(w_gate), whole(w_value), whole(w_step_t)],
        out_specs=[rows(width), rows(inner), rows(inner), rows(LANES)],
        out_shape=[
            jax.ShapeDtypeStruct((tokens, width), BF16),
            jax.ShapeDtypeStruct((tokens, inner), F32),
            jax.ShapeDtypeStruct((tokens, inner), BF16),
            jax.ShapeDtypeStruct((tokens, LANES), F32),
        ],
        cost_estimate=pl.CostEstimate(
            flops=2 * tokens * width * (2 * inner + LANES),
            bytes_accessed=tokens * (4 * width + 6 * inner) + 4 * width * inner,
            transcendentals=0,
        ),
        name="project",
    )(hidden, gain, w_gate, w_value, w_step_t)


def scan_kernel(
    cv_ref, cs_ref, halo_ref, step_ref, ids_ref, before_ref, heads_ref, taps_ref,
    y_ref, bc_ref, cum_ref, reach_ref, enter_ref, end_ref, kept_ref, tok_ref, seg_ref,
    carry, state, offset, reached,
):
    at = pl.program_id(0)
    inner = cv_ref.shape[1]
    count = SPAN

    @pl.when(at == 0)
    def _():
        carry[...] = halo_ref[...].astype(F32)
        state[...] = jnp.zeros_like(state)
        offset[...] = jnp.zeros_like(offset)
        reached[...] = jnp.ones_like(reached)

    blocks = ids_ref.shape[0]
    own_row = lambda index: ids_ref[pl.ds(index, 1), :]
    previous = jnp.where(lax.axis_index("seq") == 0, -1, before_ref[blocks - 1 : blocks])
    here = own_row(at)
    earlier = jnp.where(at == 0, previous, own_row(jnp.maximum(at - 1, 0)))
    later = jnp.where(at == blocks - 1, -2, own_row(jnp.minimum(at + 1, blocks - 1)))
    lane = iota((1, LANES), 1)
    seg = here.astype(F32)
    flags = [here == here]
    for steps in range(1, 4):
        moved = jnp.where(lane < steps, pltpu.roll(earlier, steps, 1), pltpu.roll(here, steps, 1))
        flags.append(moved == here)
    for steps in range(1, 4):
        end = lane >= LANES - steps
        moved = jnp.where(end, pltpu.roll(later, LANES - steps, 1), pltpu.roll(here, LANES - steps, 1))
        flags.append(moved == here)
    first_id = own_row(0)[:, :1]
    flags.append(here == earlier[:, LANES - 1 :])
    flags.append(here == here[:, LANES - 1 :])
    flags.append((here == first_id) & (previous[:, LANES - 1 :] == first_id))
    rows = [seg] + [jnp.where(flag, 1.0, 0.0) for flag in flags[1:]]
    tokens = jnp.transpose(jnp.concatenate(rows + [jnp.zeros((LANES - len(rows), LANES), F32)], 0))
    tok_ref[...] = tokens
    seg_ref[0] = jnp.broadcast_to(seg, (8, LANES))
    heads = heads_ref[...]
    step = softplus(step_ref[...] + heads[1:2])
    log_decay = heads[0:1] * step
    lower = jnp.where(iota((count, count), 0) >= iota((count, count), 1), 1.0, 0.0)
    cum = exact(lower, log_decay)
    cum_ref[...] = cum
    kept_ref[0] = reached[...]
    reach = jnp.exp(cum + offset[0:1]) * column(tokens, 9)
    reach_ref[...] = reach
    last = cum[count - 1 : count]
    offset[...] = offset[...] + last
    reached[...] = jnp.broadcast_to(reach[count - 1 : count], reached.shape)
    start = jnp.exp(cum) * column(tokens, 7)
    end = jnp.exp(last - cum) * column(tokens, 8)
    through = start[count - 1 : count]
    cum_t = jnp.transpose(cum)
    visible = [column(tokens, 1 + k, 2 * LANES) for k in range(3)]

    def conv(ref, low, at_column, width):
        rows = ref[:, low : low + width].astype(F32)
        wide = slice(at_column, at_column + width)
        pre, _ = conv_taps(taps_ref[:, wide], rows, carry[:, wide], [v[:, :width] for v in visible])
        carry[:, wide] = rows[count - 8 :]
        return pre * sigmoid(pre)

    both = conv(cs_ref, 0, inner, 2 * STATE).astype(BF16)
    bc_ref[...] = both
    b_low, c_low = both[:, :LANES], both[:, LANES:]
    scores = nt(c_low, b_low)
    hidden_pairs = mask_of(tokens, seg)
    enter_ref[0] = state[...]
    left = iota((count, LANES), 1) < WIDTH
    b_t = jnp.transpose(b_low.astype(F32)).astype(BF16)

    for low, width in groups(inner):
        wide = slice(low, low + width)
        values = conv(cv_ref, low, low, width)
        scaled = values * spread(step, low, width)
        entering = state[:, wide]
        y = spread(start, low, width) * nn(c_low, entering.astype(BF16))
        y = y + spread(heads[2:3], low, width) * values
        inside = []
        for part in range(0, width, LANES):
            weights, mine = [], []
            for side in range(2):
                head = (low + part) // WIDTH + side
                decay = jnp.exp(cum[:, head : head + 1] - cum_t[head : head + 1] + hidden_pairs)
                here = left if side == 0 else ~left
                mine.append(jnp.where(here, scaled[:, part : part + LANES], 0.0).astype(BF16))
                weights.append((decay * scores).astype(BF16))
            inside.append(nn(jnp.concatenate(weights, 1), jnp.concatenate(mine, 0)))
        y_ref[:, wide] = y + jnp.concatenate(inside, 1)
        state[:, wide] = spread(through, low, width) * entering + nn(
            b_t, (scaled * spread(end, low, width)).astype(BF16)
        )
    end_ref[...] = state[...]


def scan(cv, cs, halo, step_raw, ids, ids_before, heads, taps):
    tokens, inner = cv.shape
    blocks = tokens // SPAN
    rows = lambda n: pl.BlockSpec((SPAN, n), lambda i: (i, 0))
    whole = lambda a: pl.BlockSpec(a.shape, lambda i: (0, 0), pipeline_mode=ONE)
    return pl.pallas_call(
        scan_kernel,
        grid=(blocks,),
        in_specs=[
            rows(inner), rows(2 * STATE), whole(halo), rows(LANES), whole(ids), whole(ids_before), whole(heads),
            whole(taps),
        ],
        out_specs=[
            rows(inner), rows(2 * STATE), rows(LANES), rows(LANES),
            pl.BlockSpec((1, STATE, inner), lambda i: (i, 0, 0)),
            pl.BlockSpec((STATE, inner), lambda i: (0, 0)),
            pl.BlockSpec((1, 8, LANES), lambda i: (i, 0, 0)), rows(LANES), pl.BlockSpec((1, 8, SPAN), lambda i: (i, 0, 0)),
        ],
        out_shape=[
            jax.ShapeDtypeStruct((tokens, inner), F32),
            jax.ShapeDtypeStruct((tokens, 2 * STATE), BF16),
            jax.ShapeDtypeStruct((tokens, LANES), F32),
            jax.ShapeDtypeStruct((tokens, LANES), F32),
            jax.ShapeDtypeStruct((blocks, STATE, inner), F32),
            jax.ShapeDtypeStruct((STATE, inner), F32),
            jax.ShapeDtypeStruct((blocks, 8, LANES), F32),
            jax.ShapeDtypeStruct((tokens, LANES), F32),
            jax.ShapeDtypeStruct((blocks, 8, SPAN), F32),
        ],
        scratch_shapes=[
            pltpu.VMEM((8, inner + 2 * STATE), F32),
            pltpu.VMEM((STATE, inner), F32),
            pltpu.VMEM((8, LANES), F32),
            pltpu.VMEM((8, LANES), F32),
        ],
        cost_estimate=pl.CostEstimate(
            flops=2 * tokens * inner * (2 * SPAN + 2 * STATE),
            bytes_accessed=tokens * (6 * inner + 4 * STATE + 8 * LANES),
            transcendentals=tokens * inner * 4,
        ),
        name="scan",
    )(cv, cs, halo, step_raw, ids, ids_before, heads, taps)


def gate_kernel(y_ref, reach_ref, bc_ref, state_ref, gate_ref, gg_ref, gain_ref, low_ref, sums_ref):
    inner = y_ref.shape[1]
    c_low = bc_ref[:, LANES:]
    reach = reach_ref[...]
    squares = jnp.zeros((CHUNK, LANES), F32)
    dots = jnp.zeros((CHUNK, LANES), F32)
    for pair in range(inner // LANES):
        wide = slice(pair * LANES, (pair + 1) * LANES)
        ssm = y_ref[:, wide] + pair_of(reach, pair) * nn(c_low, state_ref[:, wide].astype(BF16))
        gate = gate_ref[:, wide]
        gated = ssm * gate * sigmoid(gate)
        weighted = gated * gain_ref[:, wide]
        low_ref[:, wide] = weighted.astype(BF16)
        squares = squares + gated * gated
        dots = dots + gg_ref[:, wide].astype(F32) * weighted
    square = jnp.sum(squares, 1, keepdims=True)
    dot = jnp.sum(dots, 1, keepdims=True)
    sums_ref[...] = jnp.transpose(jnp.where(iota((CHUNK, LANES), 1) == 0, square, dot))[:8]


def gate_sums(y, reach, bc, state_in, gate_raw, gg, gain):
    tokens, inner = y.shape
    rows = lambda n: pl.BlockSpec((CHUNK, n), lambda i: (i, 0))
    whole = lambda a: pl.BlockSpec(a.shape, lambda i: (0, 0), pipeline_mode=ONE)
    return pl.pallas_call(
        gate_kernel,
        grid=(tokens // CHUNK,),
        in_specs=[
            rows(inner), rows(LANES), rows(2 * STATE), whole(state_in), rows(inner), rows(inner), whole(gain),
        ],
        out_specs=[rows(inner), pl.BlockSpec((8, CHUNK), lambda i: (0, i))],
        out_shape=[
            jax.ShapeDtypeStruct((tokens, inner), BF16),
            jax.ShapeDtypeStruct((8, tokens), F32),
        ],
        cost_estimate=pl.CostEstimate(
            flops=2 * tokens * inner * STATE, bytes_accessed=tokens * inner * 12, transcendentals=tokens * inner
        ),
        name="gate",
    )(y, reach, bc, state_in, gate_raw, gg, gain)


def ungate_kernel(count, y_ref, gate_ref, gg_ref, gain_ref, reach_ref, bc_ref, in_ref, *refs):
    sums_refs, (gs_ref, ggr_ref, low_ref, scale_ref, gain_sum_ref, state_ref, gain_acc, state_acc) = (
        refs[:count], refs[count:]
    )
    at = pl.program_id(0)
    inner = y_ref.shape[1]

    @pl.when(at == 0)
    def _():
        gain_acc[...] = jnp.zeros_like(gain_acc)
        state_acc[...] = jnp.zeros_like(state_acc)

    sums = sum(ref[...] for ref in sums_refs)
    sums = jnp.transpose(jnp.concatenate([sums, jnp.zeros((LANES - 8, CHUNK), F32)], 0))
    all_inner = count * inner
    scale = lax.rsqrt(column(sums, 0) / all_inner + EPSILON)
    shift = scale * scale * scale * column(sums, 1) / all_inner
    scale_ref[...] = scale
    reach = reach_ref[...]
    c_low = bc_ref[:, LANES:]
    c_t = jnp.transpose(c_low.astype(F32)).astype(BF16)
    for pair in range(inner // LANES):
        wide = slice(pair * LANES, (pair + 1) * LANES)
        reach_pair = pair_of(reach, pair)
        ssm = y_ref[:, wide] + reach_pair * nn(c_low, in_ref[:, wide].astype(BF16))
        gate, gg = gate_ref[:, wide], gg_ref[:, wide].astype(F32)
        sg = sigmoid(gate)
        act = gate * sg
        gated = ssm * act
        scaled = gated * scale
        low_ref[:, wide] = (scaled * gain_ref[:, wide]).astype(BF16)
        gain_acc[:, wide] += jnp.sum((gg * scaled).reshape(CHUNK // 8, 8, LANES), 0)
        grad_gated = scale * gg * gain_ref[:, wide] - gated * shift
        grad_ssm = grad_gated * act
        gs_ref[:, wide] = grad_ssm
        ggr_ref[:, wide] = (grad_gated * ssm * sg * (1.0 + gate * (1.0 - sg))).astype(BF16)
        state_acc[:, wide] += nn(c_t, (grad_ssm * reach_pair).astype(BF16))
    gain_sum_ref[...] = gain_acc[...]
    state_ref[...] = state_acc[...]


def ungate(y, gate_raw, gg, gain, reach, bc, state_in, sums):
    tokens, inner = y.shape
    rows = lambda n: pl.BlockSpec((CHUNK, n), lambda i: (i, 0))
    whole = lambda a: pl.BlockSpec(a.shape, lambda i: (0, 0), pipeline_mode=ONE)
    fixed = lambda m, n: pl.BlockSpec((m, n), lambda i: (0, 0))
    return pl.pallas_call(
        partial(ungate_kernel, len(sums)),
        grid=(tokens // CHUNK,),
        in_specs=[
            rows(inner), rows(inner), rows(inner), whole(gain), rows(LANES), rows(2 * STATE), whole(state_in),
        ] + [pl.BlockSpec((8, CHUNK), lambda i: (0, i))] * len(sums),
        out_specs=[rows(inner), rows(inner), rows(inner), rows(LANES), fixed(8, inner), fixed(STATE, inner)],
        out_shape=[
            jax.ShapeDtypeStruct((tokens, inner), F32),
            jax.ShapeDtypeStruct((tokens, inner), BF16),
            jax.ShapeDtypeStruct((tokens, inner), BF16),
            jax.ShapeDtypeStruct((tokens, LANES), F32),
            jax.ShapeDtypeStruct((8, inner), F32),
            jax.ShapeDtypeStruct((STATE, inner), F32),
        ],
        scratch_shapes=[pltpu.VMEM((8, inner), F32), pltpu.VMEM((STATE, inner), F32)],
        cost_estimate=pl.CostEstimate(
            flops=2 * tokens * inner * STATE, bytes_accessed=tokens * inner * 16, transcendentals=tokens * inner
        ),
        name="ungate",
    )(y, gate_raw, gg, gain, reach, bc, state_in, *sums)


def unscan_kernel(
    gs_ref, cv_ref, cv_before_ref, cs_ref, cs_before_ref, halo_ref, bc_ref, step_ref, cum_ref, tok_ref, seg_ref,
    heads_ref, taps_ref, enter_ref, kept_ref, state_in_ref, grad_end_ref, gain_sum_ref,
    value_ref, rest_ref, small_ref, head_rows_ref,
    carry, grad, taps_acc, heads_acc, skip_acc,
):
    turn = pl.program_id(0)
    at = pl.num_programs(0) - 1 - turn
    inner = gs_ref.shape[1]
    count = SPAN

    @pl.when(turn == 0)
    def _():
        carry[...] = jnp.zeros_like(carry)
        grad[...] = grad_end_ref[...]
        taps_acc[...] = jnp.zeros_like(taps_acc)
        heads_acc[...] = jnp.zeros_like(heads_acc)
        skip_acc[...] = jnp.zeros_like(skip_acc)

    first = at == 0
    tokens = tok_ref[...]
    heads = heads_ref[...]
    step_in = step_ref[...] + heads[1:2]
    step = softplus(step_in)
    log_decay = heads[0:1] * step
    cum = cum_ref[...]
    last = cum[count - 1 : count]
    start = jnp.exp(cum) * column(tokens, 7)
    end = jnp.exp(last - cum) * column(tokens, 8)
    through = start[count - 1 : count]
    cum_t = jnp.transpose(cum)
    visible = [column(tokens, 1 + k, 2 * LANES) for k in range(3)]
    seen = [column(tokens, 4 + k, 2 * LANES) for k in range(3)]
    left = iota((count, LANES), 1) < WIDTH
    b_low, c_low = bc_ref[:, :LANES], bc_ref[:, LANES:]
    scores = nt(c_low, b_low)
    hidden_pairs = mask_of(tokens, seg_ref[0, 0:1])
    c_t = jnp.transpose(c_low.astype(F32)).astype(BF16)
    kept = kept_ref[0]

    def conv(ref, before_ref, low, at_column, width):
        rows = ref[:, low : low + width].astype(F32)
        wide = slice(at_column, at_column + width)
        before = before_ref[8:16, low : low + width].astype(F32)
        before = jnp.where(first, halo_ref[:, wide].astype(F32), before)
        pre, shifted = conv_taps(taps_ref[:, wide], rows, before, [v[:, :width] for v in visible])
        return pre, shifted, sigmoid(pre)

    def unconv(grad_out, pre, sg, shifted, at_column, width):
        wide = slice(at_column, at_column + width)
        gp = grad_out * sg * (1.0 + pre * (1.0 - sg))
        eighths = lambda v: jnp.sum(v.reshape(count // 8, 8, width), 0)
        for k in range(4):
            taps_acc[8 * k : 8 * k + 8, wide] += eighths(gp * shifted[3 - k])
        taps_acc[32:40, wide] += eighths(gp)
        taps = taps_ref[:, wide]
        following = carry[:, wide]
        total = taps[3:4] * gp
        for steps in range(1, 4):
            moved = from_after(gp, following, steps) * seen[steps - 1][:, :width]
            total = total + taps[3 - steps : 4 - steps] * moved
        if at_column < inner:
            value_ref[:, wide] = total.astype(BF16)
        else:
            rest_ref[:, :width], rest_ref[:, width : 2 * width] = halves(total)
        carry[:, wide] = gp[:8]

        @pl.when(first)
        def _():
            back = jnp.zeros((8, width), F32)
            for steps in range(1, 4):
                moved = pltpu.roll(gp[:8] * visible[steps - 1][:8, :width], 8 - steps, 0)
                back = back + jnp.where(iota((8, width), 0) >= 8 - steps, taps[3 - steps : 4 - steps] * moved, 0.0)
            head_rows_ref[:, wide] = back

    grad_b = jnp.zeros((count, STATE), F32)
    grad_c = jnp.zeros((count, STATE), F32)
    grad_scores = jnp.zeros((count, count), F32)
    grad_cum = jnp.zeros((count, LANES), F32)
    grad_step = jnp.zeros((count, LANES), F32)
    at_end = jnp.zeros((8, LANES), F32)
    down = []
    for low, width in groups(inner):
        wide = slice(low, low + width)
        pre, shifted, sg = conv(cv_ref, cv_before_ref, low, low, width)
        values = pre * sg
        step_wide = spread(step, low, width)
        scaled = values * step_wide
        scaled_low = scaled.astype(BF16)
        grad_y = gs_ref[:, wide]
        starts, ends = spread(start, low, width), spread(end, low, width)
        entering = enter_ref[0, :, wide] + spread(kept[0:1], low, width) * state_in_ref[:, wide]
        grad_state = grad[:, wide]
        grad_low = grad_state.astype(BF16)
        state_low, state_rest = halves(entering)
        to_end = ends * nn(b_low, grad_low)
        grad_y_in = grad_y * starts
        moved = scaled * to_end
        grad_cum = grad_cum + head_sums(grad_y_in * nn(c_low, state_low) - moved, low)
        through_wide = spread(through, low, width)
        ending = jnp.sum(moved, 0, keepdims=True) + through_wide * jnp.sum(grad_state * entering, 0, keepdims=True)
        at_end = at_end + head_sums(jnp.broadcast_to(ending, (8, width)), low)
        y_rest = grad_y - grad_y.astype(BF16).astype(F32)
        scaled_rest = (scaled - scaled_low.astype(F32)).astype(BF16)
        inside = []
        for part in range(0, width, LANES):
            here_lanes = slice(part, part + LANES)
            y_part, x_part = grad_y[:, here_lanes], scaled[:, here_lanes]
            y_turned, x_turned = pltpu.roll(y_rest[:, here_lanes], WIDTH, 1), pltpu.roll(x_part, WIDTH, 1)
            low_weights, low_mine = [], []
            for side in range(2):
                head = (low + part) // WIDTH + side
                here = left if side == 0 else ~left
                decay = jnp.exp(cum[:, head : head + 1] - cum_t[head : head + 1] + hidden_pairs)
                mine = jnp.where(here, y_part, 0.0).astype(BF16)
                weights = decay * scores
                grad_weights = nt(
                    jnp.concatenate([jnp.where(here, y_part, y_turned).astype(BF16), mine], 1),
                    jnp.concatenate([jnp.where(here, x_part, x_turned).astype(BF16), scaled_rest[:, here_lanes]], 1),
                )
                grad_scores = grad_scores + grad_weights * decay
                change = grad_weights * weights
                across = jnp.sum(change, 1, keepdims=True)
                down.append(jnp.sum(change, 0, keepdims=True))
                grad_cum = grad_cum + jnp.where(iota((count, LANES), 1) == head, across, 0.0)
                low_weights.append(weights.astype(BF16))
                low_mine.append(mine)
            inside.append(tn(jnp.concatenate(low_weights, 0), jnp.concatenate(low_mine, 0)))
        grad_scaled = to_end + jnp.concatenate(inside, 1)
        grad_low_in, grad_rest_in = halves(grad_y_in)
        grad_c = grad_c + nt(grad_low_in, state_low) + nt(grad_rest_in, state_low) + nt(grad_low_in, state_rest)
        grad_b = grad_b + nt((scaled * ends).astype(BF16), grad_low)
        grad[:, wide] = through_wide * grad_state + nn(c_t, grad_low_in)
        grad_step = grad_step + head_sums(grad_scaled * values, low)
        skip_acc[:, wide] += jnp.sum((grad_y * values).reshape(count // 8, 8, width), 0)
        grad_values = grad_scaled * step_wide + spread(heads[2:3], low, width) * grad_y
        unconv(grad_values, pre, sg, shifted, low, width)
    down.append(jnp.zeros((LANES - len(down), count), F32))
    grad_cum = grad_cum - jnp.transpose(jnp.concatenate(down, 0))
    for part in halves(grad_scores):
        grad_c = grad_c + nn(part, b_low)
        grad_b = grad_b + tn(part, c_low)
    pre, shifted, sg = conv(cs_ref, cs_before_ref, 0, inner, 2 * STATE)
    unconv(jnp.concatenate([grad_b, grad_c], 1), pre, sg, shifted, inner, 2 * STATE)
    upper = jnp.where(iota((count, count), 0) <= iota((count, count), 1), 1.0, 0.0)
    grad_log = exact(upper, grad_cum) + at_end[0:1]
    grad_step = grad_step + heads[0:1] * grad_log
    grad_raw = grad_step * sigmoid(step_in)
    rest_ref[:, 4 * STATE :] = grad_raw.astype(BF16)
    heads_acc[...] += jnp.concatenate(
        [
            jnp.sum(grad_log * log_decay, 0, keepdims=True),
            jnp.sum(grad_raw, 0, keepdims=True),
            jnp.zeros((6, LANES), F32),
        ],
        0,
    )

    @pl.when(first)
    def _():
        down_rows = lambda v: jnp.sum(v, 0, keepdims=True)
        skip = sum(head_sums(skip_acc[:, low : low + width], low) for low, width in groups(inner))
        wide = [down_rows(taps_acc[8 * k : 8 * k + 8]) for k in range(5)]
        wide += [heads_acc[0:1], heads_acc[1:2], down_rows(skip), down_rows(gain_sum_ref[...])]
        full = small_ref.shape[1]
        wide = [jnp.concatenate([v, jnp.zeros((1, full - v.shape[1]), F32)], 1) for v in wide]
        small_ref[...] = jnp.concatenate(wide + [jnp.zeros((16 - len(wide), full), F32)], 0)


def unscan(
    gs, cv, cs, halo, bc, step_raw, cum, tokens_info, seg_rows, heads, taps, enter, kept, state_in, grad_end, gain_sum,
    full,
):
    tokens, inner = gs.shape
    blocks = tokens // SPAN
    total = inner + 2 * STATE
    back = lambda i: blocks - 1 - i
    rows = lambda n: pl.BlockSpec((SPAN, n), lambda i: (back(i), 0))
    before = lambda n: pl.BlockSpec((16, n), lambda i: (jnp.maximum(back(i) * (SPAN // 16) - 1, 0), 0))
    whole = lambda a: pl.BlockSpec(a.shape, lambda i: (0, 0), pipeline_mode=ONE)
    fixed = lambda m, n: pl.BlockSpec((m, n), lambda i: (0, 0))
    return pl.pallas_call(
        unscan_kernel,
        grid=(blocks,),
        in_specs=[
            rows(inner), rows(inner), before(inner), rows(2 * STATE), before(2 * STATE), whole(halo), rows(2 * STATE),
            rows(LANES), rows(LANES), rows(LANES), pl.BlockSpec((1, 8, SPAN), lambda i: (back(i), 0, 0)),
            whole(heads), whole(taps), pl.BlockSpec((1, STATE, inner), lambda i: (back(i), 0, 0)),
            pl.BlockSpec((1, 8, LANES), lambda i: (back(i), 0, 0)), whole(state_in), whole(grad_end), whole(gain_sum),
        ],
        out_specs=[rows(inner), rows(4 * STATE + LANES), fixed(16, full), fixed(8, total)],
        out_shape=[
            jax.ShapeDtypeStruct((tokens, inner), BF16),
            jax.ShapeDtypeStruct((tokens, 4 * STATE + LANES), BF16),
            jax.ShapeDtypeStruct((16, full), F32),
            jax.ShapeDtypeStruct((8, total), F32),
        ],
        scratch_shapes=[
            pltpu.VMEM((8, total), F32),
            pltpu.VMEM((STATE, inner), F32),
            pltpu.VMEM((40, total), F32),
            pltpu.VMEM((8, LANES), F32),
            pltpu.VMEM((8, inner), F32),
        ],
        cost_estimate=pl.CostEstimate(
            flops=2 * tokens * inner * (6 * SPAN + 4 * STATE),
            bytes_accessed=tokens * (12 * inner),
            transcendentals=tokens * inner * 6,
        ),
        name="unscan",
    )(gs, cv, cv, cs, cs, halo, bc, step_raw, cum, tokens_info, seg_rows, heads, taps, enter, kept, state_in, grad_end, gain_sum)


def chain_kernel(
    first, size, part_ref, ggr_ref, gv_ref, gr_ref, wg_ref, wv_ref, wb_ref, ws_ref, out_ref,
    mine, outer, inner, sent_in, sent_out, came_outer, came_inner,
):
    turn = pl.program_id(0)
    items = mine.shape[0]
    place = lax.axis_index("head")
    half = size // 2
    low_side = place < half
    depth = jnp.where(low_side, place, size - 1 - place)
    toward = jnp.where(low_side, place + 1, place - 1)
    away = jnp.where(low_side, place - 1, place + 1)
    middle, edge = depth == half - 1, depth == 0
    away = jnp.where(edge, toward, away)

    def signal(target):
        pl.semaphore_signal(
            pltpu.get_barrier_semaphore(), inc=1, device_id={"head": target}, device_id_type=pl.DeviceIdType.MESH
        )

    def copy(source, target, sent, came, device):
        return pltpu.make_async_remote_copy(
            src_ref=source, dst_ref=target, send_sem=sent, recv_sem=came,
            device_id={"head": device}, device_id_type=pl.DeviceIdType.MESH,
        )

    def across(item):
        return copy(mine.at[item], inner.at[item], sent_in.at[item], came_inner.at[item], toward)

    def inward(item):
        return copy(mine.at[item], outer.at[item], sent_in.at[item], came_outer.at[item], toward)

    def outward(item):
        return copy(inner.at[item], inner.at[item], sent_out.at[item], came_inner.at[item], away)

    @pl.when(turn == 0)
    def _():
        signal(toward)

        @pl.when(jnp.logical_not(edge))
        def _():
            signal(away)
            pl.semaphore_wait(pltpu.get_barrier_semaphore(), 2)

        @pl.when(edge)
        def _():
            pl.semaphore_wait(pltpu.get_barrier_semaphore(), 1)

    @pl.when(turn < first)
    def _():
        mine[turn] = part_ref[...]

    @pl.when((turn >= first) & (turn < items) & ((turn - first) % GROUP == 0))
    def _():
        product = nt(ggr_ref[...], wg_ref[...]) + nt(gv_ref[...], wv_ref[...])
        both, steps = wb_ref.shape[0], ws_ref.shape[0]
        product = product + nn(gr_ref[:, :both], wb_ref[...]) + nn(gr_ref[:, both : 2 * both], wb_ref[...])
        product = product + nn(gr_ref[:, 2 * both : 2 * both + steps], ws_ref[...])
        for k in range(GROUP):
            mine[turn + k] = product[k * ITEM : (k + 1) * ITEM].astype(BF16)

    done = turn - behind(size)

    @pl.when(done >= 0)
    def _():
        across(done).wait_recv()

        @pl.when(middle)
        def _():
            inner[done] = (inner[done].astype(F32) + mine[done].astype(F32)).astype(BF16)

        @pl.when(jnp.logical_not(edge))
        def _():
            outward(done).start()

        out_ref[...] = inner[done]
        across(done).wait_send()

    item = turn - LAG * depth

    @pl.when((item >= 0) & (item < items))
    def _():
        @pl.when(jnp.logical_not(edge))
        def _():
            inward(item).wait_recv()
            mine[item] = (mine[item].astype(F32) + outer[item].astype(F32)).astype(BF16)

        @pl.when(middle)
        def _():
            across(item).start()

        @pl.when(jnp.logical_not(middle))
        def _():
            inward(item).start()

    @pl.when(turn == pl.num_programs(0) - 1)
    def _():
        @pl.when(jnp.logical_not(edge))
        def _():
            def wait(item, none):
                outward(item).wait_send()
                return none

            lax.fori_loop(0, items, wait, 0)


LAG = 8


def behind(size):
    return LAG * (size // 2 - 1) + 3


ITEM = 32
GROUP = 8


def chain_sums(part, ggr, grad_value, grad_rest, w_gate, w_value, w_both_t, w_step_t):
    tokens, inner = ggr.shape
    width, columns = w_gate.shape[0], grad_rest.shape[1]
    first = part.shape[0] // ITEM
    items = first + tokens // ITEM
    size = lax.axis_size("head")
    rows = lambda n, at: pl.BlockSpec((ITEM, n), lambda i: (at(i), 0))
    own = lambda n: pl.BlockSpec(
        (GROUP * ITEM, n), lambda i: (jnp.clip((i - first) // GROUP, 0, tokens // ITEM // GROUP - 1), 0)
    )
    whole = lambda a: pl.BlockSpec(a.shape, lambda i: (0, 0), pipeline_mode=ONE)
    slots = lambda: pltpu.VMEM((items, ITEM, width), BF16)
    return pl.pallas_call(
        partial(chain_kernel, first, size),
        grid=(items + behind(size),),
        in_specs=[
            rows(width, lambda i: jnp.minimum(i, first - 1)), own(inner), own(inner), own(columns), whole(w_gate),
            whole(w_value), whole(w_both_t), whole(w_step_t),
        ],
        out_specs=rows(width, lambda i: jnp.maximum(i - behind(size), 0)),
        out_shape=jax.ShapeDtypeStruct((items * ITEM, width), BF16),
        scratch_shapes=[slots(), slots(), slots()] + [pltpu.SemaphoreType.DMA((items,))] * 4,
        compiler_params=pltpu.CompilerParams(collective_id=0, has_side_effects=True),
        cost_estimate=pl.CostEstimate(
            flops=2 * tokens * width * (2 * inner + columns), bytes_accessed=600_000_000, transcendentals=0
        ),
        name="chain",
    )(part, ggr, grad_value, grad_rest, w_gate, w_value, w_both_t, w_step_t)


def finish_kernel(
    early, scale_ref, out_a_ref, out_b_ref, grad_ref, x_ref, cot_ref, gain_ref, a_ref, b_ref, c_ref,
    mixed_ref, grad_out_ref, a_out_ref, b_out_ref, c_out_ref,
):
    at = pl.program_id(0)
    x = x_ref[...].astype(F32)
    scale = scale_ref[:, 0:1]

    @pl.when(at < early)
    def _():
        mixed_ref[...] = (x + scale * out_a_ref[...].astype(F32)).astype(BF16)

    @pl.when(at >= early)
    def _():
        mixed_ref[...] = (x + scale * out_b_ref[...].astype(F32)).astype(BF16)

    width = x.shape[1]
    inverse = lax.rsqrt(jnp.mean(x * x, -1, keepdims=True) + EPSILON)
    weighted = grad_ref[...].astype(F32) * gain_ref[...]
    dot = jnp.sum(weighted * x, -1, keepdims=True)
    grad_out_ref[...] = cot_ref[...].astype(F32) + inverse * weighted - x * (inverse**3 * dot / width)
    a_out_ref[...] = a_ref[...].astype(F32)
    b_out_ref[...] = b_ref[...].astype(F32)
    c_out_ref[...] = c_ref[...].astype(F32)


def finish(scale, out_early, chained, hidden, cotangent, gain, sums):
    tokens, width = hidden.shape
    steps = tokens // SPAN
    early = out_early.shape[0] // SPAN
    late = steps - early
    rows = lambda n, at=lambda i: i: pl.BlockSpec((SPAN, n), lambda i: (at(i), 0))
    parts = [pl.BlockSpec((a.shape[0] // steps, a.shape[1]), lambda i: (i, 0)) for a in sums]
    return pl.pallas_call(
        partial(finish_kernel, early),
        grid=(steps,),
        in_specs=[
            rows(LANES), rows(width, lambda i: jnp.minimum(i, early - 1)), rows(width, lambda i: jnp.maximum(i - early, 0)),
            rows(width, lambda i: i + late), rows(width), rows(width), pl.BlockSpec((1, width), lambda i: (0, 0)),
        ] + parts,
        out_specs=[rows(width), rows(width)] + parts,
        out_shape=[jax.ShapeDtypeStruct((tokens, width), BF16), jax.ShapeDtypeStruct((tokens, width), F32)]
        + [jax.ShapeDtypeStruct(a.shape, F32) for a in sums],
        cost_estimate=pl.CostEstimate(flops=0, bytes_accessed=80_000_000, transcendentals=0),
        name="finish",
    )(scale, out_early, chained, chained, hidden, cotangent, gain, *sums)


def pack_kernel(rest_ref, wb_ref, ws_ref, pg_ref, pv_ref, norm_ref, small_ref, packed_ref):
    both, steps = wb_ref.shape[0], ws_ref.shape[0]
    state = rest_ref[:both] + rest_ref[both : 2 * both]
    step = rest_ref[2 * both : 2 * both + steps]
    products = jnp.sum(state * wb_ref[...].astype(F32), 0, keepdims=True) + pg_ref[...][None] + pv_ref[...][None]
    products = products + jnp.sum(step * ws_ref[...].astype(F32), 0, keepdims=True)
    packed_ref[:both] = state
    packed_ref[both : both + 16] = rest_ref[2 * both : 2 * both + 16]
    small = small_ref[...]
    packed_ref[both + 16 :] = jnp.where(iota(small.shape, 0) == 9, products / norm_ref[...], small)


def pack(grad_rest_t, w_both_t, w_step_t, products_gate, products_value, norm, small):
    both, width = w_both_t.shape
    return pl.pallas_call(
        pack_kernel,
        out_shape=jax.ShapeDtypeStruct((both + 32, width), F32),
        name="pack",
    )(grad_rest_t, w_both_t, w_step_t, products_gate, products_value, norm, small)


def unpack_kernel(
    count, packed_ref, *refs
):
    others, refs = refs[: count - 1], refs[count - 1 :]
    state_ref, step_ref, norm_ref, cv_ref, cvb_ref, cs_ref, csb_ref, decay_ref, bias_ref, skip_ref, gain_ref = refs
    state_local, heads, inner = state_ref.shape[0], step_ref.shape[0], cv_ref.shape[1]
    both = state_local * count
    place = lax.axis_index("head")
    own = packed_ref[pl.ds(pl.multiple_of(place * state_local, state_local), state_local), :]
    state_ref[...] = own + sum(ref[:state_local].astype(F32) for ref in others)
    step_ref[...] = packed_ref[both : both + heads]
    small = packed_ref[both + 16 :]
    total = small + sum(ref[state_local:].astype(F32) for ref in others)
    norm_ref[...] = total[9]
    cv_ref[...] = small[:4, :inner]
    cvb_ref[...] = small[4, :inner]
    for q in range(count):
        @pl.when(place == q)
        def _(q=q):
            mine = total[:8, inner + q * state_local : inner + (q + 1) * state_local]
            cs_ref[...] = mine[:4]
            csb_ref[...] = mine[4]
    decay_ref[...] = small[5, :heads]
    bias_ref[...] = small[6, :heads]
    skip_ref[...] = small[7, :heads]
    gain_ref[...] = small[8, :inner]


def unpack(packed, others, inner, heads, state_local):
    width = packed.shape[1]
    shapes = [
        (state_local, width), (heads, width), (width,), (4, inner), (inner,), (4, state_local), (state_local,),
        (heads,), (heads,), (heads,), (inner,),
    ]
    return pl.pallas_call(
        partial(unpack_kernel, len(others) + 1),
        out_shape=[jax.ShapeDtypeStruct(shape, F32) for shape in shapes],
        name="unpack",
    )(packed, *others)


def passed_along(value, axis, steps):
    count = lax.axis_size(axis)
    first, last = (max(0, -steps), min(count, count - steps))
    return lax.ppermute(value, axis, [(source, source + steps) for source in range(first, last)])


def from_all(value, axis):
    count = lax.axis_size(axis)
    moved = lambda steps: lax.ppermute(value, axis, [(s, (s + steps) % count) for s in range(count)])
    return [value] + [moved(steps) for steps in range(1, count)]


def row_major(value):
    return with_layout_constraint(value, Layout(major_to_minor=(0, 1)))


def on_device(
    hidden, segment_ids, norm_gain, w_gate, w_value, w_state, w_step, conv_value, conv_value_bias, conv_state,
    conv_state_bias, decay_log, step_bias, skip_gain, gate_gain, w_out, cotangent,
):
    tokens, width = hidden.shape
    inner, heads_local, state_local = w_value.shape[1], w_step.shape[1], w_state.shape[1]
    count, place = lax.axis_size("head"), lax.axis_index("head")

    ids = segment_ids.reshape(tokens // SPAN, SPAN)
    packed, taps_value, heads, norm, gain = prepare(
        w_state.T, conv_state, conv_state_bias, conv_value, conv_value_bias, decay_log, step_bias, skip_gain,
        norm_gain, gate_gain,
    )
    parts = from_all(packed, "head")
    ids_before = passed_along(ids, "seq", 1)
    w_step_t = jnp.pad(w_step.T, ((0, 16 - heads_local), (0, 0)))

    normed, gate_raw, cv, step_raw = project(hidden, norm, w_gate, w_value, w_step_t)
    w_both_t, taps = assemble(taps_value, parts)
    cs = nt(normed, w_both_t).astype(BF16)
    tail = jnp.concatenate([cv[tokens - 8 :], cs[tokens - 8 :]], 1)
    halo = passed_along(tail, "seq", 1)
    gg = nt(cotangent, w_out).astype(BF16)
    y, bc, cum, reach, enter, local_end, kept, tokens_info, seg_rows = scan(
        cv, cs, halo, step_raw, ids, ids_before, heads, taps
    )
    state_in = passed_along(local_end, "seq", 1)
    low, sums = gate_sums(y, reach, bc, state_in, gate_raw, gg, gain)
    sums = from_all(sums, "head")
    early = EARLY * ITEM
    out_early = lax.psum(nn(low[:early], w_out).astype(BF16), "head")
    out_late = nn(low[early:], w_out).astype(BF16)

    gs, grad_gate_raw, gate_low, scale, gain_sum, grad_state_in = ungate(
        y, gate_raw, gg, gain, reach, bc, state_in, sums
    )
    grad_end = passed_along(grad_state_in, "seq", -1)
    grad_w_out = row_major(tn(gate_low, cotangent))
    grad_value, grad_rest, small, head_rows = unscan(
        gs, cv, cs, halo, bc, step_raw, cum, tokens_info, seg_rows, heads, taps, enter, kept, state_in, grad_end,
        gain_sum, width,
    )
    from_next = passed_along(head_rows, "seq", -1)
    grad_w_gate = row_major(tn(normed, grad_gate_raw))

    def with_next(a, low, high):
        tail = (a[tokens - 8 :, : high - low].astype(F32) + from_next[:, low:high]).astype(BF16)
        return lax.dynamic_update_slice(a, tail, (tokens - 8, 0))

    grad_value = with_next(grad_value, 0, inner)
    grad_rest = with_next(grad_rest, inner, inner + 2 * STATE)
    grad_w_value = row_major(tn(normed, grad_value))
    grad_rest_t = row_major(tn(grad_rest, normed))
    chained = chain_sums(out_late, grad_gate_raw, grad_value, grad_rest, w_gate, w_value, w_both_t, w_step_t)

    packed = pack(
        grad_rest_t, w_both_t, w_step_t, jnp.sum(w_gate.astype(F32) * grad_w_gate, 1),
        jnp.sum(w_value.astype(F32) * grad_w_value, 1), norm, small,
    )
    weights = lax.psum(tuple(a.astype(BF16) for a in (grad_w_gate, grad_w_value, grad_w_out)), "seq")
    packed = lax.psum(packed, "seq")

    def part(steps):
        rows = lax.dynamic_slice_in_dim(packed, lax.rem(place + steps, count) * state_local, state_local, 0)
        return jnp.concatenate([rows, packed[2 * STATE + 16 :]], 0).astype(BF16)

    others = [
        lax.ppermute(part(steps), "head", [(s, (s + steps) % count) for s in range(count)])
        for steps in range(1, count)
    ]
    mixed, grad_hidden, *weights = finish(scale, out_early, chained, hidden, cotangent, norm, weights)
    state_t, step_t, *rest = unpack(packed, others, inner, heads_local, state_local)
    return (mixed, grad_hidden, rest[0], weights[0], weights[1], state_t.T, step_t.T, *rest[1:], weights[2])


def solution(mesh):
    columns, split = P(None, "head"), P("head")
    rows = P("seq", None)

    return jax.shard_map(
        on_device,
        mesh=mesh,
        in_specs=(
            rows, P("seq"), P(), columns, columns, columns, columns, columns, split, columns, split, split, split,
            split, split, P("head", None), rows,
        ),
        out_specs=(
            rows, rows, P(), columns, columns, columns, columns, columns, split, columns, split, split, split, split,
            split, P("head", None),
        ),
        check_vma=False,
    )
```

time: 1760 us -> 722 us (0.41)
  waiting for transfers between devices: 989 us -> 82.6 us
  Pallas kernels: 0 us -> 519 us
  other arithmetic: 223 us -> 0.85 us
  matrix products: 286 us -> 66 us
  local copies, waits for them, and re-layouts: 172 us -> 9.97 us
  blocking collectives: 54.1 us -> 0 us
  starting transfers between devices: 9.47 us -> 27.1 us
    psum x2 -> x3, waiting for transfers between devices: 988 us -> 73.9 us  [the longest x1 47.4 us: on_device(): packed = lax.psum(packed, 'seq')]
    pallas_call x0 -> x11, Pallas kernels: none -> 519 us  [the longest x1 339 us: chain_sums(): pl.pallas_call(partial(chain_kernel, first, size), grid=(items + behind(s...]
    dot_general x22 -> x8, matrix products: 286 us -> 66 us  [the longest x4 41 us: tn(): lax.dot_general(a, b, (((0,), (0,)), ((), ())), preferred_element_type=F32)]
    reduce_sum x19 -> x0, other arithmetic: 72.9 us -> none  [the longest x1 20.4 us: conv_piece(): kernel[tap_index][None, :] * extended[tap_index:tap_index + tokens]]
    psum x3 -> x0, blocking collectives: 45.5 us -> none  [the longest x1 24.4 us: on_device(): lax.psum((grad_norm_gain, grad_w_local[:, :inner_local], grad_w_local[:,...]
    unnamed x207 -> x42, local copies, waits for them, and re-layouts: 49.8 us -> 5.64 us
    another operation x9 -> x0, other arithmetic: 30 us -> none
    slice x25 -> x3, local copies, waits for them, and re-layouts: 29.7 us -> 1.61 us  [the longest x1 0.9 us: part(): return jnp.concatenate([rows, packed[2 * STATE + 16:]], 0).astype(BF16)]
  transfers between devices with their start and end apart: 9 -> 17, of which waited for: 2 -> 6; matrix products, arithmetic and copies ran while one was open for 23% -> 6% of each run, Pallas kernels for 0% -> 50%
where the time goes in v1:
time: 722 us; the launch traced here: 720 us
  Pallas kernels  519 us (72%)
  waiting for transfers between devices  82.6 us (11%)
  matrix products  66 us (9%)
  starting transfers between devices  27.1 us (4%)
  between operations  14.1 us (2%)
  local copies, waits for them, and re-layouts  9.97 us (1%)
    pallas_call x1, Pallas kernels, chain_sums(): pl.pallas_call(partial(chain_kernel, first, size), grid=(items + behind(s...  339 us
    pallas_call x1, Pallas kernels, unscan(): pl.pallas_call(unscan_kernel, grid=(blocks,), in_specs=[rows(inner), rows...  66.5 us
    psum x1, waiting for transfers between devices, on_device(): packed = lax.psum(packed, 'seq')  47.4 us
    dot_general x4, matrix products, tn(): lax.dot_general(a, b, (((0,), (0,)), ((), ())), preferred_element_type=F32)  41 us
    pallas_call x1, Pallas kernels, scan(): pl.pallas_call(scan_kernel, grid=(blocks,), in_specs=[rows(inner), rows(2...  29.3 us
    pallas_call x1, Pallas kernels, finish(): pl.pallas_call(partial(finish_kernel, early), grid=(steps,), in_specs=[ro...  27.8 us
    psum x1, waiting for transfers between devices, on_device(): lax.psum(tuple((a.astype(BF16) for a in (grad_w_gate, grad_w_value, grad_...  26.5 us
    pallas_call x1, Pallas kernels, project(): pl.pallas_call(project_kernel, grid=(tokens // CHUNK,), in_specs=[rows(wi...  17.8 us
  transfers between devices with their start and end apart: 17, of which 6 were waited for; matrix products, arithmetic and copies ran while one was open for 6% of the time, Pallas kernels for 50%

profile of v1, /device:TPU:0, one launch (start us, length us, event | category | flops | bytes accessed | tf_op | source)
XLA Modules:
  0.0 720.0 jit_solution(9677905928706648612)
XLA Ops:
  9.2 3.1 collective-permute-start
  12.2 2.6 collective-permute-start.1
  17.6 17.8 %project.1 = (bf16[2048,1536]{1,0:T(8,128)(2,1)}, f32[2048,768]{1,0:T(8,128)}, bf16[2048,768]{1,0:T(8,128)(2,1)}, f32[2048,128]{1,0:T(8,128)}) custom-call(bf16[2048,1536]{1,0:T(8,128)(2,1)} %x_ref.3, f32[1,1536]{1,0:T(1,128)} %get-tuple-element.64.gain_ref.norm_ref, bf16[1536,768]{1,0:T(8,128)(2,1)} %wg_ref.3, bf16[1536,768]{1,0:T(8,128)(2,1)} %wv_ref.3, ...), custom_call_target="tpu_custom_call" | custom-call | flops 10468982784 | bytes 26738688 | tf_op jit(solution)/shard_map/project/pallas_call | solution.py:203
  39.3 4.8 convolution_convert_fusion.4.cs_ref.cs_before_ref
  45.4 4.1 collective-permute-start.4
  51.0 29.3 %scan.1 = (f32[2048,768]{1,0:T(8,128)}, bf16[2048,256]{1,0:T(8,128)(2,1)}, f32[2048,128]{1,0:T(8,128)}, f32[2048,128]{1,0:T(8,128)}, f32[16,128,768]{2,1,0:T(8,1...) custom-call(bf16[2048,768]{1,0:T(8,128)(2,1)} %get-tuple-element.65.cv_ref.cv_bef, ...), custom_call_target="tpu_custom_call" | custom-call | flops 1610612736 | bytes 12582912 | tf_op jit(solution)/shard_map/scan/pallas_call | solution.py:326
  82.6 9.3 %convolution_convert_fusion.3.gg_ref = bf16[2048,768]{1,0:T(8,128)(2,1)} fusion(bf16[2048,1536]{1,0:T(8,128)(2,1)} %cot_ref.1, bf16[768,1536]{1,0:T(8,128)(2,1)S(1)} %copy-done), kind=kOutput, calls=%fused_computation.5 | convolution fusion | flops 4833411072 | bytes 11796480 | tf_op jit(solution)/shard_map/dot_general | solution.py:30
  92.6 11.6 %gate.1 = (bf16[2048,768]{1,0:T(8,128)(2,1)}, f32[8,2048]{1,0:T(8,128)}) custom-call(f32[2048,768]{1,0:T(8,128)} %get-tuple-element.73.y_ref, f32[2048,128]{1,0:T(8,128)} %get-tuple-element.76.reach_ref, bf16[2048,256]{1,0:T(8,128)(2,1)} %get-tuple-element.77.bc_ref, f32[128,768]{1,0:T(8,128)} %copy-done.2, f32[2048,768]{1,0:T(8,128)} %get-tuple-element.74.gate_ref, ...), custom_call_target="tpu_custom_call" | custom-call | flops 402653184 | bytes 18874368 | tf_op jit(solution)/shard_map/gate/pallas_call | solution.py:389
  108.1 2.6 collective-permute-done.6.refs_1_
  110.6 2.8 collective-permute-done.7.refs_2_
  114.7 16.3 %ungate.1 = (f32[2048,768]{1,0:T(8,128)}, bf16[2048,768]{1,0:T(8,128)(2,1)}, bf16[2048,768]{1,0:T(8,128)(2,1)}, f32[2048,128]{1,0:T(8,128)}, f32[8,768]{1,0:T(8,128)}, /*index=5*/f32[128,768]{1,0:T(8,128)}) custom-call(f32[2048,768]{1,0:T(8,128)} %get-tuple-element.73.y_ref, f32[2048,768]{1,0:T(8,128)} %get-tuple-element.74.gate_ref, ...), custom_call_target="tpu_custom_call" | custom-call | flops 402653184 | bytes 25165824 | tf_op jit(solution)/shard_map/ungate/pallas_call | solution.py:453
  135.5 66.5 %unscan.1 = (bf16[2048,768]{1,0:T(8,128)(2,1)}, bf16[2048,640]{1,0:T(8,128)(2,1)}, f32[16,1536]{1,0:T(8,128)}, f32[8,1024]{1,0:T(8,128)}) custom-call(f32[2048,768]{1,0:T(8,128)} %get-tuple-element.83.gs_ref, bf16[2048,768]{1,0:T(8,128)(2,1)} %get-tuple-element.65.cv_ref.cv_before_ref, bf16[2048,768]{1,0:T(8,128)(2,1)} %get-tuple-element.65.cv_ref.cv_before_ref, ...), custom_call_target="tpu_custom_call" | custom-call | flops 4026531840 | bytes 18874368 | tf_op jit(solution)/shard_map/unscan/pallas_call | solution.py:657
  203.3 10.4 %multiply_reduce_fusion.1 = (f32[1536]{0:T(1024)}, bf16[1536,768]{1,0:T(8,128)(2,1)}) fusion(bf16[1536,768]{1,0:T(8,128)(2,1)} %wg_ref.3, bf16[2048,1536]{1,0:T(8,128)(2,1)} %get-tuple-element.66, bf16[2048,768]{1,0:T(8,128)(2,1)} %get-tuple-element.82.ggr_ref), kind=kOutput, calls=%fused_computation.2 | convolution fusion | flops 4836555264 | bytes 14161920 | tf_op jit(solution)/shard_map/dot_general | solution.py:34
  213.8 10.0 %fusion.6.rest_ref = f32[640,1536]{1,0:T(8,128)} fusion(bf16[2048,640]{1,0:T(8,128)(2,1)S(1)} %fusion.5.gr_ref, bf16[2048,1536]{1,0:T(8,128)(2,1)} %get-tuple-element.66), kind=kOutput, calls=%fused_computation.23 | convolution fusion | flops 4026531840 | bytes 12845056 | tf_op jit(solution)/shard_map/dot_general | solution.py:34
  223.8 11.3 %multiply_reduce_fusion = (f32[1536]{0:T(1024)}, bf16[1536,768]{1,0:T(8,128)(2,1)}) fusion(bf16[1536,768]{1,0:T(8,128)(2,1)S(1)} %copy-done.18, bf16[2048,1536]{1,0:T(8,128)(2,1)} %get-tuple-element.66, bf16[2048,768]{1,0:T(8,128)(2,1)S(1)} %fusion.3.gv_ref), kind=kOutput, calls=%fused_computation.1 | convolution fusion | flops 4836555264 | bytes 14161920 | tf_op jit(solution)/shard_map/dot_general | solution.py:34
  235.1 3.9 pack.1
  239.1 6.3 convolution_convert_fusion
  245.6 9.2 %convolution_convert_fusion.1 = bf16[768,1536]{1,0:T(8,128)(2,1)} fusion(bf16[2048,768]{1,0:T(8,128)(2,1)} %get-tuple-element.94, bf16[2048,1536]{1,0:T(8,128)(2,1)} %cot_ref.1), kind=kOutput, calls=%fused_computation.3 | convolution fusion | flops 4833017856 | bytes 11796480 | tf_op jit(solution)/shard_map/dot_general | solution.py:34
  254.9 4.7 convolution_convert_fusion.2.part_ref
  259.6 47.4 %all-reduce.8.cloned.1.call-done.packed_ref = f32[288,1536]{1,0:T(8,128)} async-done(((f32[288,1536]{1,0:T(8,128)}), f32[288,1536]{1,0:T(8,128)}) %all-reduce.8.cloned.1.call-update) | async-done | bytes 1769488 | tf_op jit(solution)/shard_map/psum | solution.py:1022
  315.5 339.3 %chain.1.out_b_ref.grad_ref = bf16[2816,1536]{1,0:T(8,128)(2,1)} custom-call(bf16[768,1536]{1,0:T(8,128)(2,1)} %convolution_convert_fusion.2.part_ref, bf16[2048,768]{1,0:T(8,128)(2,1)} %get-tuple-element.82.ggr_ref, bf16[2048,768]{1,0:T(8,128)(2,1)} %copy-done.15, bf16[2048,640]{1,0:T(8,128)(2,1)} %copy-done.17, bf16[1536,768]{1,0:T(8,128)(2,1)} %wg_ref.3, ...), custom_call_target="tpu_custom_call" | custom-call | flops 13690208256 | bytes 600000000 | tf_op jit(solution)/shard_map/chain/pallas_call | solution.py:818
  656.3 2.8 unpack.1
  659.2 26.5 %all-reduce.10.cloned.1.call-done = (bf16[1536,768]{1,0:T(8,128)(2,1)}, bf16[1536,768]{1,0:T(8,128)(2,1)}, bf16[768,1536]{1,0:T(8,128)(2,1)}) async-done(((bf16[1536,768]{1,0:T(8,128)(2,1)}, bf16[1536,768]{1,0:T(8,128)(2,1)}, bf16[768,1536]{1,0:T(8,128)(2,1)}), (bf16[1536,768]{1,0:T(8,128)(2,1)}, bf16[1536,768]{1,0:T(8,128)(2,1)}, bf16[768,1536]{1,0:T(8,128)(2,1)})) %all-reduce.10.cloned.1.call-update) | async-done | bytes 7077904 | tf_op jit(solution)/shard_map/psum | solution.py:1021
  685.6 27.8 %finish.1 = (bf16[2048,1536]{1,0:T(8,128)(2,1)}, f32[2048,1536]{1,0:T(8,128)}, f32[1536,768]{1,0:T(8,128)}, f32[1536,768]{1,0:T(8,128)}, f32[768,1536]{1,0:T(8,128)}) custom-call(f32[2048,128]{1,0:T(8,128)} %get-tuple-element.80.scale_ref, bf16[1280,1536]{1,0:T(8,128)(2,1)} %all-reduce.6.cloned.1.call-done.out_a_ref, ...), custom_call_target="tpu_custom_call" | custom-call | bytes 80000000 | tf_op jit(solution)/shard_map/finish/pallas_call | solution.py:869
  (83 shorter events, 35.7 us)
Async XLA Ops:
  7.2 75.4 %copy-start = (bf16[768,1536]{1,0:T(8,128)(2,1)S(1)}, bf16[768,1536]{1,0:T(8,128)(2,1)}, u32[]{:S(2)}) copy-start(bf16[768,1536]{1,0:T(8,128)(2,1)} %param.32) | copy-start | bytes 7077892
  7.2 299.8 %all-reduce.8.cloned.1.call-start = ((), (), s32[]{:S(2)}) async-start(), calls=%async_computation.1 | async-start | bytes 3538944 | tf_op jit(solution)/shard_map/psum | solution.py:1022
  9.2 26.9 %collective-permute-start = (bf16[64,1920]{1,0:T(8,128)(2,1)}, bf16[64,1920]{1,0:T(8,128)(2,1)S(1)}, u32[]{:S(2)}, u32[]{:S(2)}) collective-permute-start(bf16[64,1920]{1,0:T(8,128)(2,1)} %get-tuple-element.68.refs_0_), channel_id=1, source_target_pairs={{0,1},{1,2},{2,3},{3,0},{4,5},{5,6},{6,7},{7,4},{8,9},{9,10},{10,1... | collective-permute-start | bytes 737288 | tf_op jit(solution)/shard_map/ppermute | solution.py:954
  12.2 23.9 %collective-permute-start.1 = (bf16[64,1920]{1,0:T(8,128)(2,1)}, bf16[64,1920]{1,0:T(8,128)(2,1)S(1)}, u32[]{:S(2)}, u32[]{:S(2)}) collective-permute-start(bf16[64,1920]{1,0:T(8,128)(2,1)} %get-tuple-element.68.refs_0_), channel_id=1, source_target_pairs={{0,2},{1,3},{2,0},{3,1},{4,6},{5,7},{6,4},{7,5},{8,10},{9,11},{10,... | collective-permute-start | bytes 737288 | tf_op jit(solution)/shard_map/ppermute | solution.py:954
  14.8 21.3 %collective-permute-start.2 = (bf16[64,1920]{1,0:T(8,128)(2,1)}, bf16[64,1920]{1,0:T(8,128)(2,1)S(1)}, u32[]{:S(2)}, u32[]{:S(2)}) collective-permute-start(bf16[64,1920]{1,0:T(8,128)(2,1)} %get-tuple-element.68.refs_0_), channel_id=1, source_target_pairs={{0,3},{1,0},{2,1},{3,2},{4,7},{5,4},{6,5},{7,6},{8,11},{9,8},{10,9... | collective-permute-start | bytes 737288 | tf_op jit(solution)/shard_map/ppermute | solution.py:954
  44.1 6.3 copy-start.1
  44.1 6.3 collective-permute-start.3
  45.4 4.9 collective-permute-start.4
  80.3 11.6 %collective-permute-start.5 = (f32[128,768]{1,0:T(8,128)}, f32[128,768]{1,0:T(8,128)S(1)}, u32[]{:S(2)}, u32[]{:S(2)}) collective-permute-start(f32[128,768]{1,0:T(8,128)} %get-tuple-element.78), channel_id=1, source_target_pairs={{0,4},{4,8},{8,12},{12,16},{16,20},{20,24},{24,28},{1,5},{5,9},{9,... | collective-permute-start | bytes 1179656 | tf_op jit(solution)/shard_map/ppermute | solution.py:949
  104.2 6.4 collective-permute-start.6
  104.9 8.6 %collective-permute-start.7 = (f32[8,2048]{1,0:T(8,128)}, f32[8,2048]{1,0:T(8,128)S(1)}, u32[]{:S(2)}, u32[]{:S(2)}) collective-permute-start(f32[8,2048]{1,0:T(8,128)} %get-tuple-element.79.refs_0_), channel_id=1, source_target_pairs={{0,2},{1,3},{2,0},{3,1},{4,6},{5,7},{6,4},{7,5},{8,10},{9,11},{10,... | collective-permute-start | bytes 196616 | tf_op jit(solution)/shard_map/ppermute | solution.py:954
  106.5 7.0 collective-permute-start.8
  131.0 3.8 collective-permute-start.9
  202.0 11.7 %collective-permute-start.10 = (f32[8,1024]{1,0:T(8,128)}, f32[8,1024]{1,0:T(8,128)S(1)}, u32[]{:S(2)}, u32[]{:S(2)}) collective-permute-start(f32[8,1024]{1,0:T(8,128)} %get-tuple-element.92), channel_id=1, source_target_pairs={{4,0},{8,4},{12,8},{16,12},{20,16},{24,20},{28,24},{5,1},{9,5},{13... | collective-permute-start | bytes 98312 | tf_op jit(solution)/shard_map/ppermute | solution.py:949
  203.3 10.4 %copy-start.16 = (bf16[2048,640]{1,0:T(8,128)(2,1)S(1)}, bf16[2048,640]{1,0:T(8,128)(2,1)}, u32[]{:S(2)}) copy-start(bf16[2048,640]{1,0:T(8,128)(2,1)} %get-tuple-element.93) | copy-start | bytes 7864324
  213.8 10.0 %copy-start.17 = (bf16[2048,640]{1,0:T(8,128)(2,1)}, bf16[2048,640]{1,0:T(8,128)(2,1)S(1)}, u32[]{:S(2)}) copy-start(bf16[2048,640]{1,0:T(8,128)(2,1)S(1)} %fusion.5.gr_ref) | copy-start | bytes 7864324
  213.8 10.0 %copy-start.14 = (bf16[2048,768]{1,0:T(8,128)(2,1)S(1)}, bf16[2048,768]{1,0:T(8,128)(2,1)}, u32[]{:S(2)}) copy-start(bf16[2048,768]{1,0:T(8,128)(2,1)} %get-tuple-element.91) | copy-start | bytes 9437188
  213.8 10.0 %copy-start.18 = (bf16[1536,768]{1,0:T(8,128)(2,1)S(1)}, bf16[1536,768]{1,0:T(8,128)(2,1)}, u32[]{:S(2)}) copy-start(bf16[1536,768]{1,0:T(8,128)(2,1)} %wv_ref.3) | copy-start | bytes 7077892
  223.8 11.3 %copy-start.15 = (bf16[2048,768]{1,0:T(8,128)(2,1)}, bf16[2048,768]{1,0:T(8,128)(2,1)S(1)}, u32[]{:S(2)}) copy-start(bf16[2048,768]{1,0:T(8,128)(2,1)S(1)} %fusion.3.gv_ref) | copy-start | bytes 9437188
  239.0 420.1 %all-reduce.6.cloned.1.call-start = ((), (), s32[]{:S(2)}) async-start(), calls=%async_computation | async-start | bytes 7864320 | tf_op jit(solution)/shard_map/psum | solution.py:992
  245.4 440.3 %all-reduce.10.cloned.1.call-start = ((), (), s32[]{:S(2)}) async-start(), calls=%async_computation.2 | async-start | bytes 14155776 | tf_op jit(solution)/shard_map/psum | solution.py:1021
  310.1 344.8 %collective-permute-start.11 = (bf16[80,1536]{1,0:T(8,128)(2,1)}, bf16[80,1536]{1,0:T(8,128)(2,1)S(1)}, u32[]{:S(2)}, u32[]{:S(2)}) collective-permute-start(bf16[80,1536]{1,0:T(8,128)(2,1)} %get-tuple-element.124), channel_id=1, source_target_pairs={{0,1},{1,2},{2,3},{3,0},{4,5},{5,6},{6,7},{7,4},{8,9},{9,10},{10,1... | collective-permute-start | bytes 737288 | tf_op jit(solution)/shard_map/ppermute | solution.py:1029
  311.7 343.2 %collective-permute-start.12 = (bf16[80,1536]{1,0:T(8,128)(2,1)}, bf16[80,1536]{1,0:T(8,128)(2,1)S(1)}, u32[]{:S(2)}, u32[]{:S(2)}) collective-permute-start(bf16[80,1536]{1,0:T(8,128)(2,1)} %get-tuple-element.123), channel_id=1, source_target_pairs={{0,2},{1,3},{2,0},{3,1},{4,6},{5,7},{6,4},{7,5},{8,10},{9,11},{10,... | collective-permute-start | bytes 737288 | tf_op jit(solution)/shard_map/ppermute | solution.py:1029
  314.1 340.8 %collective-permute-start.13 = (bf16[80,1536]{1,0:T(8,128)(2,1)S(1)}, bf16[80,1536]{1,0:T(8,128)(2,1)S(1)}, u32[]{:S(2)}, u32[]{:S(2)}) collective-permute-start(bf16[80,1536]{1,0:T(8,128)(2,1)S(1)} %get-tuple-element.122), channel_id=1, source_target_pairs={{0,3},{1,0},{2,1},{3,2},{4,7},{5,4},{6,5},{7,6},{8,11},{9,8},{10,9... | collective-permute-start | bytes 737288 | tf_op jit(solution)/shard_map/ppermute | solution.py:1029
  (14 other events, 17.3 us)
Sparse Core Ops, SparseCore 0:
  239.2 67.8 all-reduce.7
  310.0 254.3 all-reduce.5
  568.0 117.5 all-reduce.9

commit v2 on v1

--- a/solution.py
+++ b/solution.py
@@ -19,7 +19,7 @@
 F32 = jnp.float32
 BF16 = jnp.bfloat16
 ONE = pl.Buffered(1)
-EARLY = 40
+EARLY = 36
 
 
 def nn(a, b):
@@ -56,11 +56,9 @@
     return jnp.concatenate(parts, 1) if len(parts) > 1 else parts[0]
 
 
-def head_sums(values, low):
-    shape = (values.shape[1], LANES)
-    picks = jnp.where(iota(shape, 1) == (iota(shape, 0) + low) // WIDTH, 1.0, 0.0).astype(BF16)
+def head_sums(values, sums):
     high, rest = halves(values)
-    return nn(high, picks) + nn(rest, picks)
+    return nn(high, sums) + nn(rest, sums)
 
 
 def groups(inner):
@@ -117,8 +115,8 @@
 
 
 def prepare_kernel(
-    ws_ref, cs_ref, csb_ref, cv_ref, cvb_ref, decay_ref, bias_ref, skip_ref, norm_ref, gain_ref,
-    packed_ref, taps_ref, heads_ref, norm_out_ref, gain_out_ref,
+    ws_ref, cs_ref, csb_ref, cv_ref, cvb_ref, decay_ref, bias_ref, skip_ref, norm_ref, gain_ref, wstep_ref,
+    packed_ref, taps_ref, heads_ref, norm_out_ref, gain_out_ref, wstep_out_ref, picks_ref, sums_ref,
 ):
     width = ws_ref.shape[1]
     packed_ref[:, :width] = ws_ref[...]
@@ -128,6 +126,7 @@
         high = taps.astype(BF16)
         packed_ref[:, width + LANES * k : width + LANES * (k + 1)] = high
         taps = taps - high.astype(F32)
+    packed_ref[:, width + 3 * LANES :] = jnp.zeros((taps.shape[0], LANES), BF16)
     inner = cv_ref.shape[1]
     taps_ref[...] = jnp.concatenate([cv_ref[...], cvb_ref[...][None], jnp.zeros((3, inner), F32)], 0)
     rows = [-jnp.exp(decay_ref[...])[None], bias_ref[...][None], skip_ref[...][None]]
@@ -137,51 +136,31 @@
     )
     norm_out_ref[...] = norm_ref[...][None]
     gain_out_ref[...] = gain_ref[...][None]
-
-
-def prepare(w_state_t, conv_state, conv_state_bias, conv_value, conv_value_bias, decay, bias, skip, norm, gain):
+    wstep_out_ref[...] = jnp.concatenate([wstep_ref[...].astype(F32), jnp.zeros((16 - count, width), F32)], 0).astype(BF16)
+    shape = picks_ref.shape
+    picks_ref[...] = jnp.where(iota(shape, 0) % LANES == iota(shape, 1) // WIDTH, 1.0, 0.0).astype(BF16)
+    shape = sums_ref.shape
+    sums_ref[...] = jnp.where(iota(shape, 0) // WIDTH == iota(shape, 1), 1.0, 0.0).astype(BF16)
+
+
+def prepare(w_state_t, conv_state, conv_state_bias, conv_value, conv_value_bias, decay, bias, skip, norm, gain, w_step_t
+):
     state_local, width = w_state_t.shape
     inner = conv_value.shape[1]
     return pl.pallas_call(
         prepare_kernel,
         out_shape=[
-            jax.ShapeDtypeStruct((state_local, width + 3 * LANES), BF16),
+            jax.ShapeDtypeStruct((state_local, width + 4 * LANES), BF16),
             jax.ShapeDtypeStruct((8, inner), F32),
             jax.ShapeDtypeStruct((8, LANES), F32),
             jax.ShapeDtypeStruct((1, width), F32),
             jax.ShapeDtypeStruct((1, inner), F32),
+            jax.ShapeDtypeStruct((16, width), BF16),
+            jax.ShapeDtypeStruct((2 * LANES, inner), BF16),
+            jax.ShapeDtypeStruct((inner, LANES), BF16),
         ],
         name="prepare",
-    )(w_state_t, conv_state, conv_state_bias, conv_value, conv_value_bias, decay, bias, skip, norm, gain)
-
-
-def assemble_kernel(count, taps_value_ref, *refs):
-    parts, (weights_ref, taps_ref, columns) = refs[:count], refs[count:]
-    rows, width = parts[0].shape[0], weights_ref.shape[1]
-    inner = taps_value_ref.shape[1]
-    place = lax.axis_index("head")
-    for steps, part in enumerate(parts):
-        at = pl.multiple_of(lax.rem(place - steps + count, count) * rows, rows)
-        weights_ref[pl.ds(at, rows), :] = part[:, :width]
-        columns[pl.ds(at, rows), :] = sum(
-            part[:, width + LANES * k : width + LANES * (k + 1)].astype(F32) for k in range(3)
-        )
-    taps_ref[:, :inner] = taps_value_ref[...]
-    taps_ref[:, inner:] = jnp.transpose(columns[...])[:8]
-
-
-def assemble(taps_value, parts):
-    rows, width = parts[0].shape[0], parts[0].shape[1] - 3 * LANES
-    inner, total = taps_value.shape[1], rows * len(parts)
-    return pl.pallas_call(
-        partial(assemble_kernel, len(parts)),
-        out_shape=[
-            jax.ShapeDtypeStruct((total, width), BF16),
-            jax.ShapeDtypeStruct((8, inner + total), F32),
-        ],
-        scratch_shapes=[pltpu.VMEM((total, LANES), F32)],
-        name="assemble",
-    )(taps_value, *parts)
+    )(w_state_t, conv_state, conv_state_bias, conv_value, conv_value_bias, decay, bias, skip, norm, gain, w_step_t)
 
 
 def project_kernel(x_ref, gain_ref, wg_ref, wv_ref, ws_ref, normed_ref, gate_ref, conv_ref, step_ref):
@@ -189,7 +168,7 @@
     inverse = lax.rsqrt(jnp.mean(x * x, -1, keepdims=True) + EPSILON)
     normed = (x * inverse * gain_ref[...]).astype(BF16)
     normed_ref[...] = normed
-    gate_ref[...] = nn(normed, wg_ref[...])
+    gate_ref[...] = nn(normed, wg_ref[...]).astype(BF16)
     conv_ref[...] = nn(normed, wv_ref[...]).astype(BF16)
     step = nt(normed, ws_ref[...])
     step_ref[...] = jnp.concatenate([step, jnp.zeros((CHUNK, LANES - step.shape[1]), F32)], 1)
@@ -207,7 +186,7 @@
         out_specs=[rows(width), rows(inner), rows(inner), rows(LANES)],
         out_shape=[
             jax.ShapeDtypeStruct((tokens, width), BF16),
-            jax.ShapeDtypeStruct((tokens, inner), F32),
+            jax.ShapeDtypeStruct((tokens, inner), BF16),
             jax.ShapeDtypeStruct((tokens, inner), BF16),
             jax.ShapeDtypeStruct((tokens, LANES), F32),
         ],
@@ -221,29 +200,40 @@
 
 
 def scan_kernel(
-    cv_ref, cs_ref, halo_ref, step_ref, ids_ref, before_ref, heads_ref, taps_ref,
-    y_ref, bc_ref, cum_ref, reach_ref, enter_ref, end_ref, kept_ref, tok_ref, seg_ref,
-    carry, state, offset, reached,
+    cv_ref, normed_ref, halo_ref, step_ref, ids_ref, heads_ref, taps_value_ref, gathered_ref, picks_ref,
+    y_ref, bc_ref, cum_ref, reach_ref, enter_ref, end_ref, kept_ref, tok_ref, seg_ref, cs_ref, taps_ref, rim_ref,
+    carry, state, offset, reached, before,
 ):
     at = pl.program_id(0)
-    inner = cv_ref.shape[1]
+    inner, width = cv_ref.shape[1], normed_ref.shape[1]
     count = SPAN
 
     @pl.when(at == 0)
     def _():
-        carry[...] = halo_ref[...].astype(F32)
+        columns = sum(gathered_ref[:, width + LANES * k : width + LANES * (k + 1)].astype(F32) for k in range(3))
+        taps_ref[:, :inner] = taps_value_ref[...]
+        taps_ref[:, inner:] = jnp.transpose(columns)[:8]
+        halo = halo_ref[...].astype(F32)
+        rim_rows = halo[:, inner + LANES :].astype(BF16)
+        rim_state = nt(jnp.concatenate([rim_rows, rim_rows], 0), gathered_ref[:, :width])[:8].astype(BF16)
+        rim = jnp.concatenate([halo[:, :inner], rim_state.astype(F32)], 1)
+        carry[...] = rim
+        rim_ref[...] = rim
+        turned = jnp.concatenate([halo[:, inner : inner + LANES], jnp.zeros((LANES - 8, LANES), F32)], 0)
+        turned = pltpu.roll(jnp.transpose(turned)[:8], LANES - 8, 1)
+        before[...] = jnp.where(lax.axis_index("seq") == 0, -1.0, turned)
         state[...] = jnp.zeros_like(state)
         offset[...] = jnp.zeros_like(offset)
         reached[...] = jnp.ones_like(reached)
 
     blocks = ids_ref.shape[0]
-    own_row = lambda index: ids_ref[pl.ds(index, 1), :]
-    previous = jnp.where(lax.axis_index("seq") == 0, -1, before_ref[blocks - 1 : blocks])
+    own_row = lambda index: ids_ref[pl.ds(index, 1), :].astype(F32)
+    previous = before[0:1]
     here = own_row(at)
     earlier = jnp.where(at == 0, previous, own_row(jnp.maximum(at - 1, 0)))
-    later = jnp.where(at == blocks - 1, -2, own_row(jnp.minimum(at + 1, blocks - 1)))
+    later = jnp.where(at == blocks - 1, -2.0, own_row(jnp.minimum(at + 1, blocks - 1)))
     lane = iota((1, LANES), 1)
-    seg = here.astype(F32)
+    seg = here
     flags = [here == here]
     for steps in range(1, 4):
         moved = jnp.where(lane < steps, pltpu.roll(earlier, steps, 1), pltpu.roll(here, steps, 1))
@@ -278,14 +268,16 @@
     cum_t = jnp.transpose(cum)
     visible = [column(tokens, 1 + k, 2 * LANES) for k in range(3)]
 
-    def conv(ref, low, at_column, width):
-        rows = ref[:, low : low + width].astype(F32)
+    def conv(rows, at_column):
+        width = rows.shape[1]
         wide = slice(at_column, at_column + width)
         pre, _ = conv_taps(taps_ref[:, wide], rows, carry[:, wide], [v[:, :width] for v in visible])
         carry[:, wide] = rows[count - 8 :]
         return pre * sigmoid(pre)
 
-    both = conv(cs_ref, 0, inner, 2 * STATE).astype(BF16)
+    cs = nt(normed_ref[...], gathered_ref[:, :width]).astype(BF16)
+    cs_ref[...] = cs
+    both = conv(cs.astype(F32), inner).astype(BF16)
     bc_ref[...] = both
     b_low, c_low = both[:, :LANES], both[:, LANES:]
     scores = nt(c_low, b_low)
@@ -293,13 +285,15 @@
     enter_ref[0] = state[...]
     left = iota((count, LANES), 1) < WIDTH
     b_t = jnp.transpose(b_low.astype(F32)).astype(BF16)
+    factors = jnp.concatenate(halves(jnp.concatenate([step, start, end], 0)), 1)
 
     for low, width in groups(inner):
         wide = slice(low, low + width)
-        values = conv(cv_ref, low, low, width)
-        scaled = values * spread(step, low, width)
+        values = conv(cv_ref[:, wide].astype(F32), low)
+        steps_wide, starts, ends = jnp.split(nn(factors, picks_ref[:, wide]), 3)
+        scaled = values * steps_wide
         entering = state[:, wide]
-        y = spread(start, low, width) * nn(c_low, entering.astype(BF16))
+        y = starts * nn(c_low, entering.astype(BF16))
         y = y + spread(heads[2:3], low, width) * values
         inside = []
         for part in range(0, width, LANES):
@@ -311,33 +305,35 @@
                 mine.append(jnp.where(here, scaled[:, part : part + LANES], 0.0).astype(BF16))
                 weights.append((decay * scores).astype(BF16))
             inside.append(nn(jnp.concatenate(weights, 1), jnp.concatenate(mine, 0)))
-        y_ref[:, wide] = y + jnp.concatenate(inside, 1)
+        y_ref[:, wide] = (y + jnp.concatenate(inside, 1)).astype(BF16)
         state[:, wide] = spread(through, low, width) * entering + nn(
-            b_t, (scaled * spread(end, low, width)).astype(BF16)
+            b_t, (scaled * ends).astype(BF16)
         )
     end_ref[...] = state[...]
 
 
-def scan(cv, cs, halo, step_raw, ids, ids_before, heads, taps):
+def scan(cv, normed, halo, step_raw, ids, heads, taps_value, gathered, picks):
     tokens, inner = cv.shape
-    blocks = tokens // SPAN
+    blocks, total = tokens // SPAN, inner + 2 * STATE
+    fixed = lambda n: pl.BlockSpec((8, n), lambda i: (0, 0))
     rows = lambda n: pl.BlockSpec((SPAN, n), lambda i: (i, 0))
     whole = lambda a: pl.BlockSpec(a.shape, lambda i: (0, 0), pipeline_mode=ONE)
     return pl.pallas_call(
         scan_kernel,
         grid=(blocks,),
         in_specs=[
-            rows(inner), rows(2 * STATE), whole(halo), rows(LANES), whole(ids), whole(ids_before), whole(heads),
-            whole(taps),
+            rows(inner), rows(normed.shape[1]), whole(halo), rows(LANES), whole(ids), whole(heads), whole(taps_value),
+            whole(gathered), whole(picks),
         ],
         out_specs=[
             rows(inner), rows(2 * STATE), rows(LANES), rows(LANES),
             pl.BlockSpec((1, STATE, inner), lambda i: (i, 0, 0)),
             pl.BlockSpec((STATE, inner), lambda i: (0, 0)),
             pl.BlockSpec((1, 8, LANES), lambda i: (i, 0, 0)), rows(LANES), pl.BlockSpec((1, 8, SPAN), lambda i: (i, 0, 0)),
+            rows(2 * STATE), fixed(total), fixed(total),
         ],
         out_shape=[
-            jax.ShapeDtypeStruct((tokens, inner), F32),
+            jax.ShapeDtypeStruct((tokens, inner), BF16),
             jax.ShapeDtypeStruct((tokens, 2 * STATE), BF16),
             jax.ShapeDtypeStruct((tokens, LANES), F32),
             jax.ShapeDtypeStruct((tokens, LANES), F32),
@@ -346,10 +342,14 @@
             jax.ShapeDtypeStruct((blocks, 8, LANES), F32),
             jax.ShapeDtypeStruct((tokens, LANES), F32),
             jax.ShapeDtypeStruct((blocks, 8, SPAN), F32),
+            jax.ShapeDtypeStruct((tokens, 2 * STATE), BF16),
+            jax.ShapeDtypeStruct((8, total), F32),
+            jax.ShapeDtypeStruct((8, total), F32),
         ],
         scratch_shapes=[
             pltpu.VMEM((8, inner + 2 * STATE), F32),
             pltpu.VMEM((STATE, inner), F32),
+            pltpu.VMEM((8, LANES), F32),
             pltpu.VMEM((8, LANES), F32),
             pltpu.VMEM((8, LANES), F32),
         ],
@@ -359,19 +359,22 @@
             transcendentals=tokens * inner * 4,
         ),
         name="scan",
-    )(cv, cs, halo, step_raw, ids, ids_before, heads, taps)
-
-
-def gate_kernel(y_ref, reach_ref, bc_ref, state_ref, gate_ref, gg_ref, gain_ref, low_ref, sums_ref):
+    )(cv, normed, halo, step_raw, ids, heads, taps_value, gathered, picks)
+
+
+def gate_kernel(
+    y_ref, reach_ref, bc_ref, state_ref, gate_ref, gg_ref, gain_ref, picks_ref, low_ref, sums_ref
+):
     inner = y_ref.shape[1]
     c_low = bc_ref[:, LANES:]
-    reach = reach_ref[...]
+    reach = jnp.concatenate(halves(reach_ref[...]), 1)
     squares = jnp.zeros((CHUNK, LANES), F32)
     dots = jnp.zeros((CHUNK, LANES), F32)
     for pair in range(inner // LANES):
         wide = slice(pair * LANES, (pair + 1) * LANES)
-        ssm = y_ref[:, wide] + pair_of(reach, pair) * nn(c_low, state_ref[:, wide].astype(BF16))
-        gate = gate_ref[:, wide]
+        reach_pair = nn(reach, picks_ref[:, wide])
+        ssm = y_ref[:, wide].astype(F32) + reach_pair * nn(c_low, state_ref[:, wide].astype(BF16))
+        gate = gate_ref[:, wide].astype(F32)
         gated = ssm * gate * sigmoid(gate)
         weighted = gated * gain_ref[:, wide]
         low_ref[:, wide] = weighted.astype(BF16)
@@ -382,7 +385,7 @@
     sums_ref[...] = jnp.transpose(jnp.where(iota((CHUNK, LANES), 1) == 0, square, dot))[:8]
 
 
-def gate_sums(y, reach, bc, state_in, gate_raw, gg, gain):
+def gate_sums(y, reach, bc, state_in, gate_raw, gg, gain, picks):
     tokens, inner = y.shape
     rows = lambda n: pl.BlockSpec((CHUNK, n), lambda i: (i, 0))
     whole = lambda a: pl.BlockSpec(a.shape, lambda i: (0, 0), pipeline_mode=ONE)
@@ -391,6 +394,7 @@
         grid=(tokens // CHUNK,),
         in_specs=[
             rows(inner), rows(LANES), rows(2 * STATE), whole(state_in), rows(inner), rows(inner), whole(gain),
+            whole(picks),
         ],
         out_specs=[rows(inner), pl.BlockSpec((8, CHUNK), lambda i: (0, i))],
         out_shape=[
@@ -401,10 +405,10 @@
             flops=2 * tokens * inner * STATE, bytes_accessed=tokens * inner * 12, transcendentals=tokens * inner
         ),
         name="gate",
-    )(y, reach, bc, state_in, gate_raw, gg, gain)
-
-
-def ungate_kernel(count, y_ref, gate_ref, gg_ref, gain_ref, reach_ref, bc_ref, in_ref, *refs):
+    )(y, reach, bc, state_in, gate_raw, gg, gain, picks)
+
+
+def ungate_kernel(count, y_ref, gate_ref, gg_ref, gain_ref, reach_ref, bc_ref, in_ref, picks_ref, *refs):
     sums_refs, (gs_ref, ggr_ref, low_ref, scale_ref, gain_sum_ref, state_ref, gain_acc, state_acc) = (
         refs[:count], refs[count:]
     )
@@ -422,14 +426,14 @@
     scale = lax.rsqrt(column(sums, 0) / all_inner + EPSILON)
     shift = scale * scale * scale * column(sums, 1) / all_inner
     scale_ref[...] = scale
-    reach = reach_ref[...]
+    reach = jnp.concatenate(halves(reach_ref[...]), 1)
     c_low = bc_ref[:, LANES:]
     c_t = jnp.transpose(c_low.astype(F32)).astype(BF16)
     for pair in range(inner // LANES):
         wide = slice(pair * LANES, (pair + 1) * LANES)
-        reach_pair = pair_of(reach, pair)
-        ssm = y_ref[:, wide] + reach_pair * nn(c_low, in_ref[:, wide].astype(BF16))
-        gate, gg = gate_ref[:, wide], gg_ref[:, wide].astype(F32)
+        reach_pair = nn(reach, picks_ref[:, wide])
+        ssm = y_ref[:, wide].astype(F32) + reach_pair * nn(c_low, in_ref[:, wide].astype(BF16))
+        gate, gg = gate_ref[:, wide].astype(F32), gg_ref[:, wide].astype(F32)
         sg = sigmoid(gate)
         act = gate * sg
         gated = ssm * act
@@ -445,7 +449,7 @@
     state_ref[...] = state_acc[...]
 
 
-def ungate(y, gate_raw, gg, gain, reach, bc, state_in, sums):
+def ungate(y, gate_raw, gg, gain, reach, bc, state_in, picks, sums):
     tokens, inner = y.shape
     rows = lambda n: pl.BlockSpec((CHUNK, n), lambda i: (i, 0))
     whole = lambda a: pl.BlockSpec(a.shape, lambda i: (0, 0), pipeline_mode=ONE)
@@ -455,6 +459,7 @@
         grid=(tokens // CHUNK,),
         in_specs=[
             rows(inner), rows(inner), rows(inner), whole(gain), rows(LANES), rows(2 * STATE), whole(state_in),
+            whole(picks),
         ] + [pl.BlockSpec((8, CHUNK), lambda i: (0, i))] * len(sums),
         out_specs=[rows(inner), rows(inner), rows(inner), rows(LANES), fixed(8, inner), fixed(STATE, inner)],
         out_shape=[
@@ -470,12 +475,12 @@
             flops=2 * tokens * inner * STATE, bytes_accessed=tokens * inner * 16, transcendentals=tokens * inner
         ),
         name="ungate",
-    )(y, gate_raw, gg, gain, reach, bc, state_in, *sums)
+    )(y, gate_raw, gg, gain, reach, bc, state_in, picks, *sums)
 
 
 def unscan_kernel(
     gs_ref, cv_ref, cv_before_ref, cs_ref, cs_before_ref, halo_ref, bc_ref, step_ref, cum_ref, tok_ref, seg_ref,
-    heads_ref, taps_ref, enter_ref, kept_ref, state_in_ref, grad_end_ref, gain_sum_ref,
+    heads_ref, taps_ref, enter_ref, kept_ref, state_in_ref, grad_end_ref, gain_sum_ref, picks_ref, sums_ref,
     value_ref, rest_ref, small_ref, head_rows_ref,
     carry, grad, taps_acc, heads_acc, skip_acc,
 ):
@@ -555,15 +560,15 @@
     grad_step = jnp.zeros((count, LANES), F32)
     at_end = jnp.zeros((8, LANES), F32)
     down = []
+    factors = jnp.concatenate(halves(jnp.concatenate([step, start, end], 0)), 1)
     for low, width in groups(inner):
         wide = slice(low, low + width)
         pre, shifted, sg = conv(cv_ref, cv_before_ref, low, low, width)
         values = pre * sg
-        step_wide = spread(step, low, width)
+        step_wide, starts, ends = jnp.split(nn(factors, picks_ref[:, wide]), 3)
         scaled = values * step_wide
         scaled_low = scaled.astype(BF16)
         grad_y = gs_ref[:, wide]
-        starts, ends = spread(start, low, width), spread(end, low, width)
         entering = enter_ref[0, :, wide] + spread(kept[0:1], low, width) * state_in_ref[:, wide]
         grad_state = grad[:, wide]
         grad_low = grad_state.astype(BF16)
@@ -571,10 +576,10 @@
         to_end = ends * nn(b_low, grad_low)
         grad_y_in = grad_y * starts
         moved = scaled * to_end
-        grad_cum = grad_cum + head_sums(grad_y_in * nn(c_low, state_low) - moved, low)
+        grad_cum = grad_cum + head_sums(grad_y_in * nn(c_low, state_low) - moved, sums_ref[wide])
         through_wide = spread(through, low, width)
         ending = jnp.sum(moved, 0, keepdims=True) + through_wide * jnp.sum(grad_state * entering, 0, keepdims=True)
-        at_end = at_end + head_sums(jnp.broadcast_to(ending, (8, width)), low)
+        at_end = at_end + head_sums(jnp.broadcast_to(ending, (8, width)), sums_ref[wide])
         y_rest = grad_y - grad_y.astype(BF16).astype(F32)
         scaled_rest = (scaled - scaled_low.astype(F32)).astype(BF16)
         inside = []
@@ -606,7 +611,7 @@
         grad_c = grad_c + nt(grad_low_in, state_low) + nt(grad_rest_in, state_low) + nt(grad_low_in, state_rest)
         grad_b = grad_b + nt((scaled * ends).astype(BF16), grad_low)
         grad[:, wide] = through_wide * grad_state + nn(c_t, grad_low_in)
-        grad_step = grad_step + head_sums(grad_scaled * values, low)
+        grad_step = grad_step + head_sums(grad_scaled * values, sums_ref[wide])
         skip_acc[:, wide] += jnp.sum((grad_y * values).reshape(count // 8, 8, width), 0)
         grad_values = grad_scaled * step_wide + spread(heads[2:3], low, width) * grad_y
         unconv(grad_values, pre, sg, shifted, low, width)
@@ -634,7 +639,7 @@
     @pl.when(first)
     def _():
         down_rows = lambda v: jnp.sum(v, 0, keepdims=True)
-        skip = sum(head_sums(skip_acc[:, low : low + width], low) for low, width in groups(inner))
+        skip = sum(head_sums(skip_acc[:, low : low + width], sums_ref[low : low + width]) for low, width in groups(inner))
         wide = [down_rows(taps_acc[8 * k : 8 * k + 8]) for k in range(5)]
         wide += [heads_acc[0:1], heads_acc[1:2], down_rows(skip), down_rows(gain_sum_ref[...])]
         full = small_ref.shape[1]
@@ -644,7 +649,7 @@
 
 def unscan(
     gs, cv, cs, halo, bc, step_raw, cum, tokens_info, seg_rows, heads, taps, enter, kept, state_in, grad_end, gain_sum,
-    full,
+    picks, sums, full,
 ):
     tokens, inner = gs.shape
     blocks = tokens // SPAN
@@ -662,6 +667,7 @@
             rows(LANES), rows(LANES), rows(LANES), pl.BlockSpec((1, 8, SPAN), lambda i: (back(i), 0, 0)),
             whole(heads), whole(taps), pl.BlockSpec((1, STATE, inner), lambda i: (back(i), 0, 0)),
             pl.BlockSpec((1, 8, LANES), lambda i: (back(i), 0, 0)), whole(state_in), whole(grad_end), whole(gain_sum),
+            whole(picks), whole(sums),
         ],
         out_specs=[rows(inner), rows(4 * STATE + LANES), fixed(16, full), fixed(8, total)],
         out_shape=[
@@ -683,7 +689,7 @@
             transcendentals=tokens * inner * 6,
         ),
         name="unscan",
-    )(gs, cv, cv, cs, cs, halo, bc, step_raw, cum, tokens_info, seg_rows, heads, taps, enter, kept, state_in, grad_end, gain_sum)
+    )(gs, cv, cv, cs, cs, halo, bc, step_raw, cum, tokens_info, seg_rows, heads, taps, enter, kept, state_in, grad_end, gain_sum, picks, sums)
 
 
 def chain_kernel(
@@ -820,7 +826,7 @@
         grid=(items + behind(size),),
         in_specs=[
             rows(width, lambda i: jnp.minimum(i, first - 1)), own(inner), own(inner), own(columns), whole(w_gate),
-            whole(w_value), whole(w_both_t), whole(w_step_t),
+            whole(w_value), pl.BlockSpec((2 * STATE, width), lambda i: (0, 0), pipeline_mode=ONE), whole(w_step_t),
         ],
         out_specs=rows(width, lambda i: jnp.maximum(i - behind(size), 0)),
         out_shape=jax.ShapeDtypeStruct((items * ITEM, width), BF16),
@@ -838,33 +844,33 @@
     mixed_ref, grad_out_ref, a_out_ref, b_out_ref, c_out_ref,
 ):
     at = pl.program_id(0)
-    x = x_ref[...].astype(F32)
-    scale = scale_ref[:, 0:1]
-
-    @pl.when(at < early)
-    def _():
-        mixed_ref[...] = (x + scale * out_a_ref[...].astype(F32)).astype(BF16)
-
-    @pl.when(at >= early)
-    def _():
-        mixed_ref[...] = (x + scale * out_b_ref[...].astype(F32)).astype(BF16)
-
-    width = x.shape[1]
-    inverse = lax.rsqrt(jnp.mean(x * x, -1, keepdims=True) + EPSILON)
-    weighted = grad_ref[...].astype(F32) * gain_ref[...]
-    dot = jnp.sum(weighted * x, -1, keepdims=True)
-    grad_out_ref[...] = cot_ref[...].astype(F32) + inverse * weighted - x * (inverse**3 * dot / width)
-    a_out_ref[...] = a_ref[...].astype(F32)
-    b_out_ref[...] = b_ref[...].astype(F32)
-    c_out_ref[...] = c_ref[...].astype(F32)
+    width = x_ref.shape[1]
+    count = x_ref.shape[0] // 64
+
+    def part(k, none):
+        rows = pl.ds(pl.multiple_of(k * 64, 64), 64)
+        x = x_ref[rows, :].astype(F32)
+        scale = scale_ref[rows, 0:1]
+        total = jnp.where(at < early, out_a_ref[rows, :].astype(F32), out_b_ref[rows, :].astype(F32))
+        mixed_ref[rows, :] = (x + scale * total).astype(BF16)
+        inverse = lax.rsqrt(jnp.mean(x * x, -1, keepdims=True) + EPSILON)
+        weighted = grad_ref[rows, :].astype(F32) * gain_ref[...]
+        dot = jnp.sum(weighted * x, -1, keepdims=True)
+        grad_out_ref[rows, :] = cot_ref[rows, :].astype(F32) + inverse * weighted - x * (inverse**3 * dot / width)
+        return none
+
+    lax.fori_loop(0, count, part, 0)
+    for source, target in ((a_ref, a_out_ref), (b_ref, b_out_ref), (c_ref, c_out_ref)):
+        target[...] = source[...].astype(F32)
 
 
 def finish(scale, out_early, chained, hidden, cotangent, gain, sums):
     tokens, width = hidden.shape
-    steps = tokens // SPAN
-    early = out_early.shape[0] // SPAN
+    per_step = 128
+    steps = tokens // per_step
+    early = out_early.shape[0] // per_step
     late = steps - early
-    rows = lambda n, at=lambda i: i: pl.BlockSpec((SPAN, n), lambda i: (at(i), 0))
+    rows = lambda n, at=lambda i: i: pl.BlockSpec((per_step, n), lambda i: (at(i), 0))
     parts = [pl.BlockSpec((a.shape[0] // steps, a.shape[1]), lambda i: (i, 0)) for a in sums]
     return pl.pallas_call(
         partial(finish_kernel, early),
@@ -882,10 +888,10 @@
 
 
 def pack_kernel(rest_ref, wb_ref, ws_ref, pg_ref, pv_ref, norm_ref, small_ref, packed_ref):
-    both, steps = wb_ref.shape[0], ws_ref.shape[0]
+    both, steps, width = wb_ref.shape[0], ws_ref.shape[0], ws_ref.shape[1]
     state = rest_ref[:both] + rest_ref[both : 2 * both]
     step = rest_ref[2 * both : 2 * both + steps]
-    products = jnp.sum(state * wb_ref[...].astype(F32), 0, keepdims=True) + pg_ref[...][None] + pv_ref[...][None]
+    products = jnp.sum(state * wb_ref[:, :width].astype(F32), 0, keepdims=True) + pg_ref[...][None] + pv_ref[...][None]
     products = products + jnp.sum(step * ws_ref[...].astype(F32), 0, keepdims=True)
     packed_ref[:both] = state
     packed_ref[both : both + 16] = rest_ref[2 * both : 2 * both + 16]
@@ -894,7 +900,7 @@
 
 
 def pack(grad_rest_t, w_both_t, w_step_t, products_gate, products_value, norm, small):
-    both, width = w_both_t.shape
+    both, width = w_both_t.shape[0], w_step_t.shape[1]
     return pl.pallas_call(
         pack_kernel,
         out_shape=jax.ShapeDtypeStruct((both + 32, width), F32),
@@ -902,9 +908,22 @@
     )(grad_rest_t, w_both_t, w_step_t, products_gate, products_value, norm, small)
 
 
-def unpack_kernel(
-    count, packed_ref, *refs
-):
+def late_kernel(packed_ref, *parts):
+    state_local, count = parts[0].shape[0] - 16, len(parts) + 1
+    place = lax.axis_index("head")
+    small = packed_ref[count * state_local + 16 :].astype(BF16)
+    for steps, part in enumerate(parts, 1):
+        at = pl.multiple_of(lax.rem(place + steps, count) * state_local, state_local)
+        part[:state_local] = packed_ref[pl.ds(at, state_local), :].astype(BF16)
+        part[state_local:] = small
+
+
+def late_parts(packed, state_local, count):
+    shape = jax.ShapeDtypeStruct((state_local + 16, packed.shape[1]), BF16)
+    return pl.pallas_call(late_kernel, out_shape=[shape] * (count - 1), name="late")(packed)
+
+
+def unpack_kernel(count, packed_ref, *refs):
     others, refs = refs[: count - 1], refs[count - 1 :]
     state_ref, step_ref, norm_ref, cv_ref, cvb_ref, cs_ref, csb_ref, decay_ref, bias_ref, skip_ref, gain_ref = refs
     state_local, heads, inner = state_ref.shape[0], step_ref.shape[0], cv_ref.shape[1]
@@ -965,41 +984,38 @@
 ):
     tokens, width = hidden.shape
     inner, heads_local, state_local = w_value.shape[1], w_step.shape[1], w_state.shape[1]
-    count, place = lax.axis_size("head"), lax.axis_index("head")
+    count = lax.axis_size("head")
 
     ids = segment_ids.reshape(tokens // SPAN, SPAN)
-    packed, taps_value, heads, norm, gain = prepare(
+    packed, taps_value, heads, norm, gain, w_step_t, picks, sums_of = prepare(
         w_state.T, conv_state, conv_state_bias, conv_value, conv_value_bias, decay_log, step_bias, skip_gain,
-        norm_gain, gate_gain,
+        norm_gain, gate_gain, w_step.T,
     )
-    parts = from_all(packed, "head")
-    ids_before = passed_along(ids, "seq", 1)
-    w_step_t = jnp.pad(w_step.T, ((0, 16 - heads_local), (0, 0)))
+    gathered = lax.all_gather(packed, "head", axis=0, tiled=True)
 
     normed, gate_raw, cv, step_raw = project(hidden, norm, w_gate, w_value, w_step_t)
-    w_both_t, taps = assemble(taps_value, parts)
-    cs = nt(normed, w_both_t).astype(BF16)
-    tail = jnp.concatenate([cv[tokens - 8 :], cs[tokens - 8 :]], 1)
+    last_ids = jnp.pad(segment_ids[tokens - 8 :].astype(F32).astype(BF16)[:, None], ((0, 0), (0, LANES - 1)))
+    tail = jnp.concatenate([cv[tokens - 8 :], last_ids, normed[tokens - 8 :]], 1)
     halo = passed_along(tail, "seq", 1)
     gg = nt(cotangent, w_out).astype(BF16)
-    y, bc, cum, reach, enter, local_end, kept, tokens_info, seg_rows = scan(
-        cv, cs, halo, step_raw, ids, ids_before, heads, taps
+    y, bc, cum, reach, enter, local_end, kept, tokens_info, seg_rows, cs, taps, rim = scan(
+        cv, normed, halo, step_raw, ids, heads, taps_value, gathered, picks
     )
     state_in = passed_along(local_end, "seq", 1)
-    low, sums = gate_sums(y, reach, bc, state_in, gate_raw, gg, gain)
+    low, sums = gate_sums(y, reach, bc, state_in, gate_raw, gg, gain, picks)
     sums = from_all(sums, "head")
     early = EARLY * ITEM
     out_early = lax.psum(nn(low[:early], w_out).astype(BF16), "head")
     out_late = nn(low[early:], w_out).astype(BF16)
 
     gs, grad_gate_raw, gate_low, scale, gain_sum, grad_state_in = ungate(
-        y, gate_raw, gg, gain, reach, bc, state_in, sums
+        y, gate_raw, gg, gain, reach, bc, state_in, picks, sums
     )
     grad_end = passed_along(grad_state_in, "seq", -1)
     grad_w_out = row_major(tn(gate_low, cotangent))
     grad_value, grad_rest, small, head_rows = unscan(
-        gs, cv, cs, halo, bc, step_raw, cum, tokens_info, seg_rows, heads, taps, enter, kept, state_in, grad_end,
-        gain_sum, width,
+        gs, cv, cs, rim, bc, step_raw, cum, tokens_info, seg_rows, heads, taps, enter, kept, state_in, grad_end,
+        gain_sum, picks, sums_of, width,
     )
     from_next = passed_along(head_rows, "seq", -1)
     grad_w_gate = row_major(tn(normed, grad_gate_raw))
@@ -1012,22 +1028,18 @@
     grad_rest = with_next(grad_rest, inner, inner + 2 * STATE)
     grad_w_value = row_major(tn(normed, grad_value))
     grad_rest_t = row_major(tn(grad_rest, normed))
-    chained = chain_sums(out_late, grad_gate_raw, grad_value, grad_rest, w_gate, w_value, w_both_t, w_step_t)
+    chained = chain_sums(out_late, grad_gate_raw, grad_value, grad_rest, w_gate, w_value, gathered, w_step_t)
 
     packed = pack(
-        grad_rest_t, w_both_t, w_step_t, jnp.sum(w_gate.astype(F32) * grad_w_gate, 1),
+        grad_rest_t, gathered, w_step_t, jnp.sum(w_gate.astype(F32) * grad_w_gate, 1),
         jnp.sum(w_value.astype(F32) * grad_w_value, 1), norm, small,
     )
     weights = lax.psum(tuple(a.astype(BF16) for a in (grad_w_gate, grad_w_value, grad_w_out)), "seq")
     packed = lax.psum(packed, "seq")
 
-    def part(steps):
-        rows = lax.dynamic_slice_in_dim(packed, lax.rem(place + steps, count) * state_local, state_local, 0)
-        return jnp.concatenate([rows, packed[2 * STATE + 16 :]], 0).astype(BF16)
-
     others = [
-        lax.ppermute(part(steps), "head", [(s, (s + steps) % count) for s in range(count)])
-        for steps in range(1, count)
+        lax.ppermute(part, "head", [(s, (s + steps) % count) for s in range(count)])
+        for steps, part in enumerate(late_parts(packed, state_local, count), 1)
     ]
     mixed, grad_hidden, *weights = finish(scale, out_early, chained, hidden, cotangent, norm, weights)
     state_t, step_t, *rest = unpack(packed, others, inner, heads_local, state_local)

time: 722 us -> 686 us (0.950)
  starting transfers between devices: 27.1 us -> 17.5 us
  waiting for transfers between devices: 82.6 us -> 73.8 us
    psum x1, waiting for transfers between devices: 26.5 us -> 9.8 us  [on_device(): lax.psum(tuple((a.astype(BF16) for a in (grad_w_gate, grad_w_value, grad_...]
    all_gather x0 -> x1, waiting for transfers between devices: none -> 7.95 us  [on_device(): gathered = lax.all_gather(packed, 'head', axis=0, tiled=True)]
  transfers between devices with their start and end apart: 17 -> 14, of which waited for: 6 -> 8; matrix products, arithmetic and copies ran while one was open for 6% -> 6% of each run, Pallas kernels for 50% -> 52%
where the time goes in v2:
time: 686 us; the launch traced here: 684 us
  Pallas kernels  512 us (75%)
  waiting for transfers between devices  73.8 us (11%)
  matrix products  61.3 us (9%)
  starting transfers between devices  17.5 us (3%)
  between operations  14 us (2%)
    pallas_call x1, Pallas kernels, chain_sums(): pl.pallas_call(partial(chain_kernel, first, size), grid=(items + behind(s...  335 us
    pallas_call x1, Pallas kernels, unscan(): pl.pallas_call(unscan_kernel, grid=(blocks,), in_specs=[rows(inner), rows...  59.3 us
    psum x1, waiting for transfers between devices, on_device(): packed = lax.psum(packed, 'seq')  47.4 us
    dot_general x4, matrix products, tn(): lax.dot_general(a, b, (((0,), (0,)), ((), ())), preferred_element_type=F32)  41 us
    pallas_call x1, Pallas kernels, scan(): pl.pallas_call(scan_kernel, grid=(blocks,), in_specs=[rows(inner), rows(n...  30.9 us
    pallas_call x1, Pallas kernels, finish(): pl.pallas_call(partial(finish_kernel, early), grid=(steps,), in_specs=[ro...  29.5 us
    pallas_call x1, Pallas kernels, project(): pl.pallas_call(project_kernel, grid=(tokens // CHUNK,), in_specs=[rows(wi...  17.8 us
    pallas_call x1, Pallas kernels, ungate(): pl.pallas_call(partial(ungate_kernel, len(sums)), grid=(tokens // CHUNK,)...  17.5 us
  transfers between devices with their start and end apart: 14, of which 8 were waited for; matrix products, arithmetic and copies ran while one was open for 6% of the time, Pallas kernels for 52%

profile of v2, /device:TPU:0, one launch (start us, length us, event | category | flops | bytes accessed | tf_op | source)
XLA Modules:
  0.0 684.5 jit_solution(4715914057581997018)
XLA Ops:
  9.5 17.8 %project.1 = (bf16[2048,1536]{1,0:T(8,128)(2,1)}, bf16[2048,768]{1,0:T(8,128)(2,1)}, bf16[2048,768]{1,0:T(8,128)(2,1)}, f32[2048,128]{1,0:T(8,128)}) custom-call(bf16[2048,1536]{1,0:T(8,128)(2,1)} %x_ref.3, f32[1,1536]{1,0:T(1,128)} %get-tuple-element.71.gain_ref.norm_ref, bf16[1536,768]{1,0:T(8,128)(2,1)} %wg_ref.3, bf16[1536,768]{1,0:T(8,128)(2,1)} %wv_ref.3, ...), custom_call_target="tpu_custom_call" | custom-call | flops 10468982784 | bytes 26738688 | tf_op jit(solution)/shard_map/project/pallas_call | solution.py:182
  32.9 8.0 %all-gather.2.cloned.1.call-done.gathered_ref.wb_ref = bf16[256,2048]{1,0:T(8,128)(2,1)} async-done(((bf16[64,2048]{1,0:T(8,128)(2,1)}), bf16[256,2048]{1,0:T(8,128)(2,1)}) %all-gather.2.cloned.1.call-update) | async-done | bytes 1048592 | tf_op jit(solution)/shard_map/all_gather | solution.py:994
  40.8 30.9 %scan.1 = (bf16[2048,768]{1,0:T(8,128)(2,1)}, bf16[2048,256]{1,0:T(8,128)(2,1)}, f32[2048,128]{1,0:T(8,128)}, f32[2048,128]{1,0:T(8,128)}, f32[16,128,768]{2,1,0...) custom-call(bf16[2048,768]{1,0:T(8,128)(2,1)} %get-tuple-element.73., ...), custom_call_target="tpu_custom_call" | custom-call | flops 1610612736 | bytes 12582912 | tf_op jit(solution)/shard_map/scan/pallas_call | solution.py:321
  73.1 9.4 %convolution_convert_fusion.3.gg_ref = bf16[2048,768]{1,0:T(8,128)(2,1)} fusion(bf16[2048,1536]{1,0:T(8,128)(2,1)} %cot_ref.1, bf16[768,1536]{1,0:T(8,128)(2,1)S(1)} %copy-done), kind=kOutput, calls=%fused_computation.5 | convolution fusion | flops 4833411072 | bytes 11796480 | tf_op jit(solution)/shard_map/dot_general | solution.py:30
  83.3 10.5 %gate.1 = (bf16[2048,768]{1,0:T(8,128)(2,1)}, f32[8,2048]{1,0:T(8,128)}) custom-call(bf16[2048,768]{1,0:T(8,128)(2,1)} %get-tuple-element.80.y_ref, f32[2048,128]{1,0:T(8,128)} %get-tuple-element.83.reach_ref, bf16[2048,256]{1,0:T(8,128)(2,1)} %get-tuple-element.84.bc_ref, f32[128,768]{1,0:T(8,128)} %copy-done.1, ...), custom_call_target="tpu_custom_call" | custom-call | flops 402653184 | bytes 18874368 | tf_op jit(solution)/shard_map/gate/pallas_call | solution.py:392
  96.5 2.4 collective-permute-start.4
  100.1 2.4 collective-permute-done.3.refs_2_
  103.7 17.5 %ungate.1 = (f32[2048,768]{1,0:T(8,128)}, bf16[2048,768]{1,0:T(8,128)(2,1)}, bf16[2048,768]{1,0:T(8,128)(2,1)}, f32[2048,128]{1,0:T(8,128)}, f32[8,768]{1,0:T(8,128)}, /*index=5*/f32[128,768]{1,0:T(8,128)}) custom-call(bf16[2048,768]{1,0:T(8,128)(2,1)} %get-tuple-element.80.y_ref, bf16[2048,768]{1,0:T(8,128)(2,1)} %get-tuple-element.81.gate_ref, ...), custom_call_target="tpu_custom_call" | custom-call | flops 402653184 | bytes 25165824 | tf_op jit(solution)/shard_map/ungate/pallas_call | solution.py:457
  122.5 3.6 collective-permute-done.5.grad_end_ref
  126.9 59.3 %unscan.1 = (bf16[2048,768]{1,0:T(8,128)(2,1)}, bf16[2048,640]{1,0:T(8,128)(2,1)}, f32[16,1536]{1,0:T(8,128)}, f32[8,1024]{1,0:T(8,128)}) custom-call(f32[2048,768]{1,0:T(8,128)} %get-tuple-element.90.gs_ref, bf16[2048,768]{1,0:T(8,128)(2,1)} %get-tuple-element.73.cv_ref.cv_before_ref, bf16[2048,768]{1,0:T(8,128)(2,1)} %get-tuple-element.73.cv_ref.cv_before_ref, ...), custom_call_target="tpu_custom_call" | custom-call | flops 4026531840 | bytes 18874368 | tf_op jit(solution)/shard_map/unscan/pallas_call | solution.py:662
  187.7 10.4 %multiply_reduce_fusion.1 = (f32[1536]{0:T(1024)}, bf16[1536,768]{1,0:T(8,128)(2,1)}) fusion(bf16[1536,768]{1,0:T(8,128)(2,1)} %wg_ref.3, bf16[2048,1536]{1,0:T(8,128)(2,1)} %get-tuple-element.74.normed_ref, bf16[2048,768]{1,0:T(8,128)(2,1)} %get-tuple-element.89.ggr_ref), kind=kOutput, calls=%fused_computation.2 | convolution fusion | flops 4836555264 | bytes 14161920 | tf_op jit(solution)/shard_map/dot_general | solution.py:34
  198.2 10.0 %fusion.10.rest_ref = f32[640,1536]{1,0:T(8,128)} fusion(bf16[2048,640]{1,0:T(8,128)(2,1)S(1)} %fusion.9.gr_ref, bf16[2048,1536]{1,0:T(8,128)(2,1)} %get-tuple-element.74.normed_ref), kind=kOutput, calls=%fused_computation.21 | convolution fusion | flops 4026531840 | bytes 12845056 | tf_op jit(solution)/shard_map/dot_general | solution.py:34
  208.2 11.3 %multiply_reduce_fusion = (f32[1536]{0:T(1024)}, bf16[1536,768]{1,0:T(8,128)(2,1)}) fusion(bf16[1536,768]{1,0:T(8,128)(2,1)S(1)} %copy-done.14, bf16[2048,1536]{1,0:T(8,128)(2,1)} %get-tuple-element.74.normed_ref, bf16[2048,768]{1,0:T(8,128)(2,1)S(1)} %fusion.7.gv_ref), kind=kOutput, calls=%fused_computation.1 | convolution fusion | flops 4836555264 | bytes 14161920 | tf_op jit(solution)/shard_map/dot_general | solution.py:34
  219.5 4.0 pack.1
  223.6 5.8 convolution_convert_fusion
  229.7 9.2 %convolution_convert_fusion.2 = bf16[768,1536]{1,0:T(8,128)(2,1)} fusion(bf16[2048,768]{1,0:T(8,128)(2,1)} %get-tuple-element.105, bf16[2048,1536]{1,0:T(8,128)(2,1)} %cot_ref.1), kind=kOutput, calls=%fused_computation.4 | convolution fusion | flops 4833017856 | bytes 11796480 | tf_op jit(solution)/shard_map/dot_general | solution.py:34
  238.9 5.2 convolution_convert_fusion.1.part_ref
  244.1 47.4 %all-reduce.8.cloned.1.call-done.packed_ref = f32[288,1536]{1,0:T(8,128)} async-done(((f32[288,1536]{1,0:T(8,128)}), f32[288,1536]{1,0:T(8,128)}) %all-reduce.8.cloned.1.call-update) | async-done | bytes 1769488 | tf_op jit(solution)/shard_map/psum | solution.py:1038
  291.5 2.4 late.1
  295.6 2.4 collective-permute-start.8
  299.4 335.1 %chain.1.out_b_ref.grad_ref = bf16[2944,1536]{1,0:T(8,128)(2,1)} custom-call(bf16[896,1536]{1,0:T(8,128)(2,1)} %convolution_convert_fusion.1.part_ref, bf16[2048,768]{1,0:T(8,128)(2,1)} %get-tuple-element.89.ggr_ref, bf16[2048,768]{1,0:T(8,128)(2,1)} %copy-done.11, bf16[2048,640]{1,0:T(8,128)(2,1)} %copy-done.13, bf16[1536,768]{1,0:T(8,128)(2,1)} %wg_ref.3, ...), custom_call_target="tpu_custom_call" | custom-call | flops 13690208256 | bytes 600000000 | tf_op jit(solution)/shard_map/chain/pallas_call | solution.py:824
  636.0 2.6 unpack.1
  638.6 9.8 %all-reduce.10.cloned.1.call-done = (bf16[1536,768]{1,0:T(8,128)(2,1)}, bf16[1536,768]{1,0:T(8,128)(2,1)}, bf16[768,1536]{1,0:T(8,128)(2,1)}) async-done(((bf16[1536,768]{1,0:T(8,128)(2,1)}, bf16[1536,768]{1,0:T(8,128)(2,1)}, bf16[768,1536]{1,0:T(8,128)(2,1)}), (bf16[1536,768]{1,0:T(8,128)(2,1)}, bf16[1536,768]{1,0:T(8,128)(2,1)}, bf16[768,1536]{1,0:T(8,128)(2,1)})) %all-reduce.10.cloned.1.call-update) | async-done | bytes 7077904 | tf_op jit(solution)/shard_map/psum | solution.py:1037
  648.4 29.5 %finish.1 = (bf16[2048,1536]{1,0:T(8,128)(2,1)}, f32[2048,1536]{1,0:T(8,128)}, f32[1536,768]{1,0:T(8,128)}, f32[1536,768]{1,0:T(8,128)}, f32[768,1536]{1,0:T(8,128)}) custom-call(f32[2048,128]{1,0:T(8,128)} %get-tuple-element.87.scale_ref, bf16[1152,1536]{1,0:T(8,128)(2,1)} %all-reduce.6.cloned.1.call-done.out_a_ref, ...), custom_call_target="tpu_custom_call" | custom-call | bytes 80000000 | tf_op jit(solution)/shard_map/finish/pallas_call | solution.py:875
  (63 shorter events, 23.5 us)
Async XLA Ops:
  7.2 66.0 %copy-start = (bf16[768,1536]{1,0:T(8,128)(2,1)S(1)}, bf16[768,1536]{1,0:T(8,128)(2,1)}, u32[]{:S(2)}) copy-start(bf16[768,1536]{1,0:T(8,128)(2,1)} %param.32) | copy-start | bytes 7077892
  7.2 33.6 %all-gather.2.cloned.1.call-start = ((), (), s32[]{:S(2)}) async-start(), calls=%async_computation | async-start | bytes 1310720 | tf_op jit(solution)/shard_map/all_gather | solution.py:994
  9.4 282.1 %all-reduce.8.cloned.1.call-start = ((), (), s32[]{:S(2)}) async-start(), calls=%async_computation.2 | async-start | bytes 3538944 | tf_op jit(solution)/shard_map/psum | solution.py:1038
  29.6 3.2 collective-permute-start
  32.9 8.0 %copy-start.9 = (bf16[8,2432]{1,0:T(8,128)(2,1)}, bf16[8,2432]{1,0:T(8,128)(2,1)S(1)}, u32[]{:S(2)}) copy-start(bf16[8,2432]{1,0:T(8,128)(2,1)S(1)} %collective-permute-done.halo_ref) | copy-start | bytes 116740
  71.8 10.8 %collective-permute-start.1 = (f32[128,768]{1,0:T(8,128)}, f32[128,768]{1,0:T(8,128)S(1)}, u32[]{:S(2)}, u32[]{:S(2)}) collective-permute-start(f32[128,768]{1,0:T(8,128)} %get-tuple-element.85), channel_id=1, source_target_pairs={{0,4},{4,8},{8,12},{12,16},{16,20},{20,24},{24,28},{1,5},{5,9},{9,... | collective-permute-start | bytes 1179656 | tf_op jit(solution)/shard_map/ppermute | solution.py:968
  82.5 0.8 copy-start.1
  93.8 6.3 collective-permute-start.2
  95.3 7.2 %collective-permute-start.3 = (f32[8,2048]{1,0:T(8,128)}, f32[8,2048]{1,0:T(8,128)S(1)}, u32[]{:S(2)}, u32[]{:S(2)}) collective-permute-start(f32[8,2048]{1,0:T(8,128)} %get-tuple-element.86.refs_0_), channel_id=1, source_target_pairs={{0,2},{1,3},{2,0},{3,1},{4,6},{5,7},{6,4},{7,5},{8,10},{9,11},{10,... | collective-permute-start | bytes 196616 | tf_op jit(solution)/shard_map/ppermute | solution.py:973
  96.5 6.5 collective-permute-start.4
  100.1 2.9 copy-start.6
  121.2 4.9 collective-permute-start.5
  186.2 11.9 %collective-permute-start.6 = (f32[8,1024]{1,0:T(8,128)}, f32[8,1024]{1,0:T(8,128)S(1)}, u32[]{:S(2)}, u32[]{:S(2)}) collective-permute-start(f32[8,1024]{1,0:T(8,128)} %get-tuple-element.103), channel_id=1, source_target_pairs={{4,0},{8,4},{12,8},{16,12},{20,16},{24,20},{28,24},{5,1},{9,5},{13... | collective-permute-start | bytes 98312 | tf_op jit(solution)/shard_map/ppermute | solution.py:968
  187.7 10.5 %copy-start.12 = (bf16[2048,640]{1,0:T(8,128)(2,1)S(1)}, bf16[2048,640]{1,0:T(8,128)(2,1)}, u32[]{:S(2)}) copy-start(bf16[2048,640]{1,0:T(8,128)(2,1)} %get-tuple-element.104) | copy-start | bytes 7864324
  198.2 10.0 %copy-start.13 = (bf16[2048,640]{1,0:T(8,128)(2,1)}, bf16[2048,640]{1,0:T(8,128)(2,1)S(1)}, u32[]{:S(2)}) copy-start(bf16[2048,640]{1,0:T(8,128)(2,1)S(1)} %fusion.9.gr_ref) | copy-start | bytes 7864324
  198.2 10.0 %copy-start.10 = (bf16[2048,768]{1,0:T(8,128)(2,1)S(1)}, bf16[2048,768]{1,0:T(8,128)(2,1)}, u32[]{:S(2)}) copy-start(bf16[2048,768]{1,0:T(8,128)(2,1)} %get-tuple-element.102) | copy-start | bytes 9437188
  198.2 10.0 %copy-start.14 = (bf16[1536,768]{1,0:T(8,128)(2,1)S(1)}, bf16[1536,768]{1,0:T(8,128)(2,1)}, u32[]{:S(2)}) copy-start(bf16[1536,768]{1,0:T(8,128)(2,1)} %wv_ref.3) | copy-start | bytes 7077892
  208.2 11.3 %copy-start.11 = (bf16[2048,768]{1,0:T(8,128)(2,1)}, bf16[2048,768]{1,0:T(8,128)(2,1)S(1)}, u32[]{:S(2)}) copy-start(bf16[2048,768]{1,0:T(8,128)(2,1)S(1)} %fusion.7.gv_ref) | copy-start | bytes 9437188
  223.5 415.1 %all-reduce.6.cloned.1.call-start = ((), (), s32[]{:S(2)}) async-start(), calls=%async_computation.1 | async-start | bytes 7077888 | tf_op jit(solution)/shard_map/psum | solution.py:1008
  229.4 419.0 %all-reduce.10.cloned.1.call-start = ((), (), s32[]{:S(2)}) async-start(), calls=%async_computation.3 | async-start | bytes 14155776 | tf_op jit(solution)/shard_map/psum | solution.py:1037
  294.0 340.6 %collective-permute-start.7 = (bf16[80,1536]{1,0:T(8,128)(2,1)}, bf16[80,1536]{1,0:T(8,128)(2,1)S(1)}, u32[]{:S(2)}, u32[]{:S(2)}) collective-permute-start(bf16[80,1536]{1,0:T(8,128)(2,1)} %get-tuple-element.109), channel_id=1, source_target_pairs={{0,1},{1,2},{2,3},{3,0},{4,5},{5,6},{6,7},{7,4},{8,9},{9,10},{10,1... | collective-permute-start | bytes 737288 | tf_op jit(solution)/shard_map/ppermute | solution.py:1041
  295.6 339.0 %collective-permute-start.8 = (bf16[80,1536]{1,0:T(8,128)(2,1)}, bf16[80,1536]{1,0:T(8,128)(2,1)S(1)}, u32[]{:S(2)}, u32[]{:S(2)}) collective-permute-start(bf16[80,1536]{1,0:T(8,128)(2,1)} %get-tuple-element.110), channel_id=1, source_target_pairs={{0,2},{1,3},{2,0},{3,1},{4,6},{5,7},{6,4},{7,5},{8,10},{9,11},{10,... | collective-permute-start | bytes 737288 | tf_op jit(solution)/shard_map/ppermute | solution.py:1041
  298.0 336.6 %collective-permute-start.9 = (bf16[80,1536]{1,0:T(8,128)(2,1)}, bf16[80,1536]{1,0:T(8,128)(2,1)S(1)}, u32[]{:S(2)}, u32[]{:S(2)}) collective-permute-start(bf16[80,1536]{1,0:T(8,128)(2,1)} %get-tuple-element.111), channel_id=1, source_target_pairs={{0,3},{1,0},{2,1},{3,2},{4,7},{5,4},{6,5},{7,6},{8,11},{9,8},{10,9... | collective-permute-start | bytes 737288 | tf_op jit(solution)/shard_map/ppermute | solution.py:1041
  634.6 0.8 copy-start.4
  (5 other events, 3.4 us)
Sparse Core Ops, SparseCore 0:
  10.1 30.6 all-gather.1
  223.6 67.8 all-reduce.7
  294.5 232.4 all-reduce.5
  531.1 117.3 all-reduce.9

commit v3 on v2

--- a/solution.py
+++ b/solution.py
@@ -840,51 +840,58 @@
 
 
 def finish_kernel(
-    early, scale_ref, out_a_ref, out_b_ref, grad_ref, x_ref, cot_ref, gain_ref, a_ref, b_ref, c_ref,
-    mixed_ref, grad_out_ref, a_out_ref, b_out_ref, c_out_ref,
+    early, scale_ref, early_a_ref, early_b_ref, late_a_ref, late_b_ref, grad_a_ref, grad_b_ref, x_ref, cot_ref, gain_ref,
+    a_ref, b_ref, c_ref, mixed_ref, grad_out_ref, a_out_ref, b_out_ref, c_out_ref,
 ):
     at = pl.program_id(0)
     width = x_ref.shape[1]
-    count = x_ref.shape[0] // 64
-
-    def part(k, none):
-        rows = pl.ds(pl.multiple_of(k * 64, 64), 64)
-        x = x_ref[rows, :].astype(F32)
-        scale = scale_ref[rows, 0:1]
-        total = jnp.where(at < early, out_a_ref[rows, :].astype(F32), out_b_ref[rows, :].astype(F32))
-        mixed_ref[rows, :] = (x + scale * total).astype(BF16)
-        inverse = lax.rsqrt(jnp.mean(x * x, -1, keepdims=True) + EPSILON)
-        weighted = grad_ref[rows, :].astype(F32) * gain_ref[...]
-        dot = jnp.sum(weighted * x, -1, keepdims=True)
-        grad_out_ref[rows, :] = cot_ref[rows, :].astype(F32) + inverse * weighted - x * (inverse**3 * dot / width)
-        return none
-
-    lax.fori_loop(0, count, part, 0)
+
+    def half(side, early_ref, late_ref, grad_ref):
+        def part(k, none):
+            own = pl.ds(pl.multiple_of(k * 64, 64), 64)
+            rows = pl.ds(pl.multiple_of(side * SPAN + k * 64, 64), 64)
+            x = x_ref[rows, :].astype(F32)
+            is_early = 2 * at + side < early
+            total = jnp.where(is_early, early_ref[own, :].astype(F32), late_ref[own, :].astype(F32))
+            mixed_ref[rows, :] = (x + scale_ref[rows, 0:1] * total).astype(BF16)
+            inverse = lax.rsqrt(jnp.mean(x * x, -1, keepdims=True) + EPSILON)
+            weighted = grad_ref[own, :].astype(F32) * gain_ref[...]
+            dot = jnp.sum(weighted * x, -1, keepdims=True)
+            grad_out_ref[rows, :] = cot_ref[rows, :].astype(F32) + inverse * weighted - x * (inverse**3 * dot / width)
+            return none
+
+        lax.fori_loop(0, SPAN // 64, part, 0)
+
+    half(0, early_a_ref, late_a_ref, grad_a_ref)
+    half(1, early_b_ref, late_b_ref, grad_b_ref)
     for source, target in ((a_ref, a_out_ref), (b_ref, b_out_ref), (c_ref, c_out_ref)):
         target[...] = source[...].astype(F32)
 
 
 def finish(scale, out_early, chained, hidden, cotangent, gain, sums):
     tokens, width = hidden.shape
-    per_step = 128
-    steps = tokens // per_step
-    early = out_early.shape[0] // per_step
-    late = steps - early
-    rows = lambda n, at=lambda i: i: pl.BlockSpec((per_step, n), lambda i: (at(i), 0))
+    steps = tokens // CHUNK
+    early = out_early.shape[0] // SPAN
+    late = tokens // SPAN - early
+    rows = lambda n: pl.BlockSpec((CHUNK, n), lambda i: (i, 0))
+    some = lambda at: pl.BlockSpec((SPAN, width), lambda i: (at(i), 0))
     parts = [pl.BlockSpec((a.shape[0] // steps, a.shape[1]), lambda i: (i, 0)) for a in sums]
     return pl.pallas_call(
         partial(finish_kernel, early),
         grid=(steps,),
         in_specs=[
-            rows(LANES), rows(width, lambda i: jnp.minimum(i, early - 1)), rows(width, lambda i: jnp.maximum(i - early, 0)),
-            rows(width, lambda i: i + late), rows(width), rows(width), pl.BlockSpec((1, width), lambda i: (0, 0)),
+            rows(LANES),
+            some(lambda i: jnp.minimum(2 * i, early - 1)), some(lambda i: jnp.minimum(2 * i + 1, early - 1)),
+            some(lambda i: jnp.maximum(2 * i - early, 0)), some(lambda i: jnp.maximum(2 * i + 1 - early, 0)),
+            some(lambda i: late + 2 * i), some(lambda i: late + 2 * i + 1),
+            rows(width), rows(width), pl.BlockSpec((1, width), lambda i: (0, 0)),
         ] + parts,
         out_specs=[rows(width), rows(width)] + parts,
         out_shape=[jax.ShapeDtypeStruct((tokens, width), BF16), jax.ShapeDtypeStruct((tokens, width), F32)]
         + [jax.ShapeDtypeStruct(a.shape, F32) for a in sums],
         cost_estimate=pl.CostEstimate(flops=0, bytes_accessed=80_000_000, transcendentals=0),
         name="finish",
-    )(scale, out_early, chained, chained, hidden, cotangent, gain, *sums)
+    )(scale, out_early, out_early, chained, chained, chained, chained, hidden, cotangent, gain, *sums)
 
 
 def pack_kernel(rest_ref, wb_ref, ws_ref, pg_ref, pv_ref, norm_ref, small_ref, packed_ref):
@@ -1003,9 +1010,9 @@
     )
     state_in = passed_along(local_end, "seq", 1)
     low, sums = gate_sums(y, reach, bc, state_in, gate_raw, gg, gain, picks)
-    sums = from_all(sums, "head")
     early = EARLY * ITEM
     out_early = lax.psum(nn(low[:early], w_out).astype(BF16), "head")
+    sums = from_all(sums, "head")
     out_late = nn(low[early:], w_out).astype(BF16)
 
     gs, grad_gate_raw, gate_low, scale, gain_sum, grad_state_in = ungate(
@@ -1019,6 +1026,7 @@
     )
     from_next = passed_along(head_rows, "seq", -1)
     grad_w_gate = row_major(tn(normed, grad_gate_raw))
+    products_gate = jnp.sum(w_gate.astype(F32) * grad_w_gate, 1)
 
     def with_next(a, low, high):
         tail = (a[tokens - 8 :, : high - low].astype(F32) + from_next[:, low:high]).astype(BF16)
@@ -1031,7 +1039,7 @@
     chained = chain_sums(out_late, grad_gate_raw, grad_value, grad_rest, w_gate, w_value, gathered, w_step_t)
 
     packed = pack(
-        grad_rest_t, gathered, w_step_t, jnp.sum(w_gate.astype(F32) * grad_w_gate, 1),
+        grad_rest_t, gathered, w_step_t, products_gate,
         jnp.sum(w_value.astype(F32) * grad_w_value, 1), norm, small,
     )
     weights = lax.psum(tuple(a.astype(BF16) for a in (grad_w_gate, grad_w_value, grad_w_out)), "seq")

time: 686 us -> 682 us (level)
  transfers between devices with their start and end apart: 14 -> 14, of which waited for: 8 -> 8; matrix products, arithmetic and copies ran while one was open for 6% -> 6% of each run, Pallas kernels for 52% -> 53%
where the time goes in v3:
time: 682 us; the launch traced here: 681 us
  Pallas kernels  508 us (74%)
  waiting for transfers between devices  73.8 us (11%)
  matrix products  61.3 us (9%)
  starting transfers between devices  17.5 us (3%)
  between operations  14 us (2%)
    pallas_call x1, Pallas kernels, chain_sums(): pl.pallas_call(partial(chain_kernel, first, size), grid=(items + behind(s...  335 us
    pallas_call x1, Pallas kernels, unscan(): pl.pallas_call(unscan_kernel, grid=(blocks,), in_specs=[rows(inner), rows...  59.3 us
    psum x1, waiting for transfers between devices, on_device(): packed = lax.psum(packed, 'seq')  47.4 us
    dot_general x4, matrix products, tn(): lax.dot_general(a, b, (((0,), (0,)), ((), ())), preferred_element_type=F32)  41 us
    pallas_call x1, Pallas kernels, scan(): pl.pallas_call(scan_kernel, grid=(blocks,), in_specs=[rows(inner), rows(n...  30.9 us
    pallas_call x1, Pallas kernels, finish(): pl.pallas_call(partial(finish_kernel, early), grid=(steps,), in_specs=[ro...  25.8 us
    pallas_call x1, Pallas kernels, project(): pl.pallas_call(project_kernel, grid=(tokens // CHUNK,), in_specs=[rows(wi...  17.8 us
    pallas_call x1, Pallas kernels, ungate(): pl.pallas_call(partial(ungate_kernel, len(sums)), grid=(tokens // CHUNK,)...  17.5 us
  transfers between devices with their start and end apart: 14, of which 8 were waited for; matrix products, arithmetic and copies ran while one was open for 6% of the time, Pallas kernels for 53%

profile of v3, /device:TPU:0, one launch (start us, length us, event | category | flops | bytes accessed | tf_op | source)
XLA Modules:
  0.0 680.8 jit_solution(11939311666003512887)
XLA Ops:
  9.5 17.8 %project.1 = (bf16[2048,1536]{1,0:T(8,128)(2,1)}, bf16[2048,768]{1,0:T(8,128)(2,1)}, bf16[2048,768]{1,0:T(8,128)(2,1)}, f32[2048,128]{1,0:T(8,128)}) custom-call(bf16[2048,1536]{1,0:T(8,128)(2,1)} %x_ref.3, f32[1,1536]{1,0:T(1,128)} %get-tuple-element.71.gain_ref.norm_ref, bf16[1536,768]{1,0:T(8,128)(2,1)} %wg_ref.3, bf16[1536,768]{1,0:T(8,128)(2,1)} %wv_ref.3, ...), custom_call_target="tpu_custom_call" | custom-call | flops 10468982784 | bytes 26738688 | tf_op jit(solution)/shard_map/project/pallas_call | solution.py:182
  32.9 8.0 %all-gather.2.cloned.1.call-done.gathered_ref.wb_ref = bf16[256,2048]{1,0:T(8,128)(2,1)} async-done(((bf16[64,2048]{1,0:T(8,128)(2,1)}), bf16[256,2048]{1,0:T(8,128)(2,1)}) %all-gather.2.cloned.1.call-update) | async-done | bytes 1048592 | tf_op jit(solution)/shard_map/all_gather | solution.py:1001
  40.8 30.9 %scan.1 = (bf16[2048,768]{1,0:T(8,128)(2,1)}, bf16[2048,256]{1,0:T(8,128)(2,1)}, f32[2048,128]{1,0:T(8,128)}, f32[2048,128]{1,0:T(8,128)}, f32[16,128,768]{2,1,0...) custom-call(bf16[2048,768]{1,0:T(8,128)(2,1)} %get-tuple-element.73., ...), custom_call_target="tpu_custom_call" | custom-call | flops 1610612736 | bytes 12582912 | tf_op jit(solution)/shard_map/scan/pallas_call | solution.py:321
  73.1 9.4 %convolution_convert_fusion.3.gg_ref = bf16[2048,768]{1,0:T(8,128)(2,1)} fusion(bf16[2048,1536]{1,0:T(8,128)(2,1)} %cot_ref.1, bf16[768,1536]{1,0:T(8,128)(2,1)S(1)} %copy-done), kind=kOutput, calls=%fused_computation.5 | convolution fusion | flops 4833411072 | bytes 11796480 | tf_op jit(solution)/shard_map/dot_general | solution.py:30
  83.3 10.5 %gate.1 = (bf16[2048,768]{1,0:T(8,128)(2,1)}, f32[8,2048]{1,0:T(8,128)}) custom-call(bf16[2048,768]{1,0:T(8,128)(2,1)} %get-tuple-element.80.y_ref, f32[2048,128]{1,0:T(8,128)} %get-tuple-element.83.reach_ref, bf16[2048,256]{1,0:T(8,128)(2,1)} %get-tuple-element.84.bc_ref, f32[128,768]{1,0:T(8,128)} %copy-done.1, ...), custom_call_target="tpu_custom_call" | custom-call | flops 402653184 | bytes 18874368 | tf_op jit(solution)/shard_map/gate/pallas_call | solution.py:392
  96.5 2.4 collective-permute-start.4
  100.1 2.4 collective-permute-done.3.refs_2_
  103.7 17.5 %ungate.1 = (f32[2048,768]{1,0:T(8,128)}, bf16[2048,768]{1,0:T(8,128)(2,1)}, bf16[2048,768]{1,0:T(8,128)(2,1)}, f32[2048,128]{1,0:T(8,128)}, f32[8,768]{1,0:T(8,128)}, /*index=5*/f32[128,768]{1,0:T(8,128)}) custom-call(bf16[2048,768]{1,0:T(8,128)(2,1)} %get-tuple-element.80.y_ref, bf16[2048,768]{1,0:T(8,128)(2,1)} %get-tuple-element.81.gate_ref, ...), custom_call_target="tpu_custom_call" | custom-call | flops 402653184 | bytes 25165824 | tf_op jit(solution)/shard_map/ungate/pallas_call | solution.py:457
  122.5 3.6 collective-permute-done.5.grad_end_ref
  126.9 59.3 %unscan.1 = (bf16[2048,768]{1,0:T(8,128)(2,1)}, bf16[2048,640]{1,0:T(8,128)(2,1)}, f32[16,1536]{1,0:T(8,128)}, f32[8,1024]{1,0:T(8,128)}) custom-call(f32[2048,768]{1,0:T(8,128)} %get-tuple-element.90.gs_ref, bf16[2048,768]{1,0:T(8,128)(2,1)} %get-tuple-element.73.cv_ref.cv_before_ref, bf16[2048,768]{1,0:T(8,128)(2,1)} %get-tuple-element.73.cv_ref.cv_before_ref, ...), custom_call_target="tpu_custom_call" | custom-call | flops 4026531840 | bytes 18874368 | tf_op jit(solution)/shard_map/unscan/pallas_call | solution.py:662
  187.7 10.4 %multiply_reduce_fusion.1 = (f32[1536]{0:T(1024)}, bf16[1536,768]{1,0:T(8,128)(2,1)}) fusion(bf16[1536,768]{1,0:T(8,128)(2,1)} %wg_ref.3, bf16[2048,1536]{1,0:T(8,128)(2,1)} %get-tuple-element.74.normed_ref, bf16[2048,768]{1,0:T(8,128)(2,1)} %get-tuple-element.89.ggr_ref), kind=kOutput, calls=%fused_computation.2 | convolution fusion | flops 4836555264 | bytes 14161920 | tf_op jit(solution)/shard_map/dot_general | solution.py:34
  198.2 10.0 %fusion.10.rest_ref = f32[640,1536]{1,0:T(8,128)} fusion(bf16[2048,640]{1,0:T(8,128)(2,1)S(1)} %fusion.9.gr_ref, bf16[2048,1536]{1,0:T(8,128)(2,1)} %get-tuple-element.74.normed_ref), kind=kOutput, calls=%fused_computation.21 | convolution fusion | flops 4026531840 | bytes 12845056 | tf_op jit(solution)/shard_map/dot_general | solution.py:34
  208.2 11.3 %multiply_reduce_fusion = (f32[1536]{0:T(1024)}, bf16[1536,768]{1,0:T(8,128)(2,1)}) fusion(bf16[1536,768]{1,0:T(8,128)(2,1)S(1)} %copy-done.14, bf16[2048,1536]{1,0:T(8,128)(2,1)} %get-tuple-element.74.normed_ref, bf16[2048,768]{1,0:T(8,128)(2,1)S(1)} %fusion.7.gv_ref), kind=kOutput, calls=%fused_computation.1 | convolution fusion | flops 4836555264 | bytes 14161920 | tf_op jit(solution)/shard_map/dot_general | solution.py:34
  219.5 4.0 pack.1
  223.6 5.8 convolution_convert_fusion
  229.7 9.2 %convolution_convert_fusion.2 = bf16[768,1536]{1,0:T(8,128)(2,1)} fusion(bf16[2048,768]{1,0:T(8,128)(2,1)} %get-tuple-element.105, bf16[2048,1536]{1,0:T(8,128)(2,1)} %cot_ref.1), kind=kOutput, calls=%fused_computation.4 | convolution fusion | flops 4833017856 | bytes 11796480 | tf_op jit(solution)/shard_map/dot_general | solution.py:34
  238.9 5.2 convolution_convert_fusion.1.part_ref
  244.1 47.4 %all-reduce.8.cloned.1.call-done.packed_ref = f32[288,1536]{1,0:T(8,128)} async-done(((f32[288,1536]{1,0:T(8,128)}), f32[288,1536]{1,0:T(8,128)}) %all-reduce.8.cloned.1.call-update) | async-done | bytes 1769488 | tf_op jit(solution)/shard_map/psum | solution.py:1046
  291.5 2.4 late.1
  295.6 2.4 collective-permute-start.8
  299.4 335.1 %chain.1.late_a_ref.late_b_ref.grad_a_ref.grad_b_ref = bf16[2944,1536]{1,0:T(8,128)(2,1)} custom-call(bf16[896,1536]{1,0:T(8,128)(2,1)} %convolution_convert_fusion.1.part_ref, bf16[2048,768]{1,0:T(8,128)(2,1)} %get-tuple-element.89.ggr_ref, bf16[2048,768]{1,0:T(8,128)(2,1)} %copy-done.11, bf16[2048,640]{1,0:T(8,128)(2,1)} %copy-done.13, ...), custom_call_target="tpu_custom_call" | custom-call | flops 13690208256 | bytes 600000000 | tf_op jit(solution)/shard_map/chain/pallas_call | solution.py:824
  636.0 2.6 unpack.1
  638.6 9.8 %all-reduce.10.cloned.1.call-done = (bf16[1536,768]{1,0:T(8,128)(2,1)}, bf16[1536,768]{1,0:T(8,128)(2,1)}, bf16[768,1536]{1,0:T(8,128)(2,1)}) async-done(((bf16[1536,768]{1,0:T(8,128)(2,1)}, bf16[1536,768]{1,0:T(8,128)(2,1)}, bf16[768,1536]{1,0:T(8,128)(2,1)}), (bf16[1536,768]{1,0:T(8,128)(2,1)}, bf16[1536,768]{1,0:T(8,128)(2,1)}, bf16[768,1536]{1,0:T(8,128)(2,1)})) %all-reduce.10.cloned.1.call-update) | async-done | bytes 7077904 | tf_op jit(solution)/shard_map/psum | solution.py:1045
  648.4 25.8 %finish.1 = (bf16[2048,1536]{1,0:T(8,128)(2,1)}, f32[2048,1536]{1,0:T(8,128)}, f32[1536,768]{1,0:T(8,128)}, f32[1536,768]{1,0:T(8,128)}, f32[768,1536]{1,0:T(8,128)}) custom-call(f32[2048,128]{1,0:T(8,128)} %get-tuple-element.87.scale_ref, bf16[1152,1536]{1,0:T(8,128)(2,1)} %all-reduce.6.cloned.1.call-done.early_a_ref.early_b_ref, ...), custom_call_target="tpu_custom_call" | custom-call | bytes 80000000 | tf_op jit(solution)/shard_map/finish/pallas_call | solution.py:879
  (63 shorter events, 23.5 us)
Async XLA Ops:
  7.2 66.0 %copy-start = (bf16[768,1536]{1,0:T(8,128)(2,1)S(1)}, bf16[768,1536]{1,0:T(8,128)(2,1)}, u32[]{:S(2)}) copy-start(bf16[768,1536]{1,0:T(8,128)(2,1)} %param.32) | copy-start | bytes 7077892
  7.2 33.6 %all-gather.2.cloned.1.call-start = ((), (), s32[]{:S(2)}) async-start(), calls=%async_computation | async-start | bytes 1310720 | tf_op jit(solution)/shard_map/all_gather | solution.py:1001
  9.4 282.1 %all-reduce.8.cloned.1.call-start = ((), (), s32[]{:S(2)}) async-start(), calls=%async_computation.2 | async-start | bytes 3538944 | tf_op jit(solution)/shard_map/psum | solution.py:1046
  29.6 3.2 collective-permute-start
  32.9 8.0 %copy-start.9 = (bf16[8,2432]{1,0:T(8,128)(2,1)}, bf16[8,2432]{1,0:T(8,128)(2,1)S(1)}, u32[]{:S(2)}) copy-start(bf16[8,2432]{1,0:T(8,128)(2,1)S(1)} %collective-permute-done.halo_ref) | copy-start | bytes 116740
  71.8 10.8 %collective-permute-start.1 = (f32[128,768]{1,0:T(8,128)}, f32[128,768]{1,0:T(8,128)S(1)}, u32[]{:S(2)}, u32[]{:S(2)}) collective-permute-start(f32[128,768]{1,0:T(8,128)} %get-tuple-element.85), channel_id=1, source_target_pairs={{0,4},{4,8},{8,12},{12,16},{16,20},{20,24},{24,28},{1,5},{5,9},{9,... | collective-permute-start | bytes 1179656 | tf_op jit(solution)/shard_map/ppermute | solution.py:975
  82.5 0.8 copy-start.1
  93.8 6.3 collective-permute-start.2
  95.3 7.2 %collective-permute-start.3 = (f32[8,2048]{1,0:T(8,128)}, f32[8,2048]{1,0:T(8,128)S(1)}, u32[]{:S(2)}, u32[]{:S(2)}) collective-permute-start(f32[8,2048]{1,0:T(8,128)} %get-tuple-element.86.refs_0_), channel_id=1, source_target_pairs={{0,2},{1,3},{2,0},{3,1},{4,6},{5,7},{6,4},{7,5},{8,10},{9,11},{10,... | collective-permute-start | bytes 196616 | tf_op jit(solution)/shard_map/ppermute | solution.py:980
  96.5 6.5 collective-permute-start.4
  100.1 2.9 copy-start.6
  121.2 4.9 collective-permute-start.5
  186.2 11.9 %collective-permute-start.6 = (f32[8,1024]{1,0:T(8,128)}, f32[8,1024]{1,0:T(8,128)S(1)}, u32[]{:S(2)}, u32[]{:S(2)}) collective-permute-start(f32[8,1024]{1,0:T(8,128)} %get-tuple-element.103), channel_id=1, source_target_pairs={{4,0},{8,4},{12,8},{16,12},{20,16},{24,20},{28,24},{5,1},{9,5},{13... | collective-permute-start | bytes 98312 | tf_op jit(solution)/shard_map/ppermute | solution.py:975
  187.7 10.5 %copy-start.12 = (bf16[2048,640]{1,0:T(8,128)(2,1)S(1)}, bf16[2048,640]{1,0:T(8,128)(2,1)}, u32[]{:S(2)}) copy-start(bf16[2048,640]{1,0:T(8,128)(2,1)} %get-tuple-element.104) | copy-start | bytes 7864324
  198.2 10.0 %copy-start.13 = (bf16[2048,640]{1,0:T(8,128)(2,1)}, bf16[2048,640]{1,0:T(8,128)(2,1)S(1)}, u32[]{:S(2)}) copy-start(bf16[2048,640]{1,0:T(8,128)(2,1)S(1)} %fusion.9.gr_ref) | copy-start | bytes 7864324
  198.2 10.0 %copy-start.10 = (bf16[2048,768]{1,0:T(8,128)(2,1)S(1)}, bf16[2048,768]{1,0:T(8,128)(2,1)}, u32[]{:S(2)}) copy-start(bf16[2048,768]{1,0:T(8,128)(2,1)} %get-tuple-element.102) | copy-start | bytes 9437188
  198.2 10.0 %copy-start.14 = (bf16[1536,768]{1,0:T(8,128)(2,1)S(1)}, bf16[1536,768]{1,0:T(8,128)(2,1)}, u32[]{:S(2)}) copy-start(bf16[1536,768]{1,0:T(8,128)(2,1)} %wv_ref.3) | copy-start | bytes 7077892
  208.2 11.3 %copy-start.11 = (bf16[2048,768]{1,0:T(8,128)(2,1)}, bf16[2048,768]{1,0:T(8,128)(2,1)S(1)}, u32[]{:S(2)}) copy-start(bf16[2048,768]{1,0:T(8,128)(2,1)S(1)} %fusion.7.gv_ref) | copy-start | bytes 9437188
  223.5 415.1 %all-reduce.6.cloned.1.call-start = ((), (), s32[]{:S(2)}) async-start(), calls=%async_computation.1 | async-start | bytes 7077888 | tf_op jit(solution)/shard_map/psum | solution.py:1014
  229.4 419.0 %all-reduce.10.cloned.1.call-start = ((), (), s32[]{:S(2)}) async-start(), calls=%async_computation.3 | async-start | bytes 14155776 | tf_op jit(solution)/shard_map/psum | solution.py:1045
  294.0 340.6 %collective-permute-start.7 = (bf16[80,1536]{1,0:T(8,128)(2,1)}, bf16[80,1536]{1,0:T(8,128)(2,1)S(1)}, u32[]{:S(2)}, u32[]{:S(2)}) collective-permute-start(bf16[80,1536]{1,0:T(8,128)(2,1)} %get-tuple-element.109), channel_id=1, source_target_pairs={{0,1},{1,2},{2,3},{3,0},{4,5},{5,6},{6,7},{7,4},{8,9},{9,10},{10,1... | collective-permute-start | bytes 737288 | tf_op jit(solution)/shard_map/ppermute | solution.py:1049
  295.6 339.0 %collective-permute-start.8 = (bf16[80,1536]{1,0:T(8,128)(2,1)}, bf16[80,1536]{1,0:T(8,128)(2,1)S(1)}, u32[]{:S(2)}, u32[]{:S(2)}) collective-permute-start(bf16[80,1536]{1,0:T(8,128)(2,1)} %get-tuple-element.110), channel_id=1, source_target_pairs={{0,2},{1,3},{2,0},{3,1},{4,6},{5,7},{6,4},{7,5},{8,10},{9,11},{10,... | collective-permute-start | bytes 737288 | tf_op jit(solution)/shard_map/ppermute | solution.py:1049
  298.0 336.6 %collective-permute-start.9 = (bf16[80,1536]{1,0:T(8,128)(2,1)}, bf16[80,1536]{1,0:T(8,128)(2,1)S(1)}, u32[]{:S(2)}, u32[]{:S(2)}) collective-permute-start(bf16[80,1536]{1,0:T(8,128)(2,1)} %get-tuple-element.111), channel_id=1, source_target_pairs={{0,3},{1,0},{2,1},{3,2},{4,7},{5,4},{6,5},{7,6},{8,11},{9,8},{10,9... | collective-permute-start | bytes 737288 | tf_op jit(solution)/shard_map/ppermute | solution.py:1049
  634.6 0.8 copy-start.4
  (5 other events, 3.4 us)
Sparse Core Ops, SparseCore 0:
  10.1 30.6 all-gather.1
  223.6 67.8 all-reduce.7
  294.5 232.4 all-reduce.5
  531.1 117.3 all-reduce.9

commit v4 on v3

--- a/solution.py
+++ b/solution.py
@@ -19,7 +19,8 @@
 F32 = jnp.float32
 BF16 = jnp.bfloat16
 ONE = pl.Buffered(1)
-EARLY = 36
+EARLY = 40
+TOGETHER = 4
 
 
 def nn(a, b):
@@ -202,7 +203,7 @@
 def scan_kernel(
     cv_ref, normed_ref, halo_ref, step_ref, ids_ref, heads_ref, taps_value_ref, gathered_ref, picks_ref,
     y_ref, bc_ref, cum_ref, reach_ref, enter_ref, end_ref, kept_ref, tok_ref, seg_ref, cs_ref, taps_ref, rim_ref,
-    carry, state, offset, reached, before,
+    carry, state, offset, reached, before, projected,
 ):
     at = pl.program_id(0)
     inner, width = cv_ref.shape[1], normed_ref.shape[1]
@@ -275,7 +276,12 @@
         carry[:, wide] = rows[count - 8 :]
         return pre * sigmoid(pre)
 
-    cs = nt(normed_ref[...], gathered_ref[:, :width]).astype(BF16)
+
+    @pl.when(at % TOGETHER == 0)
+    def _():
+        projected[...] = nt(normed_ref[...], gathered_ref[:, :width]).astype(BF16)
+
+    cs = projected[pl.ds(pl.multiple_of(at % TOGETHER * count, count), count), :]
     cs_ref[...] = cs
     both = conv(cs.astype(F32), inner).astype(BF16)
     bc_ref[...] = both
@@ -316,13 +322,14 @@
     tokens, inner = cv.shape
     blocks, total = tokens // SPAN, inner + 2 * STATE
     fixed = lambda n: pl.BlockSpec((8, n), lambda i: (0, 0))
+    together = pl.BlockSpec((TOGETHER * SPAN, normed.shape[1]), lambda i: (i // TOGETHER, 0))
     rows = lambda n: pl.BlockSpec((SPAN, n), lambda i: (i, 0))
     whole = lambda a: pl.BlockSpec(a.shape, lambda i: (0, 0), pipeline_mode=ONE)
     return pl.pallas_call(
         scan_kernel,
         grid=(blocks,),
         in_specs=[
-            rows(inner), rows(normed.shape[1]), whole(halo), rows(LANES), whole(ids), whole(heads), whole(taps_value),
+            rows(inner), together, whole(halo), rows(LANES), whole(ids), whole(heads), whole(taps_value),
             whole(gathered), whole(picks),
         ],
         out_specs=[
@@ -352,6 +359,7 @@
             pltpu.VMEM((8, LANES), F32),
             pltpu.VMEM((8, LANES), F32),
             pltpu.VMEM((8, LANES), F32),
+            pltpu.VMEM((TOGETHER * SPAN, 2 * STATE), BF16),
         ],
         cost_estimate=pl.CostEstimate(
             flops=2 * tokens * inner * (2 * SPAN + 2 * STATE),

time: 682 us -> 705 us (1.034)
  waiting for transfers between devices: 73.8 us -> 91.2 us
    psum x1, waiting for transfers between devices: 9.8 us -> 27.3 us  [on_device(): lax.psum(tuple((a.astype(BF16) for a in (grad_w_gate, grad_w_value, grad_...]
  transfers between devices with their start and end apart: 14 -> 14, of which waited for: 8 -> 8; matrix products, arithmetic and copies ran while one was open for 6% -> 6% of each run, Pallas kernels for 53% -> 51%
where the time goes in v4:
time: 705 us; the launch traced here: 704 us
  Pallas kernels  514 us (73%)
  waiting for transfers between devices  91.2 us (13%)
  matrix products  61.3 us (9%)
  starting transfers between devices  17.5 us (2%)
  between operations  14 us (2%)
    pallas_call x1, Pallas kernels, chain_sums(): pl.pallas_call(partial(chain_kernel, first, size), grid=(items + behind(s...  339 us
    pallas_call x1, Pallas kernels, unscan(): pl.pallas_call(unscan_kernel, grid=(blocks,), in_specs=[rows(inner), rows...  59.3 us
    psum x1, waiting for transfers between devices, on_device(): packed = lax.psum(packed, 'seq')  47.4 us
    dot_general x4, matrix products, tn(): lax.dot_general(a, b, (((0,), (0,)), ((), ())), preferred_element_type=F32)  41 us
    pallas_call x1, Pallas kernels, scan(): pl.pallas_call(scan_kernel, grid=(blocks,), in_specs=[rows(inner), togeth...  32.3 us
    psum x1, waiting for transfers between devices, on_device(): lax.psum(tuple((a.astype(BF16) for a in (grad_w_gate, grad_w_value, grad_...  27.3 us
    pallas_call x1, Pallas kernels, finish(): pl.pallas_call(partial(finish_kernel, early), grid=(steps,), in_specs=[ro...  25.8 us
    pallas_call x1, Pallas kernels, project(): pl.pallas_call(project_kernel, grid=(tokens // CHUNK,), in_specs=[rows(wi...  17.8 us
  transfers between devices with their start and end apart: 14, of which 8 were waited for; matrix products, arithmetic and copies ran while one was open for 6% of the time, Pallas kernels for 51%

profile of v4, /device:TPU:0, one launch (start us, length us, event | category | flops | bytes accessed | tf_op | source)
XLA Modules:
  0.0 704.2 jit_solution(11589409272154207693)
XLA Ops:
  9.5 17.8 %project.1 = (bf16[2048,1536]{1,0:T(8,128)(2,1)}, bf16[2048,768]{1,0:T(8,128)(2,1)}, bf16[2048,768]{1,0:T(8,128)(2,1)}, f32[2048,128]{1,0:T(8,128)}) custom-call(bf16[2048,1536]{1,0:T(8,128)(2,1)} %x_ref.3, f32[1,1536]{1,0:T(1,128)} %get-tuple-element.71.gain_ref.norm_ref, bf16[1536,768]{1,0:T(8,128)(2,1)} %wg_ref.3, bf16[1536,768]{1,0:T(8,128)(2,1)} %wv_ref.3, ...), custom_call_target="tpu_custom_call" | custom-call | flops 10468982784 | bytes 26738688 | tf_op jit(solution)/shard_map/project/pallas_call | solution.py:183
  32.9 8.0 %all-gather.2.cloned.1.call-done.gathered_ref.wb_ref = bf16[256,2048]{1,0:T(8,128)(2,1)} async-done(((bf16[64,2048]{1,0:T(8,128)(2,1)}), bf16[256,2048]{1,0:T(8,128)(2,1)}) %all-gather.2.cloned.1.call-update) | async-done | bytes 1048592 | tf_op jit(solution)/shard_map/all_gather | solution.py:1009
  40.8 32.3 %scan.1 = (bf16[2048,768]{1,0:T(8,128)(2,1)}, bf16[2048,256]{1,0:T(8,128)(2,1)}, f32[2048,128]{1,0:T(8,128)}, f32[2048,128]{1,0:T(8,128)}, f32[16,128,768]{2,1,0...) custom-call(bf16[2048,768]{1,0:T(8,128)(2,1)} %get-tuple-element.73., ...), custom_call_target="tpu_custom_call" | custom-call | flops 1610612736 | bytes 12582912 | tf_op jit(solution)/shard_map/scan/pallas_call | solution.py:328
  74.5 9.4 %convolution_convert_fusion.3.gg_ref = bf16[2048,768]{1,0:T(8,128)(2,1)} fusion(bf16[2048,1536]{1,0:T(8,128)(2,1)} %cot_ref.1, bf16[768,1536]{1,0:T(8,128)(2,1)S(1)} %copy-done), kind=kOutput, calls=%fused_computation.5 | convolution fusion | flops 4833411072 | bytes 11796480 | tf_op jit(solution)/shard_map/dot_general | solution.py:31
  84.7 10.5 %gate.1 = (bf16[2048,768]{1,0:T(8,128)(2,1)}, f32[8,2048]{1,0:T(8,128)}) custom-call(bf16[2048,768]{1,0:T(8,128)(2,1)} %get-tuple-element.80.y_ref, f32[2048,128]{1,0:T(8,128)} %get-tuple-element.83.reach_ref, bf16[2048,256]{1,0:T(8,128)(2,1)} %get-tuple-element.84.bc_ref, f32[128,768]{1,0:T(8,128)} %copy-done.1, ...), custom_call_target="tpu_custom_call" | custom-call | flops 402653184 | bytes 18874368 | tf_op jit(solution)/shard_map/gate/pallas_call | solution.py:400
  97.9 2.5 collective-permute-start.4
  101.5 2.4 collective-permute-done.3.refs_2_
  105.1 17.5 %ungate.1 = (f32[2048,768]{1,0:T(8,128)}, bf16[2048,768]{1,0:T(8,128)(2,1)}, bf16[2048,768]{1,0:T(8,128)(2,1)}, f32[2048,128]{1,0:T(8,128)}, f32[8,768]{1,0:T(8,128)}, /*index=5*/f32[128,768]{1,0:T(8,128)}) custom-call(bf16[2048,768]{1,0:T(8,128)(2,1)} %get-tuple-element.80.y_ref, bf16[2048,768]{1,0:T(8,128)(2,1)} %get-tuple-element.81.gate_ref, ...), custom_call_target="tpu_custom_call" | custom-call | flops 402653184 | bytes 25165824 | tf_op jit(solution)/shard_map/ungate/pallas_call | solution.py:465
  123.9 3.5 collective-permute-done.5.grad_end_ref
  128.2 59.3 %unscan.1 = (bf16[2048,768]{1,0:T(8,128)(2,1)}, bf16[2048,640]{1,0:T(8,128)(2,1)}, f32[16,1536]{1,0:T(8,128)}, f32[8,1024]{1,0:T(8,128)}) custom-call(f32[2048,768]{1,0:T(8,128)} %get-tuple-element.90.gs_ref, bf16[2048,768]{1,0:T(8,128)(2,1)} %get-tuple-element.73.cv_ref.cv_before_ref, bf16[2048,768]{1,0:T(8,128)(2,1)} %get-tuple-element.73.cv_ref.cv_before_ref, ...), custom_call_target="tpu_custom_call" | custom-call | flops 4026531840 | bytes 18874368 | tf_op jit(solution)/shard_map/unscan/pallas_call | solution.py:670
  189.1 10.4 %multiply_reduce_fusion.1 = (f32[1536]{0:T(1024)}, bf16[1536,768]{1,0:T(8,128)(2,1)}) fusion(bf16[1536,768]{1,0:T(8,128)(2,1)} %wg_ref.3, bf16[2048,1536]{1,0:T(8,128)(2,1)} %get-tuple-element.74.normed_ref, bf16[2048,768]{1,0:T(8,128)(2,1)} %get-tuple-element.89.ggr_ref), kind=kOutput, calls=%fused_computation.2 | convolution fusion | flops 4836555264 | bytes 14161920 | tf_op jit(solution)/shard_map/dot_general | solution.py:35
  199.6 10.0 %fusion.10.rest_ref = f32[640,1536]{1,0:T(8,128)} fusion(bf16[2048,640]{1,0:T(8,128)(2,1)S(1)} %fusion.9.gr_ref, bf16[2048,1536]{1,0:T(8,128)(2,1)} %get-tuple-element.74.normed_ref), kind=kOutput, calls=%fused_computation.21 | convolution fusion | flops 4026531840 | bytes 12845056 | tf_op jit(solution)/shard_map/dot_general | solution.py:35
  209.6 11.3 %multiply_reduce_fusion = (f32[1536]{0:T(1024)}, bf16[1536,768]{1,0:T(8,128)(2,1)}) fusion(bf16[1536,768]{1,0:T(8,128)(2,1)S(1)} %copy-done.14, bf16[2048,1536]{1,0:T(8,128)(2,1)} %get-tuple-element.74.normed_ref, bf16[2048,768]{1,0:T(8,128)(2,1)S(1)} %fusion.7.gv_ref), kind=kOutput, calls=%fused_computation.1 | convolution fusion | flops 4836555264 | bytes 14161920 | tf_op jit(solution)/shard_map/dot_general | solution.py:35
  220.9 4.0 pack.1
  224.9 6.3 convolution_convert_fusion
  231.5 9.2 %convolution_convert_fusion.1 = bf16[768,1536]{1,0:T(8,128)(2,1)} fusion(bf16[2048,768]{1,0:T(8,128)(2,1)} %get-tuple-element.105, bf16[2048,1536]{1,0:T(8,128)(2,1)} %cot_ref.1), kind=kOutput, calls=%fused_computation.3 | convolution fusion | flops 4833017856 | bytes 11796480 | tf_op jit(solution)/shard_map/dot_general | solution.py:35
  240.7 4.7 convolution_convert_fusion.2.part_ref
  245.4 47.4 %all-reduce.8.cloned.1.call-done.packed_ref = f32[288,1536]{1,0:T(8,128)} async-done(((f32[288,1536]{1,0:T(8,128)}), f32[288,1536]{1,0:T(8,128)}) %all-reduce.8.cloned.1.call-update) | async-done | bytes 1769488 | tf_op jit(solution)/shard_map/psum | solution.py:1054
  292.8 2.4 late.1
  296.8 2.4 collective-permute-start.8
  300.7 339.3 %chain.1.late_a_ref.late_b_ref.grad_a_ref.grad_b_ref = bf16[2816,1536]{1,0:T(8,128)(2,1)} custom-call(bf16[768,1536]{1,0:T(8,128)(2,1)} %convolution_convert_fusion.2.part_ref, bf16[2048,768]{1,0:T(8,128)(2,1)} %get-tuple-element.89.ggr_ref, bf16[2048,768]{1,0:T(8,128)(2,1)} %copy-done.11, bf16[2048,640]{1,0:T(8,128)(2,1)} %copy-done.13, ...), custom_call_target="tpu_custom_call" | custom-call | flops 13690208256 | bytes 600000000 | tf_op jit(solution)/shard_map/chain/pallas_call | solution.py:832
  641.5 3.0 unpack.1
  644.5 27.3 %all-reduce.10.cloned.1.call-done = (bf16[1536,768]{1,0:T(8,128)(2,1)}, bf16[1536,768]{1,0:T(8,128)(2,1)}, bf16[768,1536]{1,0:T(8,128)(2,1)}) async-done(((bf16[1536,768]{1,0:T(8,128)(2,1)}, bf16[1536,768]{1,0:T(8,128)(2,1)}, bf16[768,1536]{1,0:T(8,128)(2,1)}), (bf16[1536,768]{1,0:T(8,128)(2,1)}, bf16[1536,768]{1,0:T(8,128)(2,1)}, bf16[768,1536]{1,0:T(8,128)(2,1)})) %all-reduce.10.cloned.1.call-update) | async-done | bytes 7077904 | tf_op jit(solution)/shard_map/psum | solution.py:1053
  671.8 25.8 %finish.1 = (bf16[2048,1536]{1,0:T(8,128)(2,1)}, f32[2048,1536]{1,0:T(8,128)}, f32[1536,768]{1,0:T(8,128)}, f32[1536,768]{1,0:T(8,128)}, f32[768,1536]{1,0:T(8,128)}) custom-call(f32[2048,128]{1,0:T(8,128)} %get-tuple-element.87.scale_ref, bf16[1280,1536]{1,0:T(8,128)(2,1)} %all-reduce.6.cloned.1.call-done.early_a_ref.early_b_ref, ...), custom_call_target="tpu_custom_call" | custom-call | bytes 80000000 | tf_op jit(solution)/shard_map/finish/pallas_call | solution.py:887
  (63 shorter events, 23.5 us)
Async XLA Ops:
  7.2 67.3 %copy-start = (bf16[768,1536]{1,0:T(8,128)(2,1)S(1)}, bf16[768,1536]{1,0:T(8,128)(2,1)}, u32[]{:S(2)}) copy-start(bf16[768,1536]{1,0:T(8,128)(2,1)} %param.32) | copy-start | bytes 7077892
  7.2 33.6 %all-gather.2.cloned.1.call-start = ((), (), s32[]{:S(2)}) async-start(), calls=%async_computation | async-start | bytes 1310720 | tf_op jit(solution)/shard_map/all_gather | solution.py:1009
  9.4 283.4 %all-reduce.8.cloned.1.call-start = ((), (), s32[]{:S(2)}) async-start(), calls=%async_computation.2 | async-start | bytes 3538944 | tf_op jit(solution)/shard_map/psum | solution.py:1054
  29.6 3.2 collective-permute-start
  32.9 8.0 %copy-start.9 = (bf16[8,2432]{1,0:T(8,128)(2,1)}, bf16[8,2432]{1,0:T(8,128)(2,1)S(1)}, u32[]{:S(2)}) copy-start(bf16[8,2432]{1,0:T(8,128)(2,1)S(1)} %collective-permute-done.halo_ref) | copy-start | bytes 116740
  73.1 10.8 %collective-permute-start.1 = (f32[128,768]{1,0:T(8,128)}, f32[128,768]{1,0:T(8,128)S(1)}, u32[]{:S(2)}, u32[]{:S(2)}) collective-permute-start(f32[128,768]{1,0:T(8,128)} %get-tuple-element.85), channel_id=1, source_target_pairs={{0,4},{4,8},{8,12},{12,16},{16,20},{20,24},{24,28},{1,5},{5,9},{9,... | collective-permute-start | bytes 1179656 | tf_op jit(solution)/shard_map/ppermute | solution.py:983
  83.9 0.8 copy-start.1
  95.2 6.3 collective-permute-start.2
  96.7 7.2 %collective-permute-start.3 = (f32[8,2048]{1,0:T(8,128)}, f32[8,2048]{1,0:T(8,128)S(1)}, u32[]{:S(2)}, u32[]{:S(2)}) collective-permute-start(f32[8,2048]{1,0:T(8,128)} %get-tuple-element.86.refs_0_), channel_id=1, source_target_pairs={{0,2},{1,3},{2,0},{3,1},{4,6},{5,7},{6,4},{7,5},{8,10},{9,11},{10,... | collective-permute-start | bytes 196616 | tf_op jit(solution)/shard_map/ppermute | solution.py:988
  97.9 6.5 collective-permute-start.4
  101.5 2.9 copy-start.6
  122.6 4.8 collective-permute-start.5
  187.6 11.9 %collective-permute-start.6 = (f32[8,1024]{1,0:T(8,128)}, f32[8,1024]{1,0:T(8,128)S(1)}, u32[]{:S(2)}, u32[]{:S(2)}) collective-permute-start(f32[8,1024]{1,0:T(8,128)} %get-tuple-element.103), channel_id=1, source_target_pairs={{4,0},{8,4},{12,8},{16,12},{20,16},{24,20},{28,24},{5,1},{9,5},{13... | collective-permute-start | bytes 98312 | tf_op jit(solution)/shard_map/ppermute | solution.py:983
  189.1 10.5 %copy-start.12 = (bf16[2048,640]{1,0:T(8,128)(2,1)S(1)}, bf16[2048,640]{1,0:T(8,128)(2,1)}, u32[]{:S(2)}) copy-start(bf16[2048,640]{1,0:T(8,128)(2,1)} %get-tuple-element.104) | copy-start | bytes 7864324
  199.5 10.0 %copy-start.13 = (bf16[2048,640]{1,0:T(8,128)(2,1)}, bf16[2048,640]{1,0:T(8,128)(2,1)S(1)}, u32[]{:S(2)}) copy-start(bf16[2048,640]{1,0:T(8,128)(2,1)S(1)} %fusion.9.gr_ref) | copy-start | bytes 7864324
  199.5 10.0 %copy-start.10 = (bf16[2048,768]{1,0:T(8,128)(2,1)S(1)}, bf16[2048,768]{1,0:T(8,128)(2,1)}, u32[]{:S(2)}) copy-start(bf16[2048,768]{1,0:T(8,128)(2,1)} %get-tuple-element.102) | copy-start | bytes 9437188
  199.5 10.0 %copy-start.14 = (bf16[1536,768]{1,0:T(8,128)(2,1)S(1)}, bf16[1536,768]{1,0:T(8,128)(2,1)}, u32[]{:S(2)}) copy-start(bf16[1536,768]{1,0:T(8,128)(2,1)} %wv_ref.3) | copy-start | bytes 7077892
  209.5 11.3 %copy-start.11 = (bf16[2048,768]{1,0:T(8,128)(2,1)}, bf16[2048,768]{1,0:T(8,128)(2,1)S(1)}, u32[]{:S(2)}) copy-start(bf16[2048,768]{1,0:T(8,128)(2,1)S(1)} %fusion.7.gv_ref) | copy-start | bytes 9437188
  224.9 419.6 %all-reduce.6.cloned.1.call-start = ((), (), s32[]{:S(2)}) async-start(), calls=%async_computation.1 | async-start | bytes 7864320 | tf_op jit(solution)/shard_map/psum | solution.py:1022
  231.2 440.6 %all-reduce.10.cloned.1.call-start = ((), (), s32[]{:S(2)}) async-start(), calls=%async_computation.3 | async-start | bytes 14155776 | tf_op jit(solution)/shard_map/psum | solution.py:1053
  295.2 344.8 %collective-permute-start.7 = (bf16[80,1536]{1,0:T(8,128)(2,1)}, bf16[80,1536]{1,0:T(8,128)(2,1)S(1)}, u32[]{:S(2)}, u32[]{:S(2)}) collective-permute-start(bf16[80,1536]{1,0:T(8,128)(2,1)} %get-tuple-element.109), channel_id=1, source_target_pairs={{0,1},{1,2},{2,3},{3,0},{4,5},{5,6},{6,7},{7,4},{8,9},{9,10},{10,1... | collective-permute-start | bytes 737288 | tf_op jit(solution)/shard_map/ppermute | solution.py:1057
  296.8 343.2 %collective-permute-start.8 = (bf16[80,1536]{1,0:T(8,128)(2,1)}, bf16[80,1536]{1,0:T(8,128)(2,1)S(1)}, u32[]{:S(2)}, u32[]{:S(2)}) collective-permute-start(bf16[80,1536]{1,0:T(8,128)(2,1)} %get-tuple-element.110), channel_id=1, source_target_pairs={{0,2},{1,3},{2,0},{3,1},{4,6},{5,7},{6,4},{7,5},{8,10},{9,11},{10,... | collective-permute-start | bytes 737288 | tf_op jit(solution)/shard_map/ppermute | solution.py:1057
  299.3 340.8 %collective-permute-start.9 = (bf16[80,1536]{1,0:T(8,128)(2,1)}, bf16[80,1536]{1,0:T(8,128)(2,1)S(1)}, u32[]{:S(2)}, u32[]{:S(2)}) collective-permute-start(bf16[80,1536]{1,0:T(8,128)(2,1)} %get-tuple-element.111), channel_id=1, source_target_pairs={{0,3},{1,0},{2,1},{3,2},{4,7},{5,4},{6,5},{7,6},{8,11},{9,8},{10,9... | collective-permute-start | bytes 737288 | tf_op jit(solution)/shard_map/ppermute | solution.py:1057
  640.0 0.8 copy-start.4
  (5 other events, 3.4 us)
Sparse Core Ops, SparseCore 0:
  10.1 30.6 all-gather.1
  225.0 67.7 all-reduce.7
  295.8 254.4 all-reduce.5
  554.3 117.4 all-reduce.9

commit v5 on v3

--- a/solution.py
+++ b/solution.py
@@ -19,7 +19,7 @@
 F32 = jnp.float32
 BF16 = jnp.bfloat16
 ONE = pl.Buffered(1)
-EARLY = 36
+EARLY = 40
 
 
 def nn(a, b):
@@ -200,12 +200,12 @@
 
 
 def scan_kernel(
-    cv_ref, normed_ref, halo_ref, step_ref, ids_ref, heads_ref, taps_value_ref, gathered_ref, picks_ref,
-    y_ref, bc_ref, cum_ref, reach_ref, enter_ref, end_ref, kept_ref, tok_ref, seg_ref, cs_ref, taps_ref, rim_ref,
+    cv_ref, cs_ref, halo_ref, step_ref, ids_ref, heads_ref, taps_value_ref, gathered_ref, picks_ref,
+    y_ref, bc_ref, cum_ref, reach_ref, enter_ref, end_ref, kept_ref, tok_ref, seg_ref, taps_ref, rim_ref,
     carry, state, offset, reached, before,
 ):
     at = pl.program_id(0)
-    inner, width = cv_ref.shape[1], normed_ref.shape[1]
+    inner, width = cv_ref.shape[1], gathered_ref.shape[1] - 4 * LANES
     count = SPAN
 
     @pl.when(at == 0)
@@ -275,9 +275,7 @@
         carry[:, wide] = rows[count - 8 :]
         return pre * sigmoid(pre)
 
-    cs = nt(normed_ref[...], gathered_ref[:, :width]).astype(BF16)
-    cs_ref[...] = cs
-    both = conv(cs.astype(F32), inner).astype(BF16)
+    both = conv(cs_ref[...].astype(F32), inner).astype(BF16)
     bc_ref[...] = both
     b_low, c_low = both[:, :LANES], both[:, LANES:]
     scores = nt(c_low, b_low)
@@ -309,10 +307,10 @@
         state[:, wide] = spread(through, low, width) * entering + nn(
             b_t, (scaled * ends).astype(BF16)
         )
-    end_ref[...] = state[...]
-
-
-def scan(cv, normed, halo, step_raw, ids, heads, taps_value, gathered, picks):
+    end_ref[...] = state[...].astype(BF16)
+
+
+def scan(cv, cs, halo, step_raw, ids, heads, taps_value, gathered, picks):
     tokens, inner = cv.shape
     blocks, total = tokens // SPAN, inner + 2 * STATE
     fixed = lambda n: pl.BlockSpec((8, n), lambda i: (0, 0))
@@ -322,7 +320,7 @@
         scan_kernel,
         grid=(blocks,),
         in_specs=[
-            rows(inner), rows(normed.shape[1]), whole(halo), rows(LANES), whole(ids), whole(heads), whole(taps_value),
+            rows(inner), rows(2 * STATE), whole(halo), rows(LANES), whole(ids), whole(heads), whole(taps_value),
             whole(gathered), whole(picks),
         ],
         out_specs=[
@@ -330,7 +328,7 @@
             pl.BlockSpec((1, STATE, inner), lambda i: (i, 0, 0)),
             pl.BlockSpec((STATE, inner), lambda i: (0, 0)),
             pl.BlockSpec((1, 8, LANES), lambda i: (i, 0, 0)), rows(LANES), pl.BlockSpec((1, 8, SPAN), lambda i: (i, 0, 0)),
-            rows(2 * STATE), fixed(total), fixed(total),
+            fixed(total), fixed(total),
         ],
         out_shape=[
             jax.ShapeDtypeStruct((tokens, inner), BF16),
@@ -338,11 +336,10 @@
             jax.ShapeDtypeStruct((tokens, LANES), F32),
             jax.ShapeDtypeStruct((tokens, LANES), F32),
             jax.ShapeDtypeStruct((blocks, STATE, inner), F32),
-            jax.ShapeDtypeStruct((STATE, inner), F32),
+            jax.ShapeDtypeStruct((STATE, inner), BF16),
             jax.ShapeDtypeStruct((blocks, 8, LANES), F32),
             jax.ShapeDtypeStruct((tokens, LANES), F32),
             jax.ShapeDtypeStruct((blocks, 8, SPAN), F32),
-            jax.ShapeDtypeStruct((tokens, 2 * STATE), BF16),
             jax.ShapeDtypeStruct((8, total), F32),
             jax.ShapeDtypeStruct((8, total), F32),
         ],
@@ -359,7 +356,7 @@
             transcendentals=tokens * inner * 4,
         ),
         name="scan",
-    )(cv, normed, halo, step_raw, ids, heads, taps_value, gathered, picks)
+    )(cv, cs, halo, step_raw, ids, heads, taps_value, gathered, picks)
 
 
 def gate_kernel(
@@ -373,7 +370,7 @@
     for pair in range(inner // LANES):
         wide = slice(pair * LANES, (pair + 1) * LANES)
         reach_pair = nn(reach, picks_ref[:, wide])
-        ssm = y_ref[:, wide].astype(F32) + reach_pair * nn(c_low, state_ref[:, wide].astype(BF16))
+        ssm = y_ref[:, wide].astype(F32) + reach_pair * nn(c_low, state_ref[:, wide])
         gate = gate_ref[:, wide].astype(F32)
         gated = ssm * gate * sigmoid(gate)
         weighted = gated * gain_ref[:, wide]
@@ -432,7 +429,7 @@
     for pair in range(inner // LANES):
         wide = slice(pair * LANES, (pair + 1) * LANES)
         reach_pair = nn(reach, picks_ref[:, wide])
-        ssm = y_ref[:, wide].astype(F32) + reach_pair * nn(c_low, in_ref[:, wide].astype(BF16))
+        ssm = y_ref[:, wide].astype(F32) + reach_pair * nn(c_low, in_ref[:, wide])
         gate, gg = gate_ref[:, wide].astype(F32), gg_ref[:, wide].astype(F32)
         sg = sigmoid(gate)
         act = gate * sg
@@ -569,7 +566,7 @@
         scaled = values * step_wide
         scaled_low = scaled.astype(BF16)
         grad_y = gs_ref[:, wide]
-        entering = enter_ref[0, :, wide] + spread(kept[0:1], low, width) * state_in_ref[:, wide]
+        entering = enter_ref[0, :, wide] + spread(kept[0:1], low, width) * state_in_ref[:, wide].astype(F32)
         grad_state = grad[:, wide]
         grad_low = grad_state.astype(BF16)
         state_low, state_rest = halves(entering)
@@ -1005,8 +1002,9 @@
     tail = jnp.concatenate([cv[tokens - 8 :], last_ids, normed[tokens - 8 :]], 1)
     halo = passed_along(tail, "seq", 1)
     gg = nt(cotangent, w_out).astype(BF16)
-    y, bc, cum, reach, enter, local_end, kept, tokens_info, seg_rows, cs, taps, rim = scan(
-        cv, normed, halo, step_raw, ids, heads, taps_value, gathered, picks
+    cs = nt(normed, gathered[:, :width]).astype(BF16)
+    y, bc, cum, reach, enter, local_end, kept, tokens_info, seg_rows, taps, rim = scan(
+        cv, cs, halo, step_raw, ids, heads, taps_value, gathered, picks
     )
     state_in = passed_along(local_end, "seq", 1)
     low, sums = gate_sums(y, reach, bc, state_in, gate_raw, gg, gain, picks)

time: 682 us -> 700 us (1.026)
  waiting for transfers between devices: 73.8 us -> 91.2 us
    psum x1, waiting for transfers between devices: 9.8 us -> 27.3 us  [on_device(): lax.psum(tuple((a.astype(BF16) for a in (grad_w_gate, grad_w_value, grad_...]
    dot_general x1 -> x2, matrix products: 9.39 us -> 15.1 us  [nt(): lax.dot_general(a, b, (((1,), (1,)), ((), ())), preferred_element_type=F32)]
  transfers between devices with their start and end apart: 14 -> 14, of which waited for: 8 -> 6; matrix products, arithmetic and copies ran while one was open for 6% -> 7% of each run, Pallas kernels for 53% -> 52%
where the time goes in v5:
time: 700 us; the launch traced here: 699 us
  Pallas kernels  507 us (72%)
  waiting for transfers between devices  91.2 us (13%)
  matrix products  63.4 us (9%)
  starting transfers between devices  16.2 us (2%)
  between operations  14 us (2%)
    pallas_call x1, Pallas kernels, chain_sums(): pl.pallas_call(partial(chain_kernel, first, size), grid=(items + behind(s...  339 us
    pallas_call x1, Pallas kernels, unscan(): pl.pallas_call(unscan_kernel, grid=(blocks,), in_specs=[rows(inner), rows...  59.5 us
    psum x1, waiting for transfers between devices, on_device(): packed = lax.psum(packed, 'seq')  45.8 us
    dot_general x4, matrix products, tn(): lax.dot_general(a, b, (((0,), (0,)), ((), ())), preferred_element_type=F32)  37.3 us
    psum x1, waiting for transfers between devices, on_device(): lax.psum(tuple((a.astype(BF16) for a in (grad_w_gate, grad_w_value, grad_...  27.3 us
    pallas_call x1, Pallas kernels, finish(): pl.pallas_call(partial(finish_kernel, early), grid=(steps,), in_specs=[ro...  25.9 us
    pallas_call x1, Pallas kernels, scan(): pl.pallas_call(scan_kernel, grid=(blocks,), in_specs=[rows(inner), rows(2...  24.8 us
    pallas_call x1, Pallas kernels, project(): pl.pallas_call(project_kernel, grid=(tokens // CHUNK,), in_specs=[rows(wi...  17.8 us
  transfers between devices with their start and end apart: 14, of which 6 were waited for; matrix products, arithmetic and copies ran while one was open for 7% of the time, Pallas kernels for 52%

profile of v5, /device:TPU:0, one launch (start us, length us, event | category | flops | bytes accessed | tf_op | source)
XLA Modules:
  0.0 698.5 jit_solution(9731185124709395483)
XLA Ops:
  10.3 17.8 %project.1 = (bf16[2048,1536]{1,0:T(8,128)(2,1)}, bf16[2048,768]{1,0:T(8,128)(2,1)}, bf16[2048,768]{1,0:T(8,128)(2,1)}, f32[2048,128]{1,0:T(8,128)}) custom-call(bf16[2048,1536]{1,0:T(8,128)(2,1)} %x_ref.3, f32[1,1536]{1,0:T(1,128)} %get-tuple-element.70.gain_ref.norm_ref, bf16[1536,768]{1,0:T(8,128)(2,1)} %wg_ref.3, bf16[1536,768]{1,0:T(8,128)(2,1)} %wv_ref.3, ...), custom_call_target="tpu_custom_call" | custom-call | flops 10468982784 | bytes 26738688 | tf_op jit(solution)/shard_map/project/pallas_call | solution.py:182
  29.6 2.4 collective-permute-start
  32.0 8.9 %all-gather.2.cloned.1.call-done.gathered_ref.wb_ref = bf16[256,2048]{1,0:T(8,128)(2,1)} async-done(((bf16[64,2048]{1,0:T(8,128)(2,1)}), bf16[256,2048]{1,0:T(8,128)(2,1)}) %all-gather.2.cloned.1.call-update) | async-done | bytes 1048592 | tf_op jit(solution)/shard_map/all_gather | solution.py:998
  40.9 5.7 convolution_convert_fusion.4.cs_ref.cs_before_ref
  47.3 24.8 %scan.1 = (bf16[2048,768]{1,0:T(8,128)(2,1)}, bf16[2048,256]{1,0:T(8,128)(2,1)}, f32[2048,128]{1,0:T(8,128)}, f32[2048,128]{1,0:T(8,128)}, f32[16,128,768]{2,1,0...) custom-call(bf16[2048,768]{1,0:T(8,128)(2,1)} %get-tuple-element.72., ...), custom_call_target="tpu_custom_call" | custom-call | flops 1610612736 | bytes 12582912 | tf_op jit(solution)/shard_map/scan/pallas_call | solution.py:319
  73.3 9.4 %convolution_convert_fusion.3.gg_ref = bf16[2048,768]{1,0:T(8,128)(2,1)} fusion(bf16[2048,1536]{1,0:T(8,128)(2,1)} %cot_ref.1, bf16[768,1536]{1,0:T(8,128)(2,1)S(1)} %copy-done), kind=kOutput, calls=%fused_computation.5 | convolution fusion | flops 4833411072 | bytes 11796480 | tf_op jit(solution)/shard_map/dot_general | solution.py:30
  83.4 10.4 %gate.1 = (bf16[2048,768]{1,0:T(8,128)(2,1)}, f32[8,2048]{1,0:T(8,128)}) custom-call(bf16[2048,768]{1,0:T(8,128)(2,1)} %get-tuple-element.79.y_ref, f32[2048,128]{1,0:T(8,128)} %get-tuple-element.82.reach_ref, bf16[2048,256]{1,0:T(8,128)(2,1)} %get-tuple-element.83.bc_ref, bf16[128,768]{1,0:T(8,128)(2,1)} %copy-done.1, ...), custom_call_target="tpu_custom_call" | custom-call | flops 402653184 | bytes 18874368 | tf_op jit(solution)/shard_map/gate/pallas_call | solution.py:389
  98.3 6.1 collective-permute-done.3.refs_2_
  105.7 17.5 %ungate.1 = (f32[2048,768]{1,0:T(8,128)}, bf16[2048,768]{1,0:T(8,128)(2,1)}, bf16[2048,768]{1,0:T(8,128)(2,1)}, f32[2048,128]{1,0:T(8,128)}, f32[8,768]{1,0:T(8,128)}, /*index=5*/f32[128,768]{1,0:T(8,128)}) custom-call(bf16[2048,768]{1,0:T(8,128)(2,1)} %get-tuple-element.79.y_ref, bf16[2048,768]{1,0:T(8,128)(2,1)} %get-tuple-element.80.gate_ref, ...), custom_call_target="tpu_custom_call" | custom-call | flops 402653184 | bytes 25165824 | tf_op jit(solution)/shard_map/ungate/pallas_call | solution.py:454
  127.8 59.5 %unscan.1 = (bf16[2048,768]{1,0:T(8,128)(2,1)}, bf16[2048,640]{1,0:T(8,128)(2,1)}, f32[16,1536]{1,0:T(8,128)}, f32[8,1024]{1,0:T(8,128)}) custom-call(f32[2048,768]{1,0:T(8,128)} %get-tuple-element.89.gs_ref, bf16[2048,768]{1,0:T(8,128)(2,1)} %get-tuple-element.72.cv_ref.cv_before_ref, bf16[2048,768]{1,0:T(8,128)(2,1)} %get-tuple-element.72.cv_ref.cv_before_ref, ...), custom_call_target="tpu_custom_call" | custom-call | flops 4026531840 | bytes 18874368 | tf_op jit(solution)/shard_map/unscan/pallas_call | solution.py:659
  188.7 10.4 %multiply_reduce_fusion.1 = (f32[1536]{0:T(1024)}, bf16[1536,768]{1,0:T(8,128)(2,1)}) fusion(bf16[1536,768]{1,0:T(8,128)(2,1)} %wg_ref.3, bf16[2048,1536]{1,0:T(8,128)(2,1)} %get-tuple-element.73, bf16[2048,768]{1,0:T(8,128)(2,1)} %get-tuple-element.88.ggr_ref), kind=kOutput, calls=%fused_computation.2 | convolution fusion | flops 4836555264 | bytes 14161920 | tf_op jit(solution)/shard_map/dot_general | solution.py:34
  199.1 11.4 %multiply_reduce_fusion = (f32[1536]{0:T(1024)}, bf16[1536,768]{1,0:T(8,128)(2,1)}) fusion(bf16[1536,768]{1,0:T(8,128)(2,1)S(1)} %copy-done.13, bf16[2048,1536]{1,0:T(8,128)(2,1)} %get-tuple-element.73, bf16[2048,768]{1,0:T(8,128)(2,1)S(1)} %fusion.8.gv_ref), kind=kOutput, calls=%fused_computation.1 | convolution fusion | flops 4836555264 | bytes 14161920 | tf_op jit(solution)/shard_map/dot_general | solution.py:34
  210.6 6.2 fusion.11.rest_ref
  216.8 3.9 pack.1
  221.0 6.3 convolution_convert_fusion
  227.3 9.3 %convolution_convert_fusion.1 = bf16[768,1536]{1,0:T(8,128)(2,1)} fusion(bf16[2048,768]{1,0:T(8,128)(2,1)} %get-tuple-element.103, bf16[2048,1536]{1,0:T(8,128)(2,1)} %cot_ref.1), kind=kOutput, calls=%fused_computation.3 | convolution fusion | flops 4833017856 | bytes 11796480 | tf_op jit(solution)/shard_map/dot_general | solution.py:34
  236.6 4.7 convolution_convert_fusion.2.part_ref
  241.3 45.8 %all-reduce.8.cloned.1.call-done.packed_ref = f32[288,1536]{1,0:T(8,128)} async-done(((f32[288,1536]{1,0:T(8,128)}), f32[288,1536]{1,0:T(8,128)}) %all-reduce.8.cloned.1.call-update) | async-done | bytes 1769488 | tf_op jit(solution)/shard_map/psum | solution.py:1044
  287.1 2.4 late.1
  291.2 2.4 collective-permute-start.8
  295.0 339.3 %chain.1.late_a_ref.late_b_ref.grad_a_ref.grad_b_ref = bf16[2816,1536]{1,0:T(8,128)(2,1)} custom-call(bf16[768,1536]{1,0:T(8,128)(2,1)} %convolution_convert_fusion.2.part_ref, bf16[2048,768]{1,0:T(8,128)(2,1)} %get-tuple-element.88.ggr_ref, bf16[2048,768]{1,0:T(8,128)(2,1)} %copy-done.10, bf16[2048,640]{1,0:T(8,128)(2,1)} %copy-done.12, ...), custom_call_target="tpu_custom_call" | custom-call | flops 13690208256 | bytes 600000000 | tf_op jit(solution)/shard_map/chain/pallas_call | solution.py:821
  635.8 3.0 unpack.1
  638.8 27.3 %all-reduce.10.cloned.1.call-done = (bf16[1536,768]{1,0:T(8,128)(2,1)}, bf16[1536,768]{1,0:T(8,128)(2,1)}, bf16[768,1536]{1,0:T(8,128)(2,1)}) async-done(((bf16[1536,768]{1,0:T(8,128)(2,1)}, bf16[1536,768]{1,0:T(8,128)(2,1)}, bf16[768,1536]{1,0:T(8,128)(2,1)}), (bf16[1536,768]{1,0:T(8,128)(2,1)}, bf16[1536,768]{1,0:T(8,128)(2,1)}, bf16[768,1536]{1,0:T(8,128)(2,1)})) %all-reduce.10.cloned.1.call-update) | async-done | bytes 7077904 | tf_op jit(solution)/shard_map/psum | solution.py:1043
  666.1 25.9 %finish.1 = (bf16[2048,1536]{1,0:T(8,128)(2,1)}, f32[2048,1536]{1,0:T(8,128)}, f32[1536,768]{1,0:T(8,128)}, f32[1536,768]{1,0:T(8,128)}, f32[768,1536]{1,0:T(8,128)}) custom-call(f32[2048,128]{1,0:T(8,128)} %get-tuple-element.86.scale_ref, bf16[1280,1536]{1,0:T(8,128)(2,1)} %all-reduce.6.cloned.1.call-done.early_a_ref.early_b_ref, ...), custom_call_target="tpu_custom_call" | custom-call | bytes 80000000 | tf_op jit(solution)/shard_map/finish/pallas_call | solution.py:876
  (69 shorter events, 23.7 us)
Async XLA Ops:
  7.2 66.2 %copy-start = (bf16[768,1536]{1,0:T(8,128)(2,1)S(1)}, bf16[768,1536]{1,0:T(8,128)(2,1)}, u32[]{:S(2)}) copy-start(bf16[768,1536]{1,0:T(8,128)(2,1)} %param.32) | copy-start | bytes 7077892
  7.2 33.7 %all-gather.2.cloned.1.call-start = ((), (), s32[]{:S(2)}) async-start(), calls=%async_computation | async-start | bytes 1310720 | tf_op jit(solution)/shard_map/all_gather | solution.py:998
  9.4 277.7 %all-reduce.8.cloned.1.call-start = ((), (), s32[]{:S(2)}) async-start(), calls=%async_computation.2 | async-start | bytes 3538944 | tf_op jit(solution)/shard_map/psum | solution.py:1044
  29.6 17.0 %collective-permute-start = (bf16[8,2432]{1,0:T(8,128)(2,1)S(1)}, bf16[8,2432]{1,0:T(8,128)(2,1)S(1)}, u32[]{:S(2)}, u32[]{:S(2)}) collective-permute-start(bf16[8,2432]{1,0:T(8,128)(2,1)S(1)} %fusion.6), channel_id=1, source_target_pairs={{0,4},{4,8},{8,12},{12,16},{16,20},{20,24},{24,28},{1,5},{5,9},{9,... | collective-permute-start | bytes 116744 | tf_op jit(solution)/shard_map/ppermute | solution.py:972
  72.0 10.7 %collective-permute-start.1 = (bf16[128,768]{1,0:T(8,128)(2,1)}, bf16[128,768]{1,0:T(8,128)(2,1)S(1)}, u32[]{:S(2)}, u32[]{:S(2)}) collective-permute-start(bf16[128,768]{1,0:T(8,128)(2,1)} %get-tuple-element.84), channel_id=1, source_target_pairs={{0,4},{4,8},{8,12},{12,16},{16,20},{20,24},{24,28},{1,5},{5,9},{9,... | collective-permute-start | bytes 589832 | tf_op jit(solution)/shard_map/ppermute | solution.py:972
  93.9 4.5 collective-permute-start.4
  96.0 8.5 %collective-permute-start.3 = (f32[8,2048]{1,0:T(8,128)}, f32[8,2048]{1,0:T(8,128)S(1)}, u32[]{:S(2)}, u32[]{:S(2)}) collective-permute-start(f32[8,2048]{1,0:T(8,128)} %get-tuple-element.85.refs_0_), channel_id=1, source_target_pairs={{0,2},{1,3},{2,0},{3,1},{4,6},{5,7},{6,4},{7,5},{8,10},{9,11},{10,... | collective-permute-start | bytes 196616 | tf_op jit(solution)/shard_map/ppermute | solution.py:977
  96.8 7.7 %collective-permute-start.2 = (f32[8,2048]{1,0:T(8,128)}, f32[8,2048]{1,0:T(8,128)S(1)}, u32[]{:S(2)}, u32[]{:S(2)}) collective-permute-start(f32[8,2048]{1,0:T(8,128)} %get-tuple-element.85.refs_0_), channel_id=1, source_target_pairs={{0,1},{1,2},{2,3},{3,0},{4,5},{5,6},{6,7},{7,4},{8,9},{9,10},{10,1... | collective-permute-start | bytes 196616 | tf_op jit(solution)/shard_map/ppermute | solution.py:977
  98.3 6.2 copy-start.6
  123.2 3.8 collective-permute-start.5
  187.3 11.8 %collective-permute-start.6 = (f32[8,1024]{1,0:T(8,128)}, f32[8,1024]{1,0:T(8,128)S(1)}, u32[]{:S(2)}, u32[]{:S(2)}) collective-permute-start(f32[8,1024]{1,0:T(8,128)} %get-tuple-element.101), channel_id=1, source_target_pairs={{4,0},{8,4},{12,8},{16,12},{20,16},{24,20},{28,24},{5,1},{9,5},{13... | collective-permute-start | bytes 98312 | tf_op jit(solution)/shard_map/ppermute | solution.py:972
  188.6 10.5 %copy-start.9 = (bf16[2048,768]{1,0:T(8,128)(2,1)S(1)}, bf16[2048,768]{1,0:T(8,128)(2,1)}, u32[]{:S(2)}) copy-start(bf16[2048,768]{1,0:T(8,128)(2,1)} %get-tuple-element.100) | copy-start | bytes 9437188
  188.6 10.5 %copy-start.13 = (bf16[1536,768]{1,0:T(8,128)(2,1)S(1)}, bf16[1536,768]{1,0:T(8,128)(2,1)}, u32[]{:S(2)}) copy-start(bf16[1536,768]{1,0:T(8,128)(2,1)} %wv_ref.3) | copy-start | bytes 7077892
  188.7 21.9 %slice-start = ((s8[6291456]{0:T(1024)(128)(4,1)}), s8[4194304]{0:T(1024)(128)(4,1)S(1)}, s32[]{:S(2)}) async-start(s8[6291456]{0:T(1024)(128)(4,1)} %bitcast.22), calls=%async_computation.4 | async-start | bytes 8388608
  199.1 11.5 %slice-start.1 = ((s8[6291456]{0:T(1024)(128)(4,1)}), s8[2097152]{0:T(1024)(128)(4,1)S(1)}, s32[]{:S(2)}) async-start(s8[6291456]{0:T(1024)(128)(4,1)} %bitcast.22), calls=%async_computation.5 | async-start | bytes 4194304
  199.1 11.4 %copy-start.10 = (bf16[2048,768]{1,0:T(8,128)(2,1)}, bf16[2048,768]{1,0:T(8,128)(2,1)S(1)}, u32[]{:S(2)}) copy-start(bf16[2048,768]{1,0:T(8,128)(2,1)S(1)} %fusion.8.gv_ref) | copy-start | bytes 9437188
  199.1 11.4 %copy-start.11 = (bf16[2048,640]{1,0:T(8,128)(2,1)S(1)}, bf16[2048,640]{1,0:T(8,128)(2,1)}, u32[]{:S(2)}) copy-start(bf16[2048,640]{1,0:T(8,128)(2,1)} %get-tuple-element.102) | copy-start | bytes 7864324
  210.6 6.2 copy-start.12
  220.7 418.1 %all-reduce.6.cloned.1.call-start = ((), (), s32[]{:S(2)}) async-start(), calls=%async_computation.1 | async-start | bytes 7864320 | tf_op jit(solution)/shard_map/psum | solution.py:1012
  227.3 438.8 %all-reduce.10.cloned.1.call-start = ((), (), s32[]{:S(2)}) async-start(), calls=%async_computation.3 | async-start | bytes 14155776 | tf_op jit(solution)/shard_map/psum | solution.py:1043
  289.5 344.8 %collective-permute-start.7 = (bf16[80,1536]{1,0:T(8,128)(2,1)}, bf16[80,1536]{1,0:T(8,128)(2,1)S(1)}, u32[]{:S(2)}, u32[]{:S(2)}) collective-permute-start(bf16[80,1536]{1,0:T(8,128)(2,1)} %get-tuple-element.107), channel_id=1, source_target_pairs={{0,1},{1,2},{2,3},{3,0},{4,5},{5,6},{6,7},{7,4},{8,9},{9,10},{10,1... | collective-permute-start | bytes 737288 | tf_op jit(solution)/shard_map/ppermute | solution.py:1047
  291.2 343.1 %collective-permute-start.8 = (bf16[80,1536]{1,0:T(8,128)(2,1)}, bf16[80,1536]{1,0:T(8,128)(2,1)S(1)}, u32[]{:S(2)}, u32[]{:S(2)}) collective-permute-start(bf16[80,1536]{1,0:T(8,128)(2,1)} %get-tuple-element.108), channel_id=1, source_target_pairs={{0,2},{1,3},{2,0},{3,1},{4,6},{5,7},{6,4},{7,5},{8,10},{9,11},{10,... | collective-permute-start | bytes 737288 | tf_op jit(solution)/shard_map/ppermute | solution.py:1047
  293.6 340.8 %collective-permute-start.9 = (bf16[80,1536]{1,0:T(8,128)(2,1)}, bf16[80,1536]{1,0:T(8,128)(2,1)S(1)}, u32[]{:S(2)}, u32[]{:S(2)}) collective-permute-start(bf16[80,1536]{1,0:T(8,128)(2,1)} %get-tuple-element.109), channel_id=1, source_target_pairs={{0,3},{1,0},{2,1},{3,2},{4,7},{5,4},{6,5},{7,6},{8,11},{9,8},{10,9... | collective-permute-start | bytes 737288 | tf_op jit(solution)/shard_map/ppermute | solution.py:1047
  634.3 0.8 copy-start.4
  (7 other events, 4.7 us)
Sparse Core Ops, SparseCore 0:
  10.2 30.6 all-gather.1
  220.9 66.2 all-reduce.7
  290.1 254.4 all-reduce.5
  548.6 117.4 all-reduce.9
